TPU v7x, 32 devices: a whole 2x2x4 slice. The times are simulated.
32 devices in a mesh: fsdp: 16 (over z, y, x), seq: 2 (over core).
Axes of the slice: x: 2, y: 2, z: 4, core: 2. Of those that a mesh axis runs over, the one named last changes fastest.
Arguments:
- block_input: bfloat16 [64, 512, 1024], P(('fsdp', 'seq')), may hold values from -6 to 6
- w_qkv: bfloat16 [1024, 3072], P('fsdp'), as said below
- w_out: bfloat16 [1024, 1024], P('fsdp'), may hold values from -1.5 to 1.5
- w_up: bfloat16 [1024, 4096], P('fsdp'), may hold values from -0.1875 to 0.1875
- w_down: bfloat16 [4096, 1024], P('fsdp'), may hold values from -0.09375 to 0.09375
- b_query: bfloat16 [1024], P('fsdp'), may hold values from -3 to 3
- b_value: bfloat16 [1024], P('fsdp'), may hold values from -3 to 3
- b_out: bfloat16 [1024], P('fsdp'), may hold values from -3 to 3
- b_up: bfloat16 [4096], P('fsdp'), may hold values from -3 to 3
- b_down: bfloat16 [1024], P('fsdp'), may hold values from -3 to 3
- gain_one: bfloat16 [1024], P('fsdp'), may hold values from 0.5 to 1.5
- shift_one: bfloat16 [1024], P('fsdp'), may hold values from -2 to 2
- gain_two: bfloat16 [1024], P('fsdp'), may hold values from 0.5 to 1.5
- shift_two: bfloat16 [1024], P('fsdp'), may hold values from -2 to 2
- cotangent: bfloat16 [64, 512, 1024], P(('fsdp', 'seq')), may hold values from -6 to 6
Outputs:
- block_output: bfloat16 [64, 512, 1024], P(('fsdp', 'seq'))
- input_grad: float32 [64, 512, 1024], P(('fsdp', 'seq'))
- grad_qkv: float32 [1024, 3072], P('fsdp')
- grad_out: float32 [1024, 1024], P('fsdp')
- grad_up: float32 [1024, 4096], P('fsdp')
- grad_down: float32 [4096, 1024], P('fsdp')
- grad_query_bias: float32 [1024], P('fsdp')
- grad_value_bias: float32 [1024], P('fsdp')
- grad_out_bias: float32 [1024], P('fsdp')
- grad_up_bias: float32 [4096], P('fsdp')
- grad_down_bias: float32 [1024], P('fsdp')
- grad_gain_one: float32 [1024], P('fsdp')
- grad_shift_one: float32 [1024], P('fsdp')
- grad_gain_two: float32 [1024], P('fsdp')
- grad_shift_two: float32 [1024], P('fsdp')
Inputs may be any that keep to these rules, and one draw needn't show every extreme that they name: `w_qkv`: the query, key and value projections of every head, side by side.
All inputs are finite; a program needn't handle non-finite values.
Results may differ from a plain program's by a relative error of at most 0.013.
The roundings to bfloat16 on the way count: a program that leaves them out, or rounds other values in their place, can miss the bound.
Values may be sent and summed in bfloat16 or wider, within the bound.
A program may use at most 256 MiB of HBM per device.

v0:
```python
import jax
import jax.numpy as jnp
from jax import lax
from jax.sharding import PartitionSpec as P

HD = 64


EPSILON = 1e-05
NEG_LARGE = -1e30


def layer_norm(values, gain, shift):
    center = values - jnp.mean(values, -1, keepdims=True)
    spread = jnp.mean(center * center, -1, keepdims=True)
    return center * lax.rsqrt(spread + EPSILON) * gain + shift


def gelu_tanh(values):
    return jax.nn.gelu(values, approximate=True)


def to_float(values):
    return values.astype(jnp.float32)


def to_half(values):
    return values.astype(jnp.bfloat16)


def matmul(left, right):
    return jnp.dot(left, right, preferred_element_type=jnp.float32)


def left_trans(left, right):
    return lax.dot_general(
        left, right, (((0,), (0,)), ((), ())), preferred_element_type=jnp.float32
    )


def right_trans(left, right):
    return lax.dot_general(
        left, right, (((1,), (1,)), ((), ())), preferred_element_type=jnp.float32
    )


def split_pairs(values):
    row_count = values.shape[0]
    return jnp.moveaxis(values.reshape(row_count, -1, 2, HD), 1, 0)


def join_pairs(values):
    return jnp.moveaxis(values, 0, 1).reshape(values.shape[1], -1)


def causal(row_count):
    positions = jnp.arange(row_count, dtype=jnp.int32)
    return positions[None, :] <= positions[:, None]


def pair_scores(allowed, query, keys):
    scores = jnp.einsum("rgd,kgd->grk", query, keys, preferred_element_type=jnp.float32) * 0.125
    return jnp.where(allowed[None], scores, NEG_LARGE)


def attend_pair(allowed, operands):
    query, keys, values = operands
    scores = pair_scores(allowed, query, keys)
    highest = jnp.max(scores, -1, keepdims=True)
    unnormed = jnp.exp(scores - highest)
    total = jnp.sum(unnormed, -1, keepdims=True)
    probs = to_half(unnormed / total)
    mixed = jnp.einsum("grk,kgd->rgd", probs, values, preferred_element_type=jnp.float32)
    return (to_half(mixed), (highest + jnp.log(total))[..., 0])


def attend_back(allowed, operands):
    query, keys, values, upstream, logsum = operands
    scores = pair_scores(allowed, query, keys)
    probs = jnp.exp(scores - logsum[..., None])
    prob_grad = jnp.einsum("rgd,kgd->grk", upstream, values, preferred_element_type=jnp.float32)
    inner = jnp.sum(probs * prob_grad, -1, keepdims=True)
    score_grad = to_half(probs * (prob_grad - inner))
    query_grad = (
        jnp.einsum("grk,kgd->rgd", score_grad, keys, preferred_element_type=jnp.float32) * 0.125
    )
    key_grad = (
        jnp.einsum("grk,rgd->kgd", score_grad, query, preferred_element_type=jnp.float32) * 0.125
    )
    value_grad = jnp.einsum(
        "grk,rgd->kgd", to_half(probs), upstream, preferred_element_type=jnp.float32
    )
    return (query_grad, key_grad, value_grad)


def forward(block_rows, weights):
    (
        w_qkv,
        w_out,
        w_up,
        w_down,
        b_query,
        b_value,
        b_out,
        b_up,
        b_down,
        gain_one,
        shift_one,
        gain_two,
        shift_two,
    ) = weights
    inputs = to_float(block_rows)
    row_count = inputs.shape[0]
    model_width = inputs.shape[1]
    normed_one = to_half(layer_norm(inputs, to_float(gain_one), to_float(shift_one)))
    merged = matmul(normed_one, w_qkv)
    query = to_half(merged[:, :model_width] + to_float(b_query))
    keys = to_half(merged[:, model_width : 2 * model_width])
    values = to_half(merged[:, 2 * model_width :] + to_float(b_value))
    allowed = causal(row_count)
    mixed, logsum = lax.map(
        lambda operands: attend_pair(allowed, operands),
        (split_pairs(query), split_pairs(keys), split_pairs(values)),
    )
    attended = join_pairs(mixed)
    middle = inputs + (matmul(attended, w_out) + to_float(b_out))
    normed_two = to_half(layer_norm(middle, to_float(gain_two), to_float(shift_two)))
    hidden = matmul(normed_two, w_up) + to_float(b_up)
    activated = to_half(gelu_tanh(hidden))
    output = to_half(middle + (matmul(activated, w_down) + to_float(b_down)))
    kept = (
        inputs,
        normed_one,
        query,
        keys,
        values,
        logsum,
        attended,
        middle,
        normed_two,
        hidden,
        activated,
        allowed,
    )
    return (kept, output)


def backward(upstream_rows, kept, weights):
    (
        w_qkv,
        w_out,
        w_up,
        w_down,
        b_query,
        b_value,
        b_out,
        b_up,
        b_down,
        gain_one,
        shift_one,
        gain_two,
        shift_two,
    ) = weights
    (
        inputs,
        normed_one,
        query,
        keys,
        values,
        logsum,
        attended,
        middle,
        normed_two,
        hidden,
        activated,
        allowed,
    ) = kept
    upstream = to_float(upstream_rows)
    grad_down_bias = jnp.sum(upstream, 0)
    grad_down = left_trans(activated, upstream_rows)
    act_grad = right_trans(upstream_rows, w_down)
    unused, gelu_pull = jax.vjp(gelu_tanh, hidden)
    hidden_grad = to_half(gelu_pull(act_grad)[0])
    grad_up_bias = jnp.sum(to_float(hidden_grad), 0)
    grad_up = left_trans(normed_two, hidden_grad)
    normed_two_grad = right_trans(hidden_grad, w_up)
    unused, norm_pull_two = jax.vjp(layer_norm, middle, to_float(gain_two), to_float(shift_two))
    middle_part, grad_gain_two, grad_shift_two = norm_pull_two(normed_two_grad)
    middle_grad = upstream + middle_part
    branch_grad = to_half(middle_grad)
    grad_out_bias = jnp.sum(to_float(branch_grad), 0)
    grad_out = left_trans(attended, branch_grad)
    attended_grad = to_half(right_trans(branch_grad, w_out))
    query_parts, key_parts, value_parts = lax.map(
        lambda operands: attend_back(allowed, operands),
        (
            split_pairs(query),
            split_pairs(keys),
            split_pairs(values),
            split_pairs(attended_grad),
            logsum,
        ),
    )
    query_grad = to_half(join_pairs(query_parts))
    key_grad = to_half(join_pairs(key_parts))
    value_grad = to_half(join_pairs(value_parts))
    merged_grad = jnp.concatenate([query_grad, key_grad, value_grad], axis=1)
    grad_query_bias = jnp.sum(to_float(query_grad), 0)
    grad_value_bias = jnp.sum(to_float(value_grad), 0)
    grad_qkv = left_trans(normed_one, merged_grad)
    normed_one_grad = right_trans(merged_grad, w_qkv)
    unused, norm_pull_one = jax.vjp(layer_norm, inputs, to_float(gain_one), to_float(shift_one))
    input_part, grad_gain_one, grad_shift_one = norm_pull_one(normed_one_grad)
    input_grad = middle_grad + input_part
    grads = (
        grad_qkv,
        grad_out,
        grad_up,
        grad_down,
        grad_query_bias,
        grad_value_bias,
        grad_out_bias,
        grad_up_bias,
        grad_down_bias,
        grad_gain_one,
        grad_shift_one,
        grad_gain_two,
        grad_shift_two,
    )
    return (grads, input_grad)


def gather_weights(shards):
    (
        w_qkv,
        w_out,
        w_up,
        w_down,
        b_query,
        b_value,
        b_out,
        b_up,
        b_down,
        gain_one,
        shift_one,
        gain_two,
        shift_two,
    ) = shards
    return (
        lax.all_gather(w_qkv, "fsdp", axis=0, tiled=True),
        lax.all_gather(w_out, "fsdp", axis=0, tiled=True),
        lax.all_gather(w_up, "fsdp", axis=0, tiled=True),
        lax.all_gather(w_down, "fsdp", axis=0, tiled=True),
        lax.all_gather(b_query, "fsdp", axis=0, tiled=True),
        lax.all_gather(b_value, "fsdp", axis=0, tiled=True),
        lax.all_gather(b_out, "fsdp", axis=0, tiled=True),
        lax.all_gather(b_up, "fsdp", axis=0, tiled=True),
        lax.all_gather(b_down, "fsdp", axis=0, tiled=True),
        lax.all_gather(gain_one, "fsdp", axis=0, tiled=True),
        lax.all_gather(shift_one, "fsdp", axis=0, tiled=True),
        lax.all_gather(gain_two, "fsdp", axis=0, tiled=True),
        lax.all_gather(shift_two, "fsdp", axis=0, tiled=True),
    )


def local(
    block_input,
    w_qkv,
    w_out,
    w_up,
    w_down,
    b_query,
    b_value,
    b_out,
    b_up,
    b_down,
    gain_one,
    shift_one,
    gain_two,
    shift_two,
    cotangent,
):
    owners = lax.axis_size("fsdp")
    shards = (
        w_qkv,
        w_out,
        w_up,
        w_down,
        b_query,
        b_value,
        b_out,
        b_up,
        b_down,
        gain_one,
        shift_one,
        gain_two,
        shift_two,
    )
    initial = tuple(
        (jnp.zeros((shard.shape[0] * owners,) + shard.shape[1:], jnp.float32) for shard in shards)
    )

    def micro_step(totals, inputs_pair):
        block_rows, upstream_rows = inputs_pair
        gathered = gather_weights(shards)
        kept, output = forward(block_rows, gathered)
        back_weights = (
            lax.all_gather(w_qkv, "fsdp", axis=0, tiled=True),
            lax.all_gather(w_out, "fsdp", axis=0, tiled=True),
            lax.all_gather(w_up, "fsdp", axis=0, tiled=True),
            lax.all_gather(w_down, "fsdp", axis=0, tiled=True),
            lax.all_gather(b_query, "fsdp", axis=0, tiled=True),
            lax.all_gather(b_value, "fsdp", axis=0, tiled=True),
            lax.all_gather(b_out, "fsdp", axis=0, tiled=True),
            lax.all_gather(b_up, "fsdp", axis=0, tiled=True),
            lax.all_gather(b_down, "fsdp", axis=0, tiled=True),
            lax.all_gather(gain_one, "fsdp", axis=0, tiled=True),
            lax.all_gather(shift_one, "fsdp", axis=0, tiled=True),
            lax.all_gather(gain_two, "fsdp", axis=0, tiled=True),
            lax.all_gather(shift_two, "fsdp", axis=0, tiled=True),
        )
        grads, input_grad = backward(upstream_rows, kept, back_weights)
        totals = tuple((total + grad for total, grad in zip(totals, grads)))
        return (totals, (output, input_grad))

    totals, stacked = lax.scan(micro_step, initial, (block_input, cotangent))
    outputs, input_grads = stacked
    reduced = (
        lax.psum_scatter(totals[0], "fsdp", scatter_dimension=0, tiled=True),
        lax.psum_scatter(totals[1], "fsdp", scatter_dimension=0, tiled=True),
        lax.psum_scatter(totals[2], "fsdp", scatter_dimension=0, tiled=True),
        lax.psum_scatter(totals[3], "fsdp", scatter_dimension=0, tiled=True),
        lax.psum_scatter(totals[4], "fsdp", scatter_dimension=0, tiled=True),
        lax.psum_scatter(totals[5], "fsdp", scatter_dimension=0, tiled=True),
        lax.psum_scatter(totals[6], "fsdp", scatter_dimension=0, tiled=True),
        lax.psum_scatter(totals[7], "fsdp", scatter_dimension=0, tiled=True),
        lax.psum_scatter(totals[8], "fsdp", scatter_dimension=0, tiled=True),
        lax.psum_scatter(totals[9], "fsdp", scatter_dimension=0, tiled=True),
        lax.psum_scatter(totals[10], "fsdp", scatter_dimension=0, tiled=True),
        lax.psum_scatter(totals[11], "fsdp", scatter_dimension=0, tiled=True),
        lax.psum_scatter(totals[12], "fsdp", scatter_dimension=0, tiled=True),
    )
    summed = (
        lax.psum(reduced[0].astype(jnp.bfloat16), "seq").astype(jnp.float32),
        lax.psum(reduced[1].astype(jnp.bfloat16), "seq").astype(jnp.float32),
        lax.psum(reduced[2].astype(jnp.bfloat16), "seq").astype(jnp.float32),
        lax.psum(reduced[3].astype(jnp.bfloat16), "seq").astype(jnp.float32),
        lax.psum(reduced[4].astype(jnp.bfloat16), "seq").astype(jnp.float32),
        lax.psum(reduced[5].astype(jnp.bfloat16), "seq").astype(jnp.float32),
        lax.psum(reduced[6].astype(jnp.bfloat16), "seq").astype(jnp.float32),
        lax.psum(reduced[7].astype(jnp.bfloat16), "seq").astype(jnp.float32),
        lax.psum(reduced[8].astype(jnp.bfloat16), "seq").astype(jnp.float32),
        lax.psum(reduced[9].astype(jnp.bfloat16), "seq").astype(jnp.float32),
        lax.psum(reduced[10].astype(jnp.bfloat16), "seq").astype(jnp.float32),
        lax.psum(reduced[11].astype(jnp.bfloat16), "seq").astype(jnp.float32),
        lax.psum(reduced[12].astype(jnp.bfloat16), "seq").astype(jnp.float32),
    )
    return (
        outputs,
        input_grads,
        summed[0],
        summed[1],
        summed[2],
        summed[3],
        summed[4],
        summed[5],
        summed[6],
        summed[7],
        summed[8],
        summed[9],
        summed[10],
        summed[11],
        summed[12],
    )


def solution(mesh):
    in_specs = (
        P(("fsdp", "seq"), None, None),
        P("fsdp", None),
        P("fsdp", None),
        P("fsdp", None),
        P("fsdp", None),
        P("fsdp"),
        P("fsdp"),
        P("fsdp"),
        P("fsdp"),
        P("fsdp"),
        P("fsdp"),
        P("fsdp"),
        P("fsdp"),
        P("fsdp"),
        P(("fsdp", "seq"), None, None),
    )
    out_specs = (
        P(("fsdp", "seq"), None, None),
        P(("fsdp", "seq"), None, None),
        P("fsdp", None),
        P("fsdp", None),
        P("fsdp", None),
        P("fsdp", None),
        P("fsdp"),
        P("fsdp"),
        P("fsdp"),
        P("fsdp"),
        P("fsdp"),
        P("fsdp"),
        P("fsdp"),
        P("fsdp"),
        P("fsdp"),
    )
    return jax.shard_map(local, mesh=mesh, in_specs=in_specs, out_specs=out_specs, check_vma=False)
```

profile of v0, /device:TPU:0, one launch (start us, length us, event | category | flops | bytes accessed | tf_op | source)
XLA Modules:
  0.0 2249.9 jit_solution(12940585115201816945)
XLA Ops:
  8.2 1130.1 %while.100 = (s32[]{:T(128)}, f32[1024,3072]{1,0:T(8,128)}, f32[1024,1024]{1,0:T(8,128)}, f32[1024,4096]{1,0:T(8,128)}, f32[4096,1024]{1,0:T(8,128)}, /*index=5*...) while((s32[]{:T(128)}, f32[1024,3072]{1,0:T(8,128)}, ...), condition=%wide.region_25.26_spmd.clone, body=%wide.region_0.25_spmd.clone.sunk | while | flops 39321833472 | bytes 590473728 | solution.py:326
  19.9 81.0 %all-reduce.30 = (bf16[1024]{0:T(1024)(128)(2,1)S(1)}, bf16[1024]{0:T(1024)(128)(2,1)S(1)}, bf16[1024]{0:T(1024)(128)(2,1)S(1)}, bf16[1024]{0:T(1024)(128)(2,1)S...) all-reduce(bf16[1024]{0:T(1024)(128)(2,1)S(1)} %dynamic-update-slic, ...), channel_id=1, replica_groups=mesh['fsdp'=16,'seq'=2] {'fsdp'}, use_global_device_ids=true, to_apply=%add.1 | all-reduce | flops 8192 | bytes 32768 | tf_op jit(solution)/shard_map/while
  101.5 35.8 %all-gather.3 = bf16[16,1,256]{2,1,0:T(2,128)(2,1)S(1)} all-gather(bf16[1,1,256]{2,1,0:T(2,128)(2,1)S(1)} %reshape.249), channel_id=1, replica_groups=mesh['fsdp'=16,'seq'=2] {'fsdp'}, dimensions={0}, use_global_device_ids=true | all-gather | bytes 8704 | tf_op jit(solution)/shard_map/while/body/eval_jaxpr/all_gather | solution.py:257
  139.8 5.8 fusion.172
  152.7 23.5 %while.101 = (s32[]{:T(128)}, bf16[8,512,2,64]{1,3,2,0:T(8,128)(2,1)S(1)}, f32[8,2,512]{2,1,0:T(2,128)S(1)}, bf16[8,512,2,64]{1,3,2,0:T(8,128)(2,1)}, bf16[8,512...) while((s32[]{:T(128)}, bf16[8,512,2,64]{1,3,2,0:T(8,128)(2,1)S(1)}, ...), condition=%wide.region_6.6_spmd.clone, body=%wide.region_3.5_spmd.clone.sunk | while | flops 140835840 | bytes 7899217 | solution.py:121
  177.5 3.2 fusion.174
  181.1 104.4 %all-gather.13.cloned.1.call-done = bf16[1024,4096]{1,0:T(8,128)(2,1)} async-done(((bf16[64,4096]{1,0:T(8,128)(2,1)}), bf16[1024,4096]{1,0:T(8,128)(2,1)}) %all-gather.13.cloned.1.call-update) | async-done | bytes 8388624 | tf_op jit(solution)/shard_map/while/body/eval_jaxpr/all_gather | solution.py:252
  285.5 10.2 fusion.176
  295.7 102.9 %all-gather.15.cloned.1.call-done = bf16[4096,1024]{1,0:T(8,128)(2,1)} async-done(((bf16[256,1024]{1,0:T(8,128)(2,1)}), bf16[4096,1024]{1,0:T(8,128)(2,1)}) %all-gather.15.cloned.1.call-update) | async-done | bytes 8388624 | tf_op jit(solution)/shard_map/while/body/eval_jaxpr/all_gather | solution.py:311
  398.6 13.8 convert_reduce_fusion.12
  412.4 5.0 multiply_reduce_fusion.8
  420.9 2.3 convolution_convert_fusion.3
  423.2 2.3 copy.65
  425.5 79.6 %while.102 = (s32[]{:T(128)}, bf16[8,512,2,64]{1,3,2,0:T(8,128)(2,1)}, bf16[8,512,2,64]{1,3,2,0:T(8,128)(2,1)}, bf16[8,512,2,64]{1,3,2,0:T(8,128)(2,1)}, bf16[8,...) while((s32[]{:T(128)}, ...), condition=%wide.region_13.13_spmd.clone, body=%wide.region_11.12_spmd.clone.sunk | while | flops 340655104 | bytes 17982568 | solution.py:194
  430.0 2.0 fusion.195
  439.9 2.0 fusion.195
  449.8 2.0 fusion.195
  459.7 2.0 fusion.195
  469.5 2.0 fusion.195
  479.4 2.0 fusion.195
  489.3 2.0 fusion.195
  499.2 2.0 fusion.195
  508.1 7.3 fusion.178
  516.9 10.9 select_add_fusion.24
  530.0 10.3 select_add_fusion.22
  540.3 13.1 select_add_fusion.25
  553.5 3.6 bitcast_dynamic-update-slice_fusion.4
  557.3 11.2 fusion.180
  581.7 76.3 %all-reduce.30 = (bf16[1024]{0:T(1024)(128)(2,1)S(1)}, bf16[1024]{0:T(1024)(128)(2,1)S(1)}, bf16[1024]{0:T(1024)(128)(2,1)S(1)}, bf16[1024]{0:T(1024)(128)(2,1)S...) all-reduce(bf16[1024]{0:T(1024)(128)(2,1)S(1)} %dynamic-update-slic, ...), channel_id=1, replica_groups=mesh['fsdp'=16,'seq'=2] {'fsdp'}, use_global_device_ids=true, to_apply=%add.1 | all-reduce | flops 8192 | bytes 32768 | tf_op jit(solution)/shard_map/while
  658.8 35.8 %all-gather.3 = bf16[16,1,256]{2,1,0:T(2,128)(2,1)S(1)} all-gather(bf16[1,1,256]{2,1,0:T(2,128)(2,1)S(1)} %reshape.249), channel_id=1, replica_groups=mesh['fsdp'=16,'seq'=2] {'fsdp'}, dimensions={0}, use_global_device_ids=true | all-gather | bytes 8704 | tf_op jit(solution)/shard_map/while/body/eval_jaxpr/all_gather | solution.py:257
  697.1 5.8 fusion.172
  710.0 23.4 %while.101 = (s32[]{:T(128)}, bf16[8,512,2,64]{1,3,2,0:T(8,128)(2,1)S(1)}, f32[8,2,512]{2,1,0:T(2,128)S(1)}, bf16[8,512,2,64]{1,3,2,0:T(8,128)(2,1)}, bf16[8,512...) while((s32[]{:T(128)}, bf16[8,512,2,64]{1,3,2,0:T(8,128)(2,1)S(1)}, ...), condition=%wide.region_6.6_spmd.clone, body=%wide.region_3.5_spmd.clone.sunk | while | flops 140835840 | bytes 7899217 | solution.py:121
  734.8 3.2 fusion.174
  738.4 104.1 %all-gather.13.cloned.1.call-done = bf16[1024,4096]{1,0:T(8,128)(2,1)} async-done(((bf16[64,4096]{1,0:T(8,128)(2,1)}), bf16[1024,4096]{1,0:T(8,128)(2,1)}) %all-gather.13.cloned.1.call-update) | async-done | bytes 8388624 | tf_op jit(solution)/shard_map/while/body/eval_jaxpr/all_gather | solution.py:252
  842.5 10.2 fusion.176
  852.7 103.0 %all-gather.15.cloned.1.call-done = bf16[4096,1024]{1,0:T(8,128)(2,1)} async-done(((bf16[256,1024]{1,0:T(8,128)(2,1)}), bf16[4096,1024]{1,0:T(8,128)(2,1)}) %all-gather.15.cloned.1.call-update) | async-done | bytes 8388624 | tf_op jit(solution)/shard_map/while/body/eval_jaxpr/all_gather | solution.py:311
  955.8 13.6 convert_reduce_fusion.12
  969.4 5.0 multiply_reduce_fusion.8
  977.9 2.3 convolution_convert_fusion.3
  980.2 2.3 copy.65
  982.5 79.2 %while.102 = (s32[]{:T(128)}, bf16[8,512,2,64]{1,3,2,0:T(8,128)(2,1)}, bf16[8,512,2,64]{1,3,2,0:T(8,128)(2,1)}, bf16[8,512,2,64]{1,3,2,0:T(8,128)(2,1)}, bf16[8,...) while((s32[]{:T(128)}, ...), condition=%wide.region_13.13_spmd.clone, body=%wide.region_11.12_spmd.clone.sunk | while | flops 340655104 | bytes 17982568 | solution.py:194
  986.7 2.0 fusion.195
  996.6 2.0 fusion.195
  1016.3 2.0 fusion.195
  1026.2 2.0 fusion.195
  1036.1 2.0 fusion.195
  1045.9 2.0 fusion.195
  1055.8 2.0 fusion.195
  1064.7 7.3 fusion.178
  1073.5 13.3 select_add_fusion.24
  1089.0 14.5 select_add_fusion.22
  1103.6 15.8 select_add_fusion.25
  1119.5 3.6 bitcast_dynamic-update-slice_fusion.4
  1123.4 11.2 fusion.180
  1140.8 94.5 %reduce-scatter.7.cloned.1.call-done = f32[64,1024]{1,0:T(8,128)} async-done(((f32[1024,1024]{1,0:T(8,128)}), f32[64,1024]{1,0:T(8,128)}) %reduce-scatter.7.cloned.1.call-update) | async-done | bytes 262160 | tf_op jit(solution)/shard_map/reduce_scatter | solution.py:330
  1237.0 205.4 %reduce-scatter.5.cloned.1.call-done = f32[64,3072]{1,0:T(8,128)} async-done(((f32[1024,3072]{1,0:T(8,128)}), f32[64,3072]{1,0:T(8,128)}) %reduce-scatter.5.cloned.1.call-update) | async-done | bytes 786448 | tf_op jit(solution)/shard_map/reduce_scatter | solution.py:329
  1444.4 346.1 %reduce-scatter.9.cloned.1.call-done = f32[64,4096]{1,0:T(8,128)} async-done(((f32[1024,4096]{1,0:T(8,128)}), f32[64,4096]{1,0:T(8,128)}) %reduce-scatter.9.cloned.1.call-update) | async-done | bytes 1048592 | tf_op jit(solution)/shard_map/reduce_scatter | solution.py:331
  1790.4 2.1 convert_element_type.300
  1792.5 352.3 %reduce-scatter.11.cloned.1.call-done = f32[256,1024]{1,0:T(8,128)} async-done(((f32[4096,1024]{1,0:T(8,128)}), f32[256,1024]{1,0:T(8,128)}) %reduce-scatter.11.cloned.1.call-update) | async-done | bytes 1048592 | tf_op jit(solution)/shard_map/reduce_scatter | solution.py:332
  2144.7 2.1 convert_element_type.302
  2148.8 79.5 %all-reduce.26 = (bf16[1024]{0:T(1024)(128)(2,1)S(1)}, bf16[1024]{0:T(1024)(128)(2,1)S(1)}, bf16[1024]{0:T(1024)(128)(2,1)S(1)}, bf16[4096]{0:T(1024)(128)(2,1)S...) all-reduce(f32[1024]{0:T(1024)S(1)} %copy-done.33, ...), channel_id=6, replica_groups=mesh['fsdp'=16,'seq'=2] {'fsdp'}, use_global_device_ids=true, to_apply=%region_34.35.clone | all-reduce | flops 12288 | bytes 73728
  2229.0 2.5 all-reduce.27
  2236.1 2.1 convert_element_type.301
  2238.3 2.1 convert_element_type.303
  (568 shorter events, 255.6 us)
Async XLA Ops:
  8.4 131.0 %copy-start.2 = (bf16[2,512,1024]{2,1,0:T(8,128)(2,1)S(1)}, bf16[2,512,1024]{2,1,0:T(8,128)(2,1)}, u32[]{:S(2)}) copy-start(bf16[2,512,1024]{2,1,0:T(8,128)(2,1)} %get-tuple-element.1347) | copy-start | bytes 6291460 | tf_op jit(solution)/shard_map/while
  8.4 131.4 %all-gather.9.cloned.1.call-start = ((), (), s32[]{:S(2)}) async-start(), calls=%async_computation.9 | async-start | bytes 6684672 | tf_op jit(solution)/shard_map/while/body/eval_jaxpr/all_gather | solution.py:250
  9.1 167.1 %all-gather.11.cloned.1.call-start = ((), (), s32[]{:S(2)}) async-start(), calls=%async_computation.10 | async-start | bytes 2228224 | tf_op jit(solution)/shard_map/while/body/eval_jaxpr/all_gather | solution.py:251
  9.9 275.6 %all-gather.13.cloned.1.call-start = ((), (), s32[]{:S(2)}) async-start(), calls=%async_computation.11 | async-start | bytes 8912896 | tf_op jit(solution)/shard_map/while/body/eval_jaxpr/all_gather | solution.py:252
  10.6 388.0 %all-gather.15.cloned.1.call-start = ((), (), s32[]{:S(2)}) async-start(), calls=%async_computation.12 | async-start | bytes 8912896 | tf_op jit(solution)/shard_map/while/body/eval_jaxpr/all_gather | solution.py:311
  398.6 13.8 copy-start.48
  412.4 5.0 copy-start.11
  516.9 10.9 copy-start.5
  516.9 10.9 copy-start.14
  529.8 10.5 copy-start.6
  540.3 13.1 copy-start.1
  540.3 13.1 copy-start.8
  553.4 3.9 copy-start.25
  553.4 3.9 copy-start.47
  553.5 3.9 copy-start.49
  557.1 11.5 copy-start.19
  557.1 11.5 copy-start.23
  557.2 11.5 copy-start.44
  557.2 11.4 copy-start.32
  557.2 11.4 copy-start.35
  557.3 11.4 copy-start.38
  557.3 11.4 copy-start.41
  557.3 11.3 copy-start.26
  557.3 11.3 copy-start.29
  570.4 126.3 %copy-start.2 = (bf16[2,512,1024]{2,1,0:T(8,128)(2,1)S(1)}, bf16[2,512,1024]{2,1,0:T(8,128)(2,1)}, u32[]{:S(2)}) copy-start(bf16[2,512,1024]{2,1,0:T(8,128)(2,1)} %get-tuple-element.1347) | copy-start | bytes 6291460 | tf_op jit(solution)/shard_map/while
  570.4 126.7 %all-gather.9.cloned.1.call-start = ((), (), s32[]{:S(2)}) async-start(), calls=%async_computation.9 | async-start | bytes 6684672 | tf_op jit(solution)/shard_map/while/body/eval_jaxpr/all_gather | solution.py:250
  571.0 162.5 %all-gather.11.cloned.1.call-start = ((), (), s32[]{:S(2)}) async-start(), calls=%async_computation.10 | async-start | bytes 2228224 | tf_op jit(solution)/shard_map/while/body/eval_jaxpr/all_gather | solution.py:251
  571.6 270.9 %all-gather.13.cloned.1.call-start = ((), (), s32[]{:S(2)}) async-start(), calls=%async_computation.11 | async-start | bytes 8912896 | tf_op jit(solution)/shard_map/while/body/eval_jaxpr/all_gather | solution.py:252
  572.3 383.4 %all-gather.15.cloned.1.call-start = ((), (), s32[]{:S(2)}) async-start(), calls=%async_computation.12 | async-start | bytes 8912896 | tf_op jit(solution)/shard_map/while/body/eval_jaxpr/all_gather | solution.py:311
  955.8 13.6 copy-start.48
  969.4 5.0 copy-start.11
  1073.5 13.3 copy-start.5
  1073.5 13.3 copy-start.14
  1088.8 14.7 copy-start.6
  1103.6 15.9 copy-start.1
  1103.6 15.9 copy-start.8
  1119.5 3.9 copy-start.47
  1119.5 3.9 copy-start.49
  1123.2 11.5 copy-start.19
  1123.2 11.5 copy-start.23
  1123.2 11.5 copy-start.44
  1123.3 11.4 copy-start.32
  1123.3 11.4 copy-start.35
  1123.3 11.4 copy-start.38
  1123.3 11.4 copy-start.41
  1123.4 11.3 copy-start.26
  1123.4 11.3 copy-start.29
  1138.3 97.1 %reduce-scatter.7.cloned.1.call-start = ((), (), s32[]{:S(2)}) async-start(), calls=%async_computation.5 | async-start | bytes 4456448 | tf_op jit(solution)/shard_map/reduce_scatter | solution.py:330
  1138.9 303.5 %reduce-scatter.5.cloned.1.call-start = ((), (), s32[]{:S(2)}) async-start(), calls=%async_computation.4 | async-start | bytes 13369344 | tf_op jit(solution)/shard_map/reduce_scatter | solution.py:329
  1139.5 651.0 %reduce-scatter.9.cloned.1.call-start = ((), (), s32[]{:S(2)}) async-start(), calls=%async_computation.6 | async-start | bytes 17825792 | tf_op jit(solution)/shard_map/reduce_scatter | solution.py:331
  1140.0 1004.7 %reduce-scatter.11.cloned.1.call-start = ((), (), s32[]{:S(2)}) async-start(), calls=%async_computation.7 | async-start | bytes 17825792 | tf_op jit(solution)/shard_map/reduce_scatter | solution.py:332
  1140.8 1095.3 %all-reduce.33.cloned.1.call-start = ((), (), s32[]{:S(2)}) async-start(), calls=%async_computation.8 | async-start | bytes 3145728 | tf_op jit(solution)/shard_map/psum | solution.py:344
  1444.3 702.6 %copy-start.51 = (u32[32]{0:T(128)S(1)}, u32[32]{0:T(128)}, u32[]{:S(2)}) copy-start(u32[32]{0:T(128)} %get-tuple-element.1423) | copy-start | bytes 388
  1444.3 704.5 %copy-start.20 = (f32[4096]{0:T(1024)S(1)}, f32[4096]{0:T(1024)}, u32[]{:S(2)}) copy-start(f32[4096]{0:T(1024)} %get-tuple-element.507) | copy-start | bytes 49156
  1444.3 704.5 %copy-start.24 = (f32[1024]{0:T(1024)S(1)}, f32[1024]{0:T(1024)}, u32[]{:S(2)}) copy-start(f32[1024]{0:T(1024)} %get-tuple-element.510) | copy-start | bytes 12292
  1444.3 704.5 %copy-start.27 = (f32[1024]{0:T(1024)S(1)}, f32[1024]{0:T(1024)}, u32[]{:S(2)}) copy-start(f32[1024]{0:T(1024)} %get-tuple-element.511) | copy-start | bytes 12292
  1444.3 704.5 %copy-start.30 = (f32[1024]{0:T(1024)S(1)}, f32[1024]{0:T(1024)}, u32[]{:S(2)}) copy-start(f32[1024]{0:T(1024)} %get-tuple-element.512) | copy-start | bytes 12292
  1444.3 704.5 %copy-start.33 = (f32[1024]{0:T(1024)S(1)}, f32[1024]{0:T(1024)}, u32[]{:S(2)}) copy-start(f32[1024]{0:T(1024)} %get-tuple-element.504) | copy-start | bytes 12292
  1444.3 704.5 %copy-start.36 = (f32[1024]{0:T(1024)S(1)}, f32[1024]{0:T(1024)}, u32[]{:S(2)}) copy-start(f32[1024]{0:T(1024)} %get-tuple-element.505) | copy-start | bytes 12292
  1444.3 704.5 %copy-start.39 = (f32[1024]{0:T(1024)S(1)}, f32[1024]{0:T(1024)}, u32[]{:S(2)}) copy-start(f32[1024]{0:T(1024)} %get-tuple-element.506) | copy-start | bytes 12292
  1444.3 704.5 %copy-start.42 = (f32[1024]{0:T(1024)S(1)}, f32[1024]{0:T(1024)}, u32[]{:S(2)}) copy-start(f32[1024]{0:T(1024)} %get-tuple-element.508) | copy-start | bytes 12292
  1444.3 704.5 %copy-start.45 = (f32[1024]{0:T(1024)S(1)}, f32[1024]{0:T(1024)}, u32[]{:S(2)}) copy-start(f32[1024]{0:T(1024)} %get-tuple-element.509) | copy-start | bytes 12292
  2236.1 4.3 copy-start.21
  2236.1 5.2 copy-start.46
  (41 other events, 104.5 us)
Sparse Core Ops, SparseCore 0:
  12.0 97.1 all-gather.8
  112.0 59.5 all-gather.10
  174.3 111.0 all-gather.12
  288.1 110.4 all-gather.14
  573.7 93.0 all-gather.8
  669.4 59.1 all-gather.10
  731.4 111.0 all-gather.12
  845.3 110.4 all-gather.14
Sparse Core Ops, SparseCore 1:
  1141.1 94.2 reduce-scatter.6
  1240.9 201.4 reduce-scatter.4
  1444.5 345.8 reduce-scatter.8
  1792.7 352.0 reduce-scatter.10
  2147.9 25.8 all-reduce.32
where the time goes:
time: 2250 us
  waiting for transfers between devices  1420 us (63%)
  matrix products  383 us (17%)
  blocking collectives  311 us (14%)
  other arithmetic  65 us (3%)
  local copies, waits for them, and re-layouts  45.4 us (2%)
    reduce_scatter x1, waiting for transfers between devices, local(): lax.psum_scatter(totals[3], 'fsdp', scatter_dimension=0, tiled=True)  352 us
    reduce_scatter x1, waiting for transfers between devices, local(): lax.psum_scatter(totals[2], 'fsdp', scatter_dimension=0, tiled=True)  346 us
    all_gather x2, waiting for transfers between devices, gather_weights(): lax.all_gather(w_up, 'fsdp', axis=0, tiled=True)  209 us
    all_gather x2, waiting for transfers between devices, micro_step(): lax.all_gather(w_down, 'fsdp', axis=0, tiled=True)  206 us
    reduce_scatter x1, waiting for transfers between devices, local(): lax.psum_scatter(totals[0], 'fsdp', scatter_dimension=0, tiled=True)  205 us
    while x2, blocking collectives  157 us
    reduce_scatter x1, waiting for transfers between devices, local(): lax.psum_scatter(totals[1], 'fsdp', scatter_dimension=0, tiled=True)  94.5 us
    dot_general x8, matrix products, left_trans(): lax.dot_general(left, right, (((0,), (0,)), ((), ())), preferred_element_...  81.8 us
  transfers between devices with their start and end apart: 13, of which 8 were waited for; matrix products, arithmetic and copies ran while one was open for 6% of the time, Pallas kernels for 0%

commit v1 on v0

v1 whole, which is shorter than its diff:
```python
import jax
import jax.numpy as jnp
from jax import lax
from jax.experimental import pallas as pl
from jax.experimental.pallas import tpu as pltpu
from jax.sharding import PartitionSpec as P

EPSILON = 1e-05
NEG_LARGE = -1e30
MESH = pl.DeviceIdType.MESH
NN = (((1,), (0,)), ((), ()))
NT = (((1,), (1,)), ((), ()))
TN = (((0,), (0,)), ((), ()))
BF16 = jnp.bfloat16
F32 = jnp.float32
VMEM_LIMIT = 60 * 2**20


def dot(left, right, dims=NN):
    return lax.dot_general(left, right, dims, preferred_element_type=F32)


class Place:
    def __init__(self):
        f = lax.axis_index("fsdp")
        self.c = lax.axis_index("seq")
        self.z, self.y, self.x = f // 4, (f // 2) % 2, f % 2

    def block(self, z, y, x):
        return z * 4 + y * 2 + x

    def dev(self, z, y, x):
        return (self.block(z, y, x), self.c)

    @property
    def xn(self):
        return self.dev(self.z, self.y, 1 - self.x)

    @property
    def yn(self):
        return self.dev(self.z, 1 - self.y, self.x)

    @property
    def up(self):
        return self.dev(self.z + 1, self.y, self.x)

    @property
    def down(self):
        return self.dev(self.z - 1, self.y, self.x)

    @property
    def partner(self):
        return (self.block(self.z, self.y, self.x), 1 - self.c)


def greet(p):
    barrier = pltpu.get_barrier_semaphore()

    def signal(device):
        pl.semaphore_signal(barrier, inc=1, device_id=device, device_id_type=MESH)

    for device in (p.xn, p.yn, p.partner):
        signal(device)

    @pl.when(p.z < 3)
    def _():
        signal(p.up)

    @pl.when(p.z > 0)
    def _():
        signal(p.down)

    inner = jnp.logical_and(p.z > 0, p.z < 3)

    @pl.when(inner)
    def _():
        pl.semaphore_wait(barrier, 5)

    @pl.when(jnp.logical_not(inner))
    def _():
        pl.semaphore_wait(barrier, 4)


def remote(src, dst, send, recv, device):
    return pltpu.make_async_remote_copy(
        src_ref=src, dst_ref=dst, send_sem=send, recv_sem=recv, device_id=device, device_id_type=MESH
    )


def wait_bytes(ref, sem):
    pltpu.make_async_copy(ref, ref, sem).wait()


AG_SEMS = 24


class Gather:
    def __init__(self, p, src, dst, sems):
        self.p, self.src, self.dst, self.sems = p, src, dst, sems
        self.rz = [None] * 4
        self.send, self.zsend, self.local, self.rp = (sems.at[20], sems.at[21], sems.at[22], sems.at[23])

    def half(self, z, y, x):
        return self.dst.at[2 * self.p.block(z, y, x) + self.p.c]

    def to(self, src, dst, recv, device, send=None):
        remote(src, dst, self.send if send is None else send, self.sems.at[recv], device).start()

    def spread(self, src, z):
        p = self.p
        mine = self.half(z, p.y, p.x)
        self.to(src, mine, 4 + z, p.xn)
        self.to(src, mine, 8 + z, p.yn)

    def along(self, src, z, up):
        p = self.p
        mine = self.half(z, p.y, p.x)

        @pl.when(p.z < 3 if up else p.z > 0)
        def _():
            self.to(src, mine, z, p.up if up else p.down, self.zsend)

    def start(self):
        p = self.p
        own = self.src.at[p.c]
        self.along(own, p.z, True)
        self.along(own, p.z, False)
        self.spread(own, p.z)
        me = p.block(p.z, p.y, p.x)
        pltpu.make_async_copy(self.src, self.dst.at[pl.ds(2 * me, 2)], self.local).start()

    def at_distance(self, s, body):
        p = self.p
        if s == 0:
            body(p.z, None)
            return

        @pl.when(p.z - s >= 0)
        def _():
            body(p.z - s, True)

        @pl.when(p.z + s <= 3)
        def _():
            body(p.z + s, False)

    def z_step(self, s):
        p = self.p

        def body(z, up):
            mine = self.half(z, p.y, p.x)
            wait_bytes(mine, self.sems.at[z])
            self.along(mine, z, up)
            self.spread(mine, z)
            self.to(mine, mine, 23, p.partner)

        self.at_distance(s, body)

    def xy_step(self, s):
        p = self.p

        def body(z, up):
            a = self.half(z, p.y, 1 - p.x)
            wait_bytes(a, self.sems.at[4 + z])
            self.to(a.at[0], a.at[0], 12 + z, p.yn)
            self.to(a, a, 23, p.partner)
            b = self.half(z, 1 - p.y, p.x)
            wait_bytes(b, self.sems.at[8 + z])
            self.to(b.at[1], b.at[1], 16 + z, p.xn)
            self.to(b, b, 23, p.partner)

        self.at_distance(s, body)

    def diag_step(self, s):
        p = self.p

        def body(z, up):
            d = self.half(z, 1 - p.y, 1 - p.x)
            wait_bytes(d.at[0], self.sems.at[12 + z])
            wait_bytes(d.at[1], self.sems.at[16 + z])
            self.to(d, d, 23, p.partner)

        self.at_distance(s, body)

    def finish(self):
        p = self.p
        wait_bytes(self.dst.at[pl.ds(0, 15)], self.rp)
        wait_bytes(self.dst.at[pl.ds(0, 27)], self.send)
        wait_bytes(self.dst.at[pl.ds(0, 2)], self.local)
        inner = jnp.logical_and(p.z > 0, p.z < 3)

        @pl.when(inner)
        def _():
            wait_bytes(self.dst.at[pl.ds(0, 5)], self.zsend)

        @pl.when(jnp.logical_not(inner))
        def _():
            wait_bytes(self.dst.at[pl.ds(0, 1)], self.zsend)


def gather_program(gathers):
    steps = []
    n = len(gathers)
    for i in range(n + 1):
        if i < n:
            steps.append(gathers[i].start)
            for s in (1, 2, 3):
                steps.append(lambda g=gathers[i], s=s: g.z_step(s))
        if i >= 1:
            g = gathers[i - 1]
            for s in range(5):
                if s < 4:
                    steps.append(lambda g=g, s=s: g.xy_step(s))
                if s >= 1:
                    steps.append(lambda g=g, s=s: g.diag_step(s - 1))
    for g in gathers:
        steps.append(g.finish)
    return steps


def gather_all(shards, collective_id):
    n = len(shards)
    views = []
    for shard in shards:
        r, width = shard.shape
        views.append(shard.reshape(2, 2, r // 4, width))

    def kernel(*refs):
        p = Place()
        greet(p)
        gathers = [Gather(p, refs[i], refs[n + i], refs[2 * n].at[i]) for i in range(n)]
        for step in gather_program(gathers):
            step()

    outs = pl.pallas_call(
        kernel,
        in_specs=[pl.BlockSpec(memory_space=pltpu.VMEM)] * n,
        out_specs=[pl.BlockSpec(memory_space=pl.ANY)] * n,
        out_shape=[jax.ShapeDtypeStruct((32,) + v.shape[1:], v.dtype) for v in views],
        scratch_shapes=[pltpu.SemaphoreType.DMA((n, AG_SEMS))],
        compiler_params=pltpu.CompilerParams(
            collective_id=collective_id, has_side_effects=True, vmem_limit_bytes=VMEM_LIMIT
        ),
        name="gather",
    )(*views)
    return [out.reshape(16 * shard.shape[0], shard.shape[1]) for out, shard in zip(outs, shards)]


RS_SEMS = 4 * 8 + 8


class Scatter:
    def __init__(self, p, g, out, bufs, sems):
        self.p, self.g, self.out, self.sems = p, g, out, sems
        self.o, self.pr, self.x1, self.y1, self.x2, self.y2, self.u, self.d = bufs
        self.psend, self.zsend, self.fsend, self.frecv = (sems.at[36 + i] for i in range(4))

    @staticmethod
    def scratch(q, width, dtype):
        return [
            pltpu.VMEM((4, 2, 2, 2, q, width), dtype),
            pltpu.VMEM((4, 2, 2, 2, q, width), dtype),
            pltpu.VMEM((4, 2, q, width), dtype),
            pltpu.VMEM((4, 2, q, width), dtype),
            pltpu.VMEM((4, q, width), dtype),
            pltpu.VMEM((4, q, width), dtype),
            pltpu.VMEM((4, 2, q, width), dtype),
            pltpu.VMEM((4, 2, q, width), dtype),
        ]

    def level(self, i):
        z = self.p.z
        return jnp.where(z < 2, 3 - i, i)

    def sem(self, kind, i):
        return self.sems.at[4 * kind + i]

    def start(self):
        p = self.p
        for i in range(4):
            z = self.level(i)
            theirs = self.g.at[z, :, :, 1 - p.c]
            remote(theirs, self.pr.at[z], self.psend, self.sem(0, i), p.partner).start()
            pltpu.make_async_copy(self.g.at[z, :, :, p.c], self.o.at[z], self.sem(1, i)).start()

    def stage0(self, i):
        p = self.p
        z = self.level(i)
        wait_bytes(self.o.at[z], self.sem(1, i))
        wait_bytes(self.pr.at[z], self.sem(0, i))

        def add(j, carry):
            y, x, k = j // 4, (j // 2) % 2, j % 2
            self.o[z, y, x, k] = self.o[z, y, x, k] + self.pr[z, y, x, k]
            return carry

        lax.fori_loop(0, 8, add, 0)
        remote(self.o.at[z, :, 1 - p.x, 0], self.x1.at[z], self.sems.at[32], self.sem(2, i), p.xn).start()
        remote(self.o.at[z, 1 - p.y, :, 1], self.y1.at[z], self.sems.at[33], self.sem(3, i), p.yn).start()

    def stage1(self, i):
        p = self.p
        z = self.level(i)
        wait_bytes(self.x1.at[z], self.sem(2, i))
        for y in range(2):
            self.o[z, y, p.x, 0] = self.o[z, y, p.x, 0] + self.x1[z, y]
        remote(self.o.at[z, 1 - p.y, p.x, 0], self.y2.at[z], self.sems.at[35], self.sem(4, i), p.yn).start()
        wait_bytes(self.y1.at[z], self.sem(3, i))
        for x in range(2):
            self.o[z, p.y, x, 1] = self.o[z, p.y, x, 1] + self.y1[z, x]
        remote(self.o.at[z, p.y, 1 - p.x, 1], self.x2.at[z], self.sems.at[34], self.sem(5, i), p.xn).start()

    def stage2(self, i):
        p = self.p
        z = self.level(i)
        wait_bytes(self.y2.at[z], self.sem(4, i))
        wait_bytes(self.x2.at[z], self.sem(5, i))
        self.o[z, p.y, p.x, 0] = self.o[z, p.y, p.x, 0] + self.y2[z]
        self.o[z, p.y, p.x, 1] = self.o[z, p.y, p.x, 1] + self.x2[z]

    def chain(self, z, up):
        p = self.p
        buf = self.u if up else self.d
        kind = 6 if up else 7
        mine = self.o.at[z, p.y, p.x]

        @pl.when(p.z > 0 if up else p.z < 3)
        def _():
            wait_bytes(buf.at[z], self.sems.at[4 * kind + z])
            self.o[z, p.y, p.x] = self.o[z, p.y, p.x] + buf[z]

        remote(mine, buf.at[z], self.zsend, self.sems.at[4 * kind + z], p.up if up else p.down).start()

    def stage3(self, i):
        p = self.p
        z = self.level(i)

        @pl.when(z > p.z)
        def _():
            self.chain(z, True)

        @pl.when(z < p.z)
        def _():
            self.chain(z, False)

    def stage4(self):
        p = self.p
        z = p.z
        self.out[p.c] = self.o[z, p.y, p.x].astype(F32)

        @pl.when(z > 0)
        def _():
            wait_bytes(self.u.at[z], self.sems.at[24 + z])
            self.out[p.c] = self.out[p.c] + self.u[z].astype(F32)

        @pl.when(z < 3)
        def _():
            wait_bytes(self.d.at[z], self.sems.at[28 + z])
            self.out[p.c] = self.out[p.c] + self.d[z].astype(F32)

        remote(self.out.at[p.c], self.out.at[p.c], self.fsend, self.frecv, p.partner).start()

    def finish(self):
        p = self.p
        wait_bytes(self.out.at[1 - p.c], self.frecv)
        wait_bytes(self.out.at[p.c], self.fsend)
        wait_bytes(self.o, self.psend)
        for k, ref in enumerate((self.x1, self.y1, self.x2, self.y2)):
            wait_bytes(ref, self.sems.at[32 + k])
        wait_bytes(self.u.at[pl.ds(0, 3)], self.zsend)


def scatter_program(scatters):
    steps = []
    for s in scatters:
        steps.append(s.start)
    chunks = [(s, i) for s in scatters for i in range(4)]
    n = len(chunks)
    for t in range(n + 12):
        for lag, name in ((0, "stage0"), (3, "stage1"), (6, "stage2"), (6, "stage3")):
            k = t - lag
            if 0 <= k < n:
                s, i = chunks[k]
                steps.append(lambda s=s, i=i, name=name: getattr(s, name)(i))
        k = t - 12
        if 0 <= k < n and chunks[k][1] == 3:
            steps.append(chunks[k][0].stage4)
    for s in scatters:
        steps.append(s.finish)
    return steps


def scatter_all(grads, collective_id):
    n = len(grads)
    views = []
    for grad in grads:
        rows, width = grad.shape
        views.append(grad.reshape(4, 2, 2, 2, 2, rows // 64, width))
    scratch = []
    for v in views:
        scratch += Scatter.scratch(v.shape[5], v.shape[6], v.dtype)

    def kernel(*refs):
        p = Place()
        greet(p)
        bufs = refs[2 * n : 2 * n + 8 * n]
        sems = refs[10 * n]
        scatters = [Scatter(p, refs[i], refs[n + i], bufs[8 * i : 8 * i + 8], sems.at[i]) for i in range(n)]
        for step in scatter_program(scatters):
            step()

    outs = pl.pallas_call(
        kernel,
        in_specs=[pl.BlockSpec(memory_space=pl.ANY)] * n,
        out_specs=[pl.BlockSpec(memory_space=pltpu.VMEM)] * n,
        out_shape=[jax.ShapeDtypeStruct((2, 2) + v.shape[5:], F32) for v in views],
        scratch_shapes=scratch + [pltpu.SemaphoreType.DMA((n, RS_SEMS))],
        compiler_params=pltpu.CompilerParams(
            collective_id=collective_id, has_side_effects=True, vmem_limit_bytes=VMEM_LIMIT
        ),
        name="scatter",
    )(*views)
    return [out.reshape(grad.shape[0] // 16, grad.shape[1]) for out, grad in zip(outs, grads)]


def lane_masks(rows, width, dtype=BF16):
    lanes = lax.broadcasted_iota(jnp.int32,(rows,width),1)
    return lanes < width//2
def pick(h, low, v):
    z=jnp.zeros_like(v)
    return jnp.where(low, v, z) if h==0 else jnp.where(low, z, v)
def fwd_body(q_ref,k_ref,v_ref,o_ref,l_ref, B):
    S=q_ref.shape[0]
    low=lane_masks(S,128)
    q=q_ref[...]*BF16(0.125); k=k_ref[...]; v=v_ref[...]
    qs=[pick(h,low,q) for h in (0,1)]; vs=[pick(h,low,v) for h in (0,1)]
    for b in range(S//B):
        end=(b+1)*B
        acc=None
        for h in (0,1):
            st=dot(k[:end],qs[h][b*B:end],NT)
            key=lax.broadcasted_iota(jnp.int32,(B,B),0); qry=lax.broadcasted_iota(jnp.int32,(B,B),1)
            diag=jnp.where(key<=qry, st[b*B:end], NEG_LARGE)
            st=jnp.concatenate([st[:b*B],diag],0) if b else diag
            m=jnp.max(st,0,keepdims=True)
            p=jnp.exp(st-m)
            l=jnp.sum(p,0,keepdims=True)
            l_ref[h:h+1,b*B:end]=m+jnp.log(l)
            pt=(p*(1.0/l)).astype(BF16)
            o=dot(pt,vs[h][:end],TN)
            acc=o if acc is None else acc+o
        o_ref[b*B:end,:]=acc.astype(BF16)
def bwd_body(q_ref,k_ref,v_ref,g_ref,l_ref,dq_ref,dk_ref,dv_ref,dk_acc,dv_acc,B):
    S=q_ref.shape[0]
    low=lane_masks(S,128)
    q=q_ref[...]*BF16(0.125); k=k_ref[...]; v=v_ref[...]; g=g_ref[...]
    qs=[pick(h,low,q) for h in (0,1)]; gs=[pick(h,low,g) for h in (0,1)]; ks=[pick(h,low,k) for h in (0,1)]
    for b in reversed(range(S//B)):
        end=(b+1)*B
        dq=None; dk=None; dv=None
        for h in (0,1):
            qb=qs[h][b*B:end]; gb=gs[h][b*B:end]
            st=dot(k[:end],qb,NT)
            p=jnp.exp(st-l_ref[h:h+1,b*B:end])
            key=lax.broadcasted_iota(jnp.int32,(B,B),0); qry=lax.broadcasted_iota(jnp.int32,(B,B),1)
            diag=jnp.where(key<=qry, p[b*B:end], 0.0)
            p=jnp.concatenate([p[:b*B],diag],0) if b else diag
            dp=dot(v[:end],gb,NT)
            inner=jnp.sum(p*dp,0,keepdims=True)
            ds=(p*(dp-inner)).astype(BF16)
            pb=p.astype(BF16)
            dvh=dot(pb,gb,NN); dkh=dot(ds,qb,NN); dqh=dot(ds,ks[h][:end],TN)
            dq=dqh if dq is None else dq+dqh
            dk=dkh if dk is None else dk+dkh
            dv=dvh if dv is None else dv+dvh
        dq_ref[b*B:end,:]=(dq*0.125).astype(BF16)
        if b==S//B-1:
            dk_acc[...]=dk; dv_acc[...]=dv
        else:
            dk_acc[:end,:]+=dk; dv_acc[:end,:]+=dv
    dk_ref[...]=dk_acc[...].astype(BF16)
    dv_ref[...]=dv_acc[...].astype(BF16)
def attn_fwd(merged, S, B=256):
    T=merged.shape[0]; D=merged.shape[1]//3; n=D//128
    def body(q,k,v,o,l): fwd_body(q,k,v,o,l.at[0,0],B)
    sp=lambda off: pl.BlockSpec((S,128),lambda s,h: (s,off+h))
    return pl.pallas_call(body,grid=(T//S,n),in_specs=[sp(0),sp(n),sp(2*n)],
        out_specs=[pl.BlockSpec((S,128),lambda s,h:(s,h)),pl.BlockSpec((1,1,2,S),lambda s,h:(s,h,0,0))],
        out_shape=[jax.ShapeDtypeStruct((T,D),BF16),jax.ShapeDtypeStruct((T//S,n,2,S),F32)],
        name="attn_fwd",compiler_params=pltpu.CompilerParams(vmem_limit_bytes=40*2**20))(merged,merged,merged)
def attn_bwd(merged, g, lse, S, B=256):
    T=merged.shape[0]; D=merged.shape[1]//3; n=D//128
    def body(q,k,v,gr,l,d,dka,dva): bwd_body(q,k,v,gr,l.at[0,0],d.at[0],d.at[1],d.at[2],dka,dva,B)
    sp=lambda off: pl.BlockSpec((S,128),lambda s,h: (s,off+h))
    return pl.pallas_call(body,grid=(T//S,n),in_specs=[sp(0),sp(n),sp(2*n),sp(0),pl.BlockSpec((1,1,2,S),lambda s,h:(s,h,0,0))],
        out_specs=pl.BlockSpec((3,S,128),lambda s,h:(0,s,h)),
        out_shape=jax.ShapeDtypeStruct((3,T,D),BF16),
        scratch_shapes=[pltpu.VMEM((S,128),F32)]*2,
        name="attn_bwd",compiler_params=pltpu.CompilerParams(vmem_limit_bytes=40*2**20))(merged,merged,merged,g,lse)


def layer_norm(values, gain, shift):
    center = values - jnp.mean(values, -1, keepdims=True)
    spread = jnp.mean(center * center, -1, keepdims=True)
    return center * lax.rsqrt(spread + EPSILON) * gain + shift


def norm_back(values, gain, grad):
    center = values - jnp.mean(values, -1, keepdims=True)
    inverse = lax.rsqrt(jnp.mean(center * center, -1, keepdims=True) + EPSILON)
    unit = center * inverse
    scaled = grad * gain
    first = jnp.mean(scaled, -1, keepdims=True)
    second = jnp.mean(scaled * unit, -1, keepdims=True)
    return (inverse * (scaled - first - unit * second), jnp.sum(grad * unit, 0), jnp.sum(grad, 0))


def gelu_pair(u):
    a = 0.7978845608028654
    inner = jnp.tanh(a * (u + 0.044715 * u * u * u))
    half = 0.5 * (1.0 + inner)
    slope = half + 0.5 * u * (1.0 - inner * inner) * (a * (1.0 + 3.0 * 0.044715 * u * u))
    return u * half, slope


def up_project(normed, w_up, b_up):
    rows, depth = normed.shape
    width = w_up.shape[1]
    tile = 512

    def body(n_ref, w_ref, b_ref, a_ref, s_ref):
        value, slope = gelu_pair(dot(n_ref[...], w_ref[...]) + b_ref[...])
        a_ref[...] = value.astype(BF16)
        s_ref[...] = slope.astype(BF16)

    out = pl.BlockSpec((rows // 2, tile), lambda j, i: (i, j))
    return pl.pallas_call(
        body,
        grid=(width // tile, 2),
        in_specs=[
            pl.BlockSpec((rows // 2, depth), lambda j, i: (i, 0)),
            pl.BlockSpec((depth, tile), lambda j, i: (0, j)),
            pl.BlockSpec((1, tile), lambda j, i: (0, j)),
        ],
        out_specs=[out, out],
        out_shape=[jax.ShapeDtypeStruct((rows, width), BF16)] * 2,
        compiler_params=pltpu.CompilerParams(vmem_limit_bytes=VMEM_LIMIT),
        name="up_project",
    )(normed, w_up, b_up)


def compute(rows, upstream, weights, small):
    w_qkv, w_out, w_up, w_down = weights
    b_query, b_value, b_out, b_up, b_down, gain_one, shift_one, gain_two, shift_two = small
    length, width = rows.shape[1], rows.shape[2]
    tokens = rows.shape[0] * length
    x = rows.reshape(tokens, width)
    c = upstream.reshape(tokens, width)
    xf, cf = x.astype(F32), c.astype(F32)
    normed_one = layer_norm(xf, gain_one, shift_one).astype(BF16)
    qkv_bias = jnp.concatenate([b_query, jnp.zeros_like(b_query), b_value])
    merged = (dot(normed_one, w_qkv) + qkv_bias).astype(BF16)
    attended, logsum = attn_fwd(merged, length)
    middle = xf + (dot(attended, w_out) + b_out)
    normed_two = layer_norm(middle, gain_two, shift_two).astype(BF16)
    activated, slope = up_project(normed_two, w_up, b_up[None])
    output = (middle + (dot(activated, w_down) + b_down)).astype(BF16)

    grad_down_bias = jnp.sum(cf, 0)
    grad_down = dot(activated, c, TN).astype(BF16)
    hidden_grad = (dot(c, w_down, NT) * slope.astype(F32)).astype(BF16)
    grad_up_bias = jnp.sum(hidden_grad.astype(F32), 0)
    grad_up = dot(normed_two, hidden_grad, TN).astype(BF16)
    part, grad_gain_two, grad_shift_two = norm_back(middle, gain_two, dot(hidden_grad, w_up, NT))
    middle_grad = cf + part
    branch_grad = middle_grad.astype(BF16)
    grad_out_bias = jnp.sum(branch_grad.astype(F32), 0)
    grad_out = dot(attended, branch_grad, TN).astype(BF16)
    attended_grad = dot(branch_grad, w_out, NT).astype(BF16)
    back = attn_bwd(merged, attended_grad, logsum, length)
    grad_query_bias = jnp.sum(back[0].astype(F32), 0)
    grad_value_bias = jnp.sum(back[2].astype(F32), 0)
    grad_qkv = jnp.concatenate([dot(normed_one, back[j], TN).astype(BF16) for j in range(3)], 1)
    normed_one_grad = sum(dot(back[j], w_qkv[:, j * width : (j + 1) * width], NT) for j in range(3))
    part, grad_gain_one, grad_shift_one = norm_back(xf, gain_one, normed_one_grad)
    input_grad = middle_grad + part
    return (
        output.reshape(rows.shape),
        input_grad.reshape(rows.shape),
        (grad_qkv, grad_out, grad_up, grad_down),
        (
            grad_query_bias,
            grad_value_bias,
            grad_out_bias,
            grad_up_bias,
            grad_down_bias,
            grad_gain_one,
            grad_shift_one,
            grad_gain_two,
            grad_shift_two,
        ),
    )


def pack_shards(vectors):
    wide = vectors[3]
    narrow = jnp.stack([v for k, v in enumerate(vectors) if k != 3])
    zeros = jnp.zeros_like(narrow)
    odd = lax.axis_index("fsdp") % 2 == 1
    lanes = jnp.concatenate([jnp.where(odd, zeros, narrow), jnp.where(odd, narrow, zeros)], 1)
    rows = jnp.concatenate([lanes, wide.reshape(2, 128)], 0)
    return jnp.pad(rows, ((0, 64 - rows.shape[0]), (0, 0)))


def unpack_whole(packed):
    blocks = packed.reshape(8, 2, 64, 128)
    narrow = (blocks[:, 0, :8] + blocks[:, 1, :8]).astype(F32)
    narrow = jnp.moveaxis(narrow, 0, 1).reshape(8, 1024)
    wide = blocks[:, :, 8:10].astype(F32).reshape(4096)
    return tuple(narrow[j] for j in range(3)) + (wide,) + tuple(narrow[j] for j in range(3, 8))


def pack_grads(vectors):
    narrow = jnp.stack([v for k, v in enumerate(vectors) if k != 3]).reshape(8, 8, 128)
    narrow = jnp.repeat(jnp.moveaxis(narrow, 1, 0), 2, axis=0)
    wide = vectors[3].reshape(16, 2, 128)
    rows = jnp.concatenate([narrow, wide], 1)
    return jnp.pad(rows, ((0, 0), (0, 22), (0, 0))).reshape(16 * 32, 128)


def unpack_shard(packed):
    odd = lax.axis_index("fsdp") % 2 == 1
    narrow = jnp.where(odd, packed[:8, 64:], packed[:8, :64])
    wide = packed[8:10].reshape(256)
    return tuple(narrow[j] for j in range(3)) + (wide,) + tuple(narrow[j] for j in range(3, 8))


def local_ring(block_input, *rest):
    shards, cotangent = rest[:13], rest[13]
    w_qkv, w_out, w_up, w_down, packed = gather_all(shards[:4] + (pack_shards(shards[4:]),), 0)
    small = unpack_whole(packed)
    output, input_grad, mats, vecs = compute(block_input, cotangent, (w_qkv, w_out, w_up, w_down), small)
    grad_down, grad_up, grad_out, grad_qkv, vec = scatter_all(
        [mats[3], mats[2], mats[1], mats[0], pack_grads(vecs)], 1
    )
    return (output, input_grad, grad_qkv, grad_out, grad_up, grad_down) + unpack_shard(vec)


def local_any(block_input, *rest):
    shards, cotangent = rest[:13], rest[13]
    whole = [lax.all_gather(shard, "fsdp", axis=0, tiled=True) for shard in shards]
    small = tuple(v.astype(F32) for v in whole[4:])
    output, input_grad, mats, vecs = compute(block_input, cotangent, whole[:4], small)

    def reduce(grad):
        part = lax.psum_scatter(grad.astype(F32), "fsdp", scatter_dimension=0, tiled=True)
        return lax.psum(part, "seq")

    return (output, input_grad) + tuple(reduce(grad) for grad in mats + vecs)


def solution(mesh):
    split = P(("fsdp", "seq"), None, None)
    matrix, vector = P("fsdp", None), P("fsdp")
    in_specs = (split,) + (matrix,) * 4 + (vector,) * 9 + (split,)
    out_specs = (split, split) + (matrix,) * 4 + (vector,) * 9
    local = local_ring if (mesh.shape["fsdp"], mesh.shape["seq"]) == (16, 2) else local_any
    return jax.shard_map(local, mesh=mesh, in_specs=in_specs, out_specs=out_specs, check_vma=False)
```

time: 2250 us -> 516 us (0.23)
  waiting for transfers between devices: 1420 us -> 0 us
  Pallas kernels: 0 us -> 339 us
  blocking collectives: 311 us -> 0 us
  matrix products: 383 us -> 120 us
  other arithmetic: 65 us -> 35.2 us
  local copies, waits for them, and re-layouts: 45.4 us -> 17 us
    reduce_scatter x4 -> x0, waiting for transfers between devices: 998 us -> none  [the longest x1 352 us: local(): lax.psum_scatter(totals[3], 'fsdp', scatter_dimension=0, tiled=True)]
    all_gather x8 -> x0, waiting for transfers between devices: 414 us -> none  [the longest x2 209 us: gather_weights(): lax.all_gather(w_up, 'fsdp', axis=0, tiled=True)]
    pallas_call x0 -> x5, Pallas kernels: none -> 339 us  [the longest x1 137 us: gather_all(): pl.pallas_call(kernel, in_specs=[pl.BlockSpec(memory_space=pltpu.VMEM)] *...]
    dot_general x136 -> x15, matrix products: 383 us -> 120 us  [dot(): return lax.dot_general(left, right, dims, preferred_element_type=F32)]
    while x2 -> x0, blocking collectives: 157 us -> none
    unnamed x1 -> x0, blocking collectives: 79.5 us -> none
    all_gather x2 -> x0, blocking collectives: 71.6 us -> none  [gather_weights(): lax.all_gather(b_up, 'fsdp', axis=0, tiled=True)]
    convert_element_type x53 -> x2, other arithmetic: 31.7 us -> 2.95 us  [the longest x1 2.12 us: compute(): normed_two = layer_norm(middle, gain_two, shift_two).astype(BF16)]
  transfers between devices with their start and end apart: 13 -> 0, of which waited for: 8 -> 0; matrix products, arithmetic and copies ran while one was open for 6% -> 0% of each run, Pallas kernels for 0% -> 0%
where the time goes in v1:
time: 516 us; the launch traced here: 512 us
  Pallas kernels  339 us (66%)
  matrix products  120 us (23%)
  other arithmetic  35.2 us (7%)
  local copies, waits for them, and re-layouts  17 us (3%)
    pallas_call x1, Pallas kernels, gather_all(): pl.pallas_call(kernel, in_specs=[pl.BlockSpec(memory_space=pltpu.VMEM)] *...  137 us
    pallas_call x1, Pallas kernels, scatter_all(): pl.pallas_call(kernel, in_specs=[pl.BlockSpec(memory_space=pl.ANY)] * n,...  126 us
    dot_general x15, matrix products, dot(): return lax.dot_general(left, right, dims, preferred_element_type=F32)  120 us
    pallas_call x1, Pallas kernels, attn_bwd(): pl.pallas_call(body, grid=(T // S, n), in_specs=[sp(0), sp(n), sp(2 * n),...  28.2 us
    pallas_call x1, Pallas kernels, up_project(): pl.pallas_call(body, grid=(width // tile, 2), in_specs=[pl.BlockSpec((row...  27.8 us
    pallas_call x1, Pallas kernels, attn_fwd(): pl.pallas_call(body, grid=(T // S, n), in_specs=[sp(0), sp(n), sp(2 * n)]...  20 us
    concatenate x1, other arithmetic, compute(): jnp.concatenate([dot(normed_one, back[j], TN).astype(BF16) for j in range...  13.4 us

profile of v1, /device:TPU:0, one launch (start us, length us, event | category | flops | bytes accessed | tf_op | source)
XLA Modules:
  0.0 512.4 jit_solution(18144989676944772176)
XLA Ops:
  0.6 0.0 copy-start.5
  0.7 0.9 stack.62
  1.6 1.3 fusion.28
  3.0 136.6 %gather.1 = (bf16[32,2,16,3072]{3,2,1,0:T(8,128)(2,1)}, bf16[32,2,16,1024]{3,2,1,0:T(8,128)(2,1)}, bf16[32,2,16,4096]{3,2,1,0:T(8,128)(2,1)}, bf16[32,2,64,1024]{3,2,1,0:T(8,128)(2,1)}, bf16[32,2,16,128]{3,2,1,0:T(8,128)(2,1)}) custom-call(bf16[2,2,16,3072]{3,2,1,0:T(8,128)(2,1)} %bitcast.169, bf16[2,2,16,1024]{3,2,1,0:T(8,128)(2,1)} %bitcast.172, ...), custom_call_target="tpu_custom_call" | custom-call | tf_op jit(solution)/shard_map/gather/pallas_call | solution.py:234
  139.6 0.7 convert_bitcast_fusion
  140.4 0.6 fusion.34
  141.0 2.1 convert_reduce_fusion.1
  143.1 0.0 copy-done.5
  143.1 0.7 fusion.3
  143.8 0.8 fusion.6
  144.6 0.0 copy-start.13
  144.7 1.3 copy-done.13
  146.0 7.3 %add_convert_fusion.q.k.v = bf16[1024,3072]{1,0:T(8,128)(2,1)S(1)} fusion(f32[3072]{0:T(1024)S(1)} %pad_maximum_fusion.1, bf16[1024,1024]{1,0:T(8,128)(2,1)S(1)} %bitcast.159, bf16[1024,3072]{1,0:T(8,128)(2,1)S(1)} %bitcast.219), kind=kOutput, calls=%fused_computation.3 | convolution fusion | flops 6448742400 | bytes 14692352 | tf_op jit(solution)/shard_map/dot_general | solution.py:20
  153.3 0.0 copy-start.6
  153.3 0.0 copy-start.21
  153.3 20.0 %attn_fwd.1 = (bf16[1024,1024]{1,0:T(8,128)(2,1)S(1)}, f32[2,8,2,512]{3,2,1,0:T(2,128)S(1)}) custom-call(bf16[1024,3072]{1,0:T(8,128)(2,1)S(1)} %add_convert_fusion.q.k.v, bf16[1024,3072]{1,0:T(8,128)(2,1)S(1)} %add_convert_fusion.q.k.v, bf16[1024,3072]{1,0:T(8,128)(2,1)S(1)} %add_convert_fusion.q.k.v), custom_call_target="tpu_custom_call" | custom-call | tf_op jit(solution)/shard_map/attn_fwd/pallas_call | solution.py:486
  173.3 0.0 copy-done
  173.3 0.0 copy-done.6
  173.3 0.0 copy-done.21
  173.4 2.5 fusion.35
  175.8 0.5 multiply_reduce_fusion.2
  176.4 2.1 add_convert_fusion.2.n_ref
  178.5 1.4 slice_convert_fusion
  179.9 27.8 %up_project.1 = (bf16[1024,4096]{1,0:T(8,128)(2,1)}, bf16[1024,4096]{1,0:T(8,128)(2,1)}) custom-call(bf16[1024,1024]{1,0:T(8,128)(2,1)} %add_convert_fusion.2.n_ref, bf16[1024,4096]{1,0:T(8,128)(2,1)} %bitcast.153, f32[1,4096]{1,0:T(1,128)} %bitcast.175), custom_call_target="tpu_custom_call" | custom-call | tf_op jit(solution)/shard_map/up_project/pallas_call | solution.py:536
  207.7 16.2 %convert_reduce_fusion = (f32[4096]{0:T(1024)S(1)}, bf16[1024,4096]{1,0:T(8,128)(2,1)}) fusion(bf16[1024,4096]{1,0:T(8,128)(2,1)} %get-tuple-element.36, bf16[4096,1024]{1,0:T(8,128)(2,1)} %bitcast.214, bf16[1024,1024]{1,0:T(8,128)(2,1)} %bitcast.155), kind=kOutput, calls=%fused_computation.2 | convolution fusion | flops 8610902016 | bytes 27279360 | tf_op jit(solution)/shard_map/dot_general | solution.py:20
  223.9 0.0 copy-done.3
  223.9 16.4 %multiply_reduce_fusion = (f32[1024]{0:T(1024)S(1)}, f32[1024]{0:T(1024)S(1)}, f32[1024]{0:T(1024)S(1)}, f32[1024]{0:T(1024)S(1)}, f32[1024,1024]{1,0:T(8,128)}) fusion(f32[1024,1024]{1,0:T(8,128)S(1)} %copy-done.3, f32[1024]{0:T(1024)S(1)} %add_rsqrt_fusion, f32[1024]{0:T(1024)S(1)} %broadcast_multiply_fusion.4, f32[1024]{0:T(1024)S(1)} %bitcast.180, ...), kind=kOutput, calls=%fused_computation.26 | convolution fusion | flops 8599367680 | bytes 25194496 | tf_op jit(solution)/shard_map/dot_general | solution.py:20
  240.4 0.0 copy-done.11
  240.4 0.0 copy-start.22
  240.4 3.4 convert_reduce_fusion.3
  243.8 0.0 copy-start.9
  243.8 0.0 copy-done.22
  243.8 2.4 convolution_convert_fusion.6.gr
  246.2 28.2 %attn_bwd.1 = bf16[3,1024,1024]{2,1,0:T(8,128)(2,1)S(1)} custom-call(bf16[1024,3072]{1,0:T(8,128)(2,1)} %copy-done, bf16[1024,3072]{1,0:T(8,128)(2,1)} %copy-done, bf16[1024,3072]{1,0:T(8,128)(2,1)} %copy-done, bf16[1024,1024]{1,0:T(8,128)(2,1)S(1)} %convolution_convert_fusion.6.gr, f32[2,8,2,512]{3,2,1,0:T(2,128)S(1)} %get-tuple-element.37.l), custom_call_target="tpu_custom_call" | custom-call | tf_op jit(solution)/shard_map/attn_bwd/pallas_call | solution.py:494
  274.4 5.5 %fusion.18 = f32[1024,1024]{1,0:T(8,128)S(1)} fusion(bf16[1024,3072]{1,0:T(8,128)(2,1)} %bitcast.216, bf16[3,1024,1024]{2,1,0:T(8,128)(2,1)S(1)} %attn_bwd.1), kind=kOutput, calls=%fused_computation.43 | convolution fusion | flops 2147483648 | bytes 8388608 | tf_op jit(solution)/shard_map/dot_general | solution.py:20
  280.0 0.0 copy-start.7
  280.0 4.1 fusion.16
  284.1 7.2 %fusion.15 = (f32[1024]{0:T(1024)S(1)}, f32[1024]{0:T(1024)S(1)}, f32[1024]{0:T(1024)S(1)}, f32[1024]{0:T(1024)S(1)}, f32[1024,1024]{1,0:T(8,128)}) fusion(bf16[2,512,1024]{2,1,0:T(8,128)(2,1)S(1)} %copy-done.7, f32[1024]{0:T(1024)S(1)} %bitcast.186, f32[1024]{0:T(1024)S(1)} %bitcast.184, f32[1024]{0:T(1024)S(1)} %bitcast.177, ...), kind=kOutput, calls=%fused_computation.25 | convolution fusion | flops 2160062464 | bytes 18903040 | tf_op jit(solution)/shard_map/dot_general | solution.py:20
  291.3 0.8 convert_reduce_fusion.4
  292.1 0.4 convert_reduce_fusion.2
  292.5 0.1 stack.71
  292.6 0.0 slice-start
  292.6 0.7 select_maximum_fusion
  293.3 5.1 convolution_convert_fusion.2
  298.4 0.0 slice-done
  298.4 0.0 slice-done.1
  298.4 2.5 convolution_convert_fusion.3
  300.9 2.5 convolution_convert_fusion.4
  303.3 13.4 %pad_maximum_fusion = bf16[1024,3072]{0,1:T(8,128)(2,1)} fusion(bf16[1024,1024]{0,1:T(8,128)(2,1)S(1)} %convolution_convert_fusion.2, bf16[1024,1024]{0,1:T(8,128)(2,1)S(1)} %convolution_convert_fusion.3, bf16[1024,1024]{0,1:T(8,128)(2,1)S(1)} %convolution_convert_fusion.4), kind=kLoop, calls=%fused_computation.6 | loop fusion | flops 18874368 | bytes 12582912 | tf_op jit(solution)/shard_map/concatenate | solution.py:582
  316.8 8.6 %copy.30 = bf16[1024,3072]{1,0:T(8,128)(2,1)} copy(bf16[1024,3072]{0,1:T(8,128)(2,1)} %pad_maximum_fusion) | data formatting | bytes 12582912 | tf_op jit(solution)/shard_map/concatenate | solution.py:582
  325.4 14.9 %convolution_convert_fusion = bf16[1024,4096]{1,0:T(8,128)(2,1)} fusion(bf16[1024,1024]{1,0:T(8,128)(2,1)} %add_convert_fusion.2.n_ref, bf16[1024,4096]{1,0:T(8,128)(2,1)} %get-tuple-element.82), kind=kOutput, calls=%fused_computation.4 | convolution fusion | flops 8594128896 | bytes 18874368 | tf_op jit(solution)/shard_map/dot_general | solution.py:20
  340.4 3.7 convolution_convert_fusion.5
  344.1 14.8 %convolution_convert_fusion.1 = bf16[4096,1024]{1,0:T(8,128)(2,1)} fusion(bf16[1024,4096]{1,0:T(8,128)(2,1)} %get-tuple-element.34, bf16[1024,1024]{1,0:T(8,128)(2,1)S(1)} %bitcast.156), kind=kOutput, calls=%fused_computation.5 | convolution fusion | flops 8594128896 | bytes 18874368 | tf_op jit(solution)/shard_map/dot_general | solution.py:20
  358.9 126.3 %scatter.1 = (f32[2,2,64,1024]{3,2,1,0:T(8,128)}, f32[2,2,16,4096]{3,2,1,0:T(8,128)}, f32[2,2,16,1024]{3,2,1,0:T(8,128)}, f32[2,2,16,3072]{3,2,1,0:T(8,128)}, f32[2,2,8,128]{3,2,1,0:T(8,128)}) custom-call(bf16[4,2,2,2,2,64,1024]{6,5,4,3,2,1,0:T(8,128)(2,1)} %bitcast.152, bf16[4,2,2,2,2,16,4096]{6,5,4,3,2,1,0:T(8,128)(2,1)} %bitcast.151, ...), custom_call_target="tpu_custom_call" | custom-call | tf_op jit(solution)/shard_map/scatter/pallas_call | solution.py:411
  485.3 0.8 slice_select_fusion
  486.1 0.5 slice_bitcast_fusion.10
  486.6 1.2 slice_bitcast_fusion.9
  487.9 0.0 copy-start.19
  487.9 5.9 %fusion.14 = f32[1024,1024]{1,0:T(8,128)} fusion(f32[1024,1024]{1,0:T(8,128)} %copy-done.9, bf16[2,512,1024]{2,1,0:T(8,128)(2,1)S(1)} %copy-done.8, f32[1024,1024]{1,0:T(8,128)} %get-tuple-element.80, f32[1024]{0:T(1024)S(1)} %broadcast_multiply_fusion, f32[1024]{0:T(1024)S(1)} %bitcast.187, f32[1024]{0:T(1024)S(1)} %broadcast_multiply_fusion.1, ...), kind=kLoop, calls=%fused_computation.24 | loop fusion | flops 9437184 | bytes 14700544 | tf_op jit(solution)/shard_map/add | solution.py:585
  493.8 14.8 %add_convert_fusion.1 = bf16[1024,1024]{1,0:T(8,128)(2,1)} fusion(f32[1024,1024]{1,0:T(8,128)S(1)} %copy-done.4, f32[1024]{0:T(1024)S(1)} %bitcast.199, bf16[1024,4096]{1,0:T(8,128)(2,1)} %get-tuple-element.34, bf16[4096,1024]{1,0:T(8,128)(2,1)} %bitcast.215), kind=kOutput, calls=%fused_computation.34 | convolution fusion | flops 8593080320 | bytes 23072768 | tf_op jit(solution)/shard_map/dot_general | solution.py:20
  508.6 0.9 copy.37
  509.5 0.7 copy.38
  510.2 1.0 copy.39
  511.2 1.0 copy.40
  (45 shorter events, 0.1 us)
Async XLA Ops:
  0.6 142.4 %copy-start.5 = (bf16[2,512,1024]{2,1,0:T(8,128)(2,1)S(1)}, bf16[2,512,1024]{2,1,0:T(8,128)(2,1)}, u32[]{:S(2)}) copy-start(bf16[2,512,1024]{2,1,0:T(8,128)(2,1)} %param.15) | copy-start | bytes 6291460
  141.0 5.0 copy-start.20
  144.6 1.4 copy-start.13
  153.3 20.0 %copy-start = (bf16[1024,3072]{1,0:T(8,128)(2,1)}, bf16[1024,3072]{1,0:T(8,128)(2,1)S(1)}, u32[]{:S(2)}) copy-start(bf16[1024,3072]{1,0:T(8,128)(2,1)S(1)} %add_convert_fusion.q.k.v) | copy-start | bytes 18874372
  153.3 20.0 %copy-start.6 = (bf16[2,512,1024]{2,1,0:T(8,128)(2,1)S(1)}, bf16[2,512,1024]{2,1,0:T(8,128)(2,1)}, u32[]{:S(2)}) copy-start(bf16[2,512,1024]{2,1,0:T(8,128)(2,1)} %param.15) | copy-start | bytes 6291460
  153.3 20.0 %copy-start.21 = (bf16[32,2,16,1024]{3,2,1,0:T(8,128)(2,1)S(1)}, bf16[32,2,16,1024]{3,2,1,0:T(8,128)(2,1)}, u32[]{:S(2)}) copy-start(bf16[32,2,16,1024]{3,2,1,0:T(8,128)(2,1)} %get-tuple-element.32) | copy-start | bytes 6291460
  175.8 2.7 copy-start.2
  207.7 16.2 %copy-start.3 = (f32[1024,1024]{1,0:T(8,128)S(1)}, f32[1024,1024]{1,0:T(8,128)}, u32[]{:S(2)}) copy-start(f32[1024,1024]{1,0:T(8,128)} %copy-done.2) | copy-start | bytes 12582916
  223.9 16.4 %copy-start.11 = (bf16[2,512,1024]{2,1,0:T(8,128)(2,1)S(1)}, bf16[2,512,1024]{2,1,0:T(8,128)(2,1)}, u32[]{:S(2)}) copy-start(bf16[2,512,1024]{2,1,0:T(8,128)(2,1)} %param.29) | copy-start | bytes 6291460
  240.4 3.4 copy-start.22
  243.8 2.4 copy-start.9
  274.4 16.9 %copy-start.1 = (bf16[3,1024,1024]{2,1,0:T(8,128)(2,1)}, bf16[3,1024,1024]{2,1,0:T(8,128)(2,1)S(1)}, u32[]{:S(2)}) copy-start(bf16[3,1024,1024]{2,1,0:T(8,128)(2,1)S(1)} %attn_bwd.1) | copy-start | bytes 18874372
  280.0 4.1 copy-start.7
  292.6 5.8 %slice-start = ((s8[6291456]{0:T(1024)(128)(4,1)}), s8[4194304]{0:T(1024)(128)(4,1)S(1)}, s32[]{:S(2)}) async-start(s8[6291456]{0:T(1024)(128)(4,1)} %bitcast.148), calls=%async_computation | async-start | bytes 8388608
  293.3 5.1 slice-start.1
  293.3 5.1 copy-start.14
  325.4 15.0 %copy-start.10 = (f32[1024,1024]{1,0:T(8,128)S(1)}, f32[1024,1024]{1,0:T(8,128)}, u32[]{:S(2)}) copy-start(f32[1024,1024]{1,0:T(8,128)} %copy-done.9) | copy-start | bytes 12582916
  340.4 3.7 copy-start.12
  358.9 129.0 %copy-start.8 = (bf16[2,512,1024]{2,1,0:T(8,128)(2,1)S(1)}, bf16[2,512,1024]{2,1,0:T(8,128)(2,1)}, u32[]{:S(2)}) copy-start(bf16[2,512,1024]{2,1,0:T(8,128)(2,1)} %param.15) | copy-start | bytes 6291460
  487.9 5.9 %copy-start.4 = (f32[1024,1024]{1,0:T(8,128)S(1)}, f32[1024,1024]{1,0:T(8,128)}, u32[]{:S(2)}) copy-start(f32[1024,1024]{1,0:T(8,128)} %copy-done.2) | copy-start | bytes 12582916
  487.9 5.9 %copy-start.19 = (f32[1,8,128]{2,0,1:T(1,128)S(1)}, f32[1,8,128]{2,0,1:T(1,128)}, u32[]{:S(2)}) copy-start(f32[1,8,128]{2,0,1:T(1,128)} %get-tuple-element.56) | copy-start | bytes 12292
  493.8 14.8 %copy-start.17 = (f32[2,2,16,3072]{3,2,1,0:T(8,128)S(1)}, f32[2,2,16,3072]{3,2,1,0:T(8,128)}, u32[]{:S(2)}) copy-start(f32[2,2,16,3072]{3,2,1,0:T(8,128)} %get-tuple-element.38) | copy-start | bytes 2359300
  493.8 15.7 %copy-start.18 = (f32[2,2,16,1024]{3,2,1,0:T(8,128)S(1)}, f32[2,2,16,1024]{3,2,1,0:T(8,128)}, u32[]{:S(2)}) copy-start(f32[2,2,16,1024]{3,2,1,0:T(8,128)} %get-tuple-element.39) | copy-start | bytes 786436
  493.8 16.4 %copy-start.16 = (f32[2,2,16,4096]{3,2,1,0:T(8,128)S(1)}, f32[2,2,16,4096]{3,2,1,0:T(8,128)}, u32[]{:S(2)}) copy-start(f32[2,2,16,4096]{3,2,1,0:T(8,128)} %get-tuple-element.40) | copy-start | bytes 3145732
  508.6 2.6 copy-start.15

commit v2 on v1

--- a/solution.py
+++ b/solution.py
@@ -181,11 +181,13 @@
 
         self.at_distance(s, body)
 
-    def finish(self):
-        p = self.p
+    def arrived(self):
         wait_bytes(self.dst.at[pl.ds(0, 15)], self.rp)
+        wait_bytes(self.dst.at[pl.ds(0, 2)], self.local)
+
+    def drain(self):
+        p = self.p
         wait_bytes(self.dst.at[pl.ds(0, 27)], self.send)
-        wait_bytes(self.dst.at[pl.ds(0, 2)], self.local)
         inner = jnp.logical_and(p.z > 0, p.z < 3)
 
         @pl.when(inner)
@@ -197,75 +199,51 @@
             wait_bytes(self.dst.at[pl.ds(0, 1)], self.zsend)
 
 
-def gather_program(gathers):
-    steps = []
-    n = len(gathers)
-    for i in range(n + 1):
-        if i < n:
-            steps.append(gathers[i].start)
-            for s in (1, 2, 3):
-                steps.append(lambda g=gathers[i], s=s: g.z_step(s))
-        if i >= 1:
-            g = gathers[i - 1]
-            for s in range(5):
-                if s < 4:
-                    steps.append(lambda g=g, s=s: g.xy_step(s))
-                if s >= 1:
-                    steps.append(lambda g=g, s=s: g.diag_step(s - 1))
-    for g in gathers:
-        steps.append(g.finish)
-    return steps
-
-
-def gather_all(shards, collective_id):
-    n = len(shards)
-    views = []
-    for shard in shards:
-        r, width = shard.shape
-        views.append(shard.reshape(2, 2, r // 4, width))
-
-    def kernel(*refs):
-        p = Place()
-        greet(p)
-        gathers = [Gather(p, refs[i], refs[n + i], refs[2 * n].at[i]) for i in range(n)]
-        for step in gather_program(gathers):
-            step()
-
-    outs = pl.pallas_call(
-        kernel,
-        in_specs=[pl.BlockSpec(memory_space=pltpu.VMEM)] * n,
-        out_specs=[pl.BlockSpec(memory_space=pl.ANY)] * n,
-        out_shape=[jax.ShapeDtypeStruct((32,) + v.shape[1:], v.dtype) for v in views],
-        scratch_shapes=[pltpu.SemaphoreType.DMA((n, AG_SEMS))],
-        compiler_params=pltpu.CompilerParams(
-            collective_id=collective_id, has_side_effects=True, vmem_limit_bytes=VMEM_LIMIT
-        ),
-        name="gather",
-    )(*views)
-    return [out.reshape(16 * shard.shape[0], shard.shape[1]) for out, shard in zip(outs, shards)]
-
-
-RS_SEMS = 4 * 8 + 8
+def z_steps(g):
+    return [g.start] + [lambda s=s: g.z_step(s) for s in (1, 2, 3)]
+
+
+def xy_steps(g):
+    return [lambda s=s: g.xy_step(s) for s in range(4)]
+
+
+def diag_steps(g):
+    return [lambda s=s: g.diag_step(s) for s in range(4)]
+
+
+def weave(*lists):
+    return [item[k] for k in range(max(map(len, lists))) for item in lists if k < len(item)]
+
+
+def hook(index, table):
+    for k, steps in table.items():
+
+        @pl.when(index == k)
+        def _(steps=steps):
+            for step in steps:
+                step()
+
+
+def spread(steps, slots):
+    table = {}
+    for k, step in enumerate(steps):
+        table.setdefault(slots[min(k * len(slots) // len(steps), len(slots) - 1)], []).append(step)
+    return table
+
+
+RS_SEMS = 44
 
 
 class Scatter:
-    def __init__(self, p, g, out, bufs, sems):
-        self.p, self.g, self.out, self.sems = p, g, out, sems
-        self.o, self.pr, self.x1, self.y1, self.x2, self.y2, self.u, self.d = bufs
+    def __init__(self, p, g, out, pr, bufs, tmp, sems):
+        self.p, self.g, self.out, self.pr, self.tmp, self.sems = p, g, out, pr, tmp, sems
+        self.o, self.x1, self.y1, self.x2, self.y2, self.u, self.d = bufs
         self.psend, self.zsend, self.fsend, self.frecv = (sems.at[36 + i] for i in range(4))
 
     @staticmethod
     def scratch(q, width, dtype):
-        return [
-            pltpu.VMEM((4, 2, 2, 2, q, width), dtype),
-            pltpu.VMEM((4, 2, 2, 2, q, width), dtype),
-            pltpu.VMEM((4, 2, q, width), dtype),
-            pltpu.VMEM((4, 2, q, width), dtype),
-            pltpu.VMEM((4, q, width), dtype),
-            pltpu.VMEM((4, q, width), dtype),
-            pltpu.VMEM((4, 2, q, width), dtype),
-            pltpu.VMEM((4, 2, q, width), dtype),
-        ]
+        shapes = [(4, 2, 2, 2), (4, 2), (4, 2), (4,), (4,), (4, 2), (4, 2)]
+        return [pltpu.VMEM(shape + (q, width), dtype) for shape in shapes]
 
     def level(self, i):
         z = self.p.z
@@ -282,15 +260,20 @@
             remote(theirs, self.pr.at[z], self.psend, self.sem(0, i), p.partner).start()
             pltpu.make_async_copy(self.g.at[z, :, :, p.c], self.o.at[z], self.sem(1, i)).start()
 
+    def fetch(self, i):
+        z = self.level(i)
+        wait_bytes(self.pr.at[z], self.sem(0, i))
+        pltpu.make_async_copy(self.pr.at[z], self.tmp.at[i % 2], self.sems.at[40 + i]).start()
+
     def stage0(self, i):
         p = self.p
         z = self.level(i)
         wait_bytes(self.o.at[z], self.sem(1, i))
-        wait_bytes(self.pr.at[z], self.sem(0, i))
+        wait_bytes(self.tmp.at[i % 2], self.sems.at[40 + i])
 
         def add(j, carry):
             y, x, k = j // 4, (j // 2) % 2, j % 2
-            self.o[z, y, x, k] = self.o[z, y, x, k] + self.pr[z, y, x, k]
+            self.o[z, y, x, k] = self.o[z, y, x, k] + self.tmp[i % 2, y, x, k]
             return carry
 
         lax.fori_loop(0, 8, add, 0)
@@ -309,6 +292,20 @@
             self.o[z, p.y, x, 1] = self.o[z, p.y, x, 1] + self.y1[z, x]
         remote(self.o.at[z, p.y, 1 - p.x, 1], self.x2.at[z], self.sems.at[34], self.sem(5, i), p.xn).start()
 
+    def along(self, z, up):
+        p = self.p
+        buf, kind = (self.u, 6) if up else (self.d, 7)
+        remote(
+            self.o.at[z, p.y, p.x], buf.at[z], self.zsend, self.sems.at[4 * kind + z], p.up if up else p.down
+        ).start()
+
+    def chain(self, z, up):
+        p = self.p
+        buf, kind = (self.u, 6) if up else (self.d, 7)
+        wait_bytes(buf.at[z], self.sems.at[4 * kind + z])
+        self.o[z, p.y, p.x] = self.o[z, p.y, p.x] + buf[z]
+        self.along(z, up)
+
     def stage2(self, i):
         p = self.p
         z = self.level(i)
@@ -317,32 +314,28 @@
         self.o[z, p.y, p.x, 0] = self.o[z, p.y, p.x, 0] + self.y2[z]
         self.o[z, p.y, p.x, 1] = self.o[z, p.y, p.x, 1] + self.x2[z]
 
-    def chain(self, z, up):
-        p = self.p
-        buf = self.u if up else self.d
-        kind = 6 if up else 7
-        mine = self.o.at[z, p.y, p.x]
-
-        @pl.when(p.z > 0 if up else p.z < 3)
-        def _():
-            wait_bytes(buf.at[z], self.sems.at[4 * kind + z])
-            self.o[z, p.y, p.x] = self.o[z, p.y, p.x] + buf[z]
-
-        remote(mine, buf.at[z], self.zsend, self.sems.at[4 * kind + z], p.up if up else p.down).start()
+        @pl.when(jnp.logical_and(p.z == 0, z > 0))
+        def _():
+            self.along(z, True)
+
+        @pl.when(jnp.logical_and(p.z == 3, z < 3))
+        def _():
+            self.along(z, False)
 
     def stage3(self, i):
         p = self.p
         z = self.level(i)
-
-        @pl.when(z > p.z)
+        inner = jnp.logical_and(p.z > 0, p.z < 3)
+
+        @pl.when(jnp.logical_and(inner, z > p.z))
         def _():
             self.chain(z, True)
 
-        @pl.when(z < p.z)
+        @pl.when(jnp.logical_and(inner, z < p.z))
         def _():
             self.chain(z, False)
 
-    def stage4(self):
+    def stage4(self, i=0):
         p = self.p
         z = p.z
         self.out[p.c] = self.o[z, p.y, p.x].astype(F32)
@@ -367,59 +360,6 @@
         for k, ref in enumerate((self.x1, self.y1, self.x2, self.y2)):
             wait_bytes(ref, self.sems.at[32 + k])
         wait_bytes(self.u.at[pl.ds(0, 3)], self.zsend)
-
-
-def scatter_program(scatters):
-    steps = []
-    for s in scatters:
-        steps.append(s.start)
-    chunks = [(s, i) for s in scatters for i in range(4)]
-    n = len(chunks)
-    for t in range(n + 12):
-        for lag, name in ((0, "stage0"), (3, "stage1"), (6, "stage2"), (6, "stage3")):
-            k = t - lag
-            if 0 <= k < n:
-                s, i = chunks[k]
-                steps.append(lambda s=s, i=i, name=name: getattr(s, name)(i))
-        k = t - 12
-        if 0 <= k < n and chunks[k][1] == 3:
-            steps.append(chunks[k][0].stage4)
-    for s in scatters:
-        steps.append(s.finish)
-    return steps
-
-
-def scatter_all(grads, collective_id):
-    n = len(grads)
-    views = []
-    for grad in grads:
-        rows, width = grad.shape
-        views.append(grad.reshape(4, 2, 2, 2, 2, rows // 64, width))
-    scratch = []
-    for v in views:
-        scratch += Scatter.scratch(v.shape[5], v.shape[6], v.dtype)
-
-    def kernel(*refs):
-        p = Place()
-        greet(p)
-        bufs = refs[2 * n : 2 * n + 8 * n]
-        sems = refs[10 * n]
-        scatters = [Scatter(p, refs[i], refs[n + i], bufs[8 * i : 8 * i + 8], sems.at[i]) for i in range(n)]
-        for step in scatter_program(scatters):
-            step()
-
-    outs = pl.pallas_call(
-        kernel,
-        in_specs=[pl.BlockSpec(memory_space=pl.ANY)] * n,
-        out_specs=[pl.BlockSpec(memory_space=pltpu.VMEM)] * n,
-        out_shape=[jax.ShapeDtypeStruct((2, 2) + v.shape[5:], F32) for v in views],
-        scratch_shapes=scratch + [pltpu.SemaphoreType.DMA((n, RS_SEMS))],
-        compiler_params=pltpu.CompilerParams(
-            collective_id=collective_id, has_side_effects=True, vmem_limit_bytes=VMEM_LIMIT
-        ),
-        name="scatter",
-    )(*views)
-    return [out.reshape(grad.shape[0] // 16, grad.shape[1]) for out, grad in zip(outs, grads)]
 
 
 def lane_masks(rows, width, dtype=BF16):
@@ -516,57 +456,570 @@
 
 def gelu_pair(u):
     a = 0.7978845608028654
-    inner = jnp.tanh(a * (u + 0.044715 * u * u * u))
-    half = 0.5 * (1.0 + inner)
-    slope = half + 0.5 * u * (1.0 - inner * inner) * (a * (1.0 + 3.0 * 0.044715 * u * u))
-    return u * half, slope
-
-
-def up_project(normed, w_up, b_up):
-    rows, depth = normed.shape
-    width = w_up.shape[1]
+    square = u * u
+    half = 0.5 + 0.5 * jnp.tanh(u * (a + (a * 0.044715) * square))
+    value = u * half
+    slope = half + value * (1.0 - half) * (2.0 * a + (6.0 * a * 0.044715) * square)
+    return value, slope
+
+
+def whole_spec(ref, tile=None):
+    n, two, q, width = ref.shape
+    if tile is None:
+        return pl.BlockSpec((n, two, q, width), lambda j: (0, 0, 0, 0))
+    return pl.BlockSpec((n, two, q, tile), lambda j: (0, 0, 0, j))
+
+
+def rows_of(block):
+    value = block[...]
+    return value.reshape(-1, value.shape[-1])
+
+
+def forward_kernel(length, *refs):
+    (shards, refs) = (refs[:5], refs[5:])
+    x_ref, c_ref = refs[:2]
+    (wholes, refs) = (refs[2:7], refs[7:])
+    n1_ref, merged, logsum, attended, middle, n2_ref, act, slope, grad_down, small, refs = refs[:10] + (refs[10:],)
+    b_up, qkv_bias, vec, hidden, sems, vsem = refs
+    tokens, width = x_ref.shape
+    p = Place()
+    greet(p)
+    order = [4, 0, 1, 2, 3]
+    g_vec, g_qkv, g_out, g_up, g_down = [Gather(p, shards[i], wholes[i], sems.at[i]) for i in order]
+    head = z_steps(g_vec) + weave(z_steps(g_qkv), xy_steps(g_vec))
+    head += weave(z_steps(g_out), xy_steps(g_qkv), diag_steps(g_vec))
+    for step in head:
+        step()
+    g_vec.arrived()
+    load = pltpu.make_async_copy(wholes[4], vec, vsem)
+    load.start()
+    load.wait()
+    for k in range(8):
+        small[:, pl.ds(128 * k, 128)] = (vec[4 * k, 0, :8] + vec[4 * k + 2, 0, :8]).astype(F32)
+    for k in range(16):
+        for i in range(2):
+            b_up[:, pl.ds(256 * k + 128 * i, 128)] = vec[2 * k, 0, 8 + i : 9 + i].astype(F32)
+    qkv_bias[:, :width] = small[0:1]
+    qkv_bias[:, width : 2 * width] = jnp.zeros_like(small[0:1])
+    qkv_bias[:, 2 * width :] = small[1:2]
+
+    def norm_rows(i, carry):
+        rows = pl.ds(i * 128, 128)
+        n1_ref[rows, :] = layer_norm(x_ref[rows, :].astype(F32), small[4:5], small[5:6]).astype(BF16)
+        return carry
+
+    lax.fori_loop(0, tokens // 128, norm_rows, 0)
+    for step in weave(z_steps(g_up), diag_steps(g_qkv)):
+        step()
+    g_qkv.arrived()
+
+    rest = weave(xy_steps(g_out), z_steps(g_down)) + diag_steps(g_out) + xy_steps(g_up)
+    n_qkv, tile = 3 * width // 512, 512
+    table = spread(rest[:8], range(n_qkv))
+
+    def qkv_body(w_ref, o_ref):
+        j = pl.program_id(0)
+        hook(j, table)
+        bias = qkv_bias[:, pl.ds(pl.multiple_of(j * tile, tile), tile)]
+        o_ref[...] = (dot(n1_ref[...], rows_of(w_ref)) + bias).astype(BF16)
+
+    pltpu.emit_pipeline(
+        qkv_body,
+        grid=(n_qkv,),
+        in_specs=[whole_spec(wholes[0], tile)],
+        out_specs=[pl.BlockSpec((tokens, tile), lambda j: (0, j))],
+    )(wholes[0], merged)
+
+    pairs = width // 128
+    attend_table = spread(rest[8:], range(0, (tokens // length) * pairs, 2))
+
+    def attend_body(q, k, v, o, l):
+        s, h = pl.program_id(0), pl.program_id(1)
+        hook(s * pairs + h, attend_table)
+        fwd_body(q, k, v, o, l.at[0, 0], 256)
+
+    def head_spec(off):
+        return pl.BlockSpec((length, 128), lambda s, h: (s, off + h))
+
+    pltpu.emit_pipeline(
+        attend_body,
+        grid=(tokens // length, pairs),
+        in_specs=[head_spec(0), head_spec(pairs), head_spec(2 * pairs)],
+        out_specs=[head_spec(0), pl.BlockSpec((1, 1, 2, length), lambda s, h: (s, h, 0, 0))],
+    )(merged, merged, merged, attended, logsum)
+
+    g_out.arrived()
+    out_table = spread(diag_steps(g_up), range(tokens // 256))
+
+    def out_body(a_ref, w_ref, m_ref):
+        i = pl.program_id(0)
+        hook(i, out_table)
+        rows = pl.ds(pl.multiple_of(i * 256, 256), 256)
+        value = x_ref[rows, :].astype(F32) + (dot(a_ref[...], rows_of(w_ref)) + small[2:3])
+        m_ref[...] = value
+        n2_ref[rows, :] = layer_norm(value, small[6:7], small[7:8]).astype(BF16)
+
+    pltpu.emit_pipeline(
+        out_body,
+        grid=(tokens // 256,),
+        in_specs=[pl.BlockSpec((256, width), lambda i: (i, 0)), whole_spec(wholes[1])],
+        out_specs=[pl.BlockSpec((256, width), lambda i: (i, 0))],
+    )(attended, wholes[1], middle)
+
+    g_up.arrived()
+    n_up = act.shape[1] // tile
+    up_table = spread(xy_steps(g_down), range(1, n_up, 2))
+
+    def gelu_tile(j, a_ref, s_ref):
+        bias = b_up[:, pl.ds(pl.multiple_of(j * tile, tile), tile)]
+
+        value, grad = gelu_pair(hidden[j % 2] + bias)
+        a_ref[...] = value.astype(BF16)
+        s_ref[...] = grad.astype(BF16)
+
+    def up_body(w_ref, a_ref, s_ref):
+        j = pl.program_id(0)
+        hook(j, up_table)
+
+        @pl.when(j == 0)
+        def _():
+            hidden[0] = dot(n2_ref[...], rows_of(w_ref))
+
+        @pl.when(jnp.logical_and(j > 0, j < n_up))
+        def _():
+            gelu_tile(j - 1, a_ref, s_ref)
+            hidden[j % 2] = dot(n2_ref[...], rows_of(w_ref))
+
+        @pl.when(j == n_up)
+        def _():
+            gelu_tile(j - 1, a_ref, s_ref)
+
+    n, two, q, _ = wholes[2].shape
+    late = pl.BlockSpec((tokens, tile), lambda j: (0, jnp.maximum(j - 1, 0)))
+    pltpu.emit_pipeline(
+        up_body,
+        grid=(n_up + 1,),
+        in_specs=[pl.BlockSpec((n, two, q, tile), lambda j: (0, 0, 0, jnp.minimum(j, n_up - 1)))],
+        out_specs=[late, late],
+    )(wholes[2], act, slope)
+
+    down_table = spread(diag_steps(g_down), range(1, n_up, 2))
+
+    def grad_body(a_ref, o_ref):
+        hook(pl.program_id(0), down_table)
+        o_ref[...] = dot(a_ref[...], c_ref[...], TN).astype(BF16)
+
+    pltpu.emit_pipeline(
+        grad_body,
+        grid=(n_up,),
+        in_specs=[pl.BlockSpec((tokens, tile), lambda j: (0, j))],
+        out_specs=[pl.BlockSpec((tile, width), lambda j: (j, 0))],
+    )(act, grad_down)
+    g_down.arrived()
+    for g in (g_vec, g_qkv, g_out, g_up, g_down):
+        g.drain()
+
+
+def forward_call(shards, x, c, length):
+    tokens, width = x.shape
+    hidden = 16 * shards[3].shape[0]
+    views = [s.reshape(2, 2, s.shape[0] // 4, s.shape[1]) for s in shards]
+    whole = [jax.ShapeDtypeStruct((32,) + v.shape[1:], v.dtype) for v in views]
+    vmem, any_space = pl.BlockSpec(memory_space=pltpu.VMEM), pl.BlockSpec(memory_space=pl.ANY)
+    low = lambda *shape: jax.ShapeDtypeStruct(shape, BF16)
+    outs = pl.pallas_call(
+        lambda *refs: forward_kernel(length, *refs),
+        in_specs=[vmem] * 7,
+        out_specs=[any_space] * 5 + [vmem] + [any_space] * 4 + [vmem] + [any_space] * 3 + [vmem],
+        out_shape=whole
+        + [
+            low(tokens, width),
+            low(tokens, 3 * width),
+            jax.ShapeDtypeStruct((tokens // length, width // 128, 2, length), F32),
+            low(tokens, width),
+            jax.ShapeDtypeStruct((tokens, width), F32),
+            low(tokens, width),
+            low(tokens, hidden),
+            low(tokens, hidden),
+            low(hidden, width),
+            jax.ShapeDtypeStruct((8, width), F32),
+        ],
+        scratch_shapes=[
+            pltpu.VMEM((1, hidden), F32),
+            pltpu.VMEM((1, 3 * width), F32),
+            pltpu.VMEM(whole[4].shape, BF16),
+            pltpu.VMEM((2, tokens, 512), F32),
+            pltpu.SemaphoreType.DMA((5, AG_SEMS)),
+            pltpu.SemaphoreType.DMA,
+        ],
+        compiler_params=pltpu.CompilerParams(collective_id=0, has_side_effects=True, vmem_limit_bytes=VMEM_LIMIT),
+        name="forward",
+    )(*views, x, c)
+    return outs[:4], outs[5:]
+
+
+PLAN = (
+    (4, 0, 0, 0), (5, 1, 0, 0), (5, 0, 0, 1), (6, 1, 0, 1), (7, 0, 0, 2), (8, 1, 0, 2), (8, 2, 0, 0), (8, 0, 0, 3),
+    (9, 1, 0, 3), (11, 2, 0, 1), (14, 2, 0, 2), (16, 3, 0, 0), (17, 0, 1, 0), (18, 1, 1, 0), (18, 0, 1, 1), (19, 2, 0, 3),
+    (19, 1, 1, 1), (19, 0, 1, 2), (20, 4, 0, 0), (20, 3, 0, 1), (20, 1, 1, 2), (20, 0, 1, 3), (21, 3, 0, 2), (21, 4, 0, 2),
+    (21, 1, 1, 3), (22, 2, 1, 0), (24, 4, 0, 1), (24, 3, 0, 3), (24, 4, 0, 3), (27, 2, 1, 1), (28, 0, 2, 0), (30, 2, 1, 2),
+    (30, 1, 2, 0), (30, 0, 2, 1), (32, 5, 0, 0), (32, 2, 1, 3), (32, 1, 2, 1), (32, 0, 2, 2), (33, 3, 1, 0), (33, 3, 1, 1),
+    (33, 1, 2, 2), (33, 0, 2, 3), (34, 3, 1, 2), (34, 4, 1, 2), (34, 1, 2, 3), (35, 4, 1, 0), (35, 2, 2, 0), (36, 3, 1, 3),
+    (37, 4, 1, 1), (37, 2, 2, 1), (37, 4, 1, 3), (37, 0, 3, 0), (38, 2, 2, 2), (38, 1, 3, 0), (38, 0, 3, 1), (38, 0, 3, 2),
+    (39, 5, 1, 0), (39, 2, 2, 3), (39, 1, 3, 1), (39, 1, 3, 2), (39, 3, 2, 0), (39, 0, 3, 3), (40, 3, 2, 1), (40, 1, 3, 3),
+    (40, 3, 2, 2), (40, 4, 2, 2), (41, 4, 2, 0), (41, 2, 3, 0), (42, 4, 2, 1), (42, 3, 2, 3), (42, 2, 3, 1), (43, 4, 2, 3),
+    (43, 2, 3, 2), (43, 2, 3, 3), (43, 3, 3, 0), (44, 3, 3, 1), (44, 3, 3, 2), (44, 4, 3, 2), (44, 3, 3, 3), (45, 5, 2, 0),
+    (45, 4, 3, 0), (45, 4, 3, 1), (47, 4, 3, 3), (49, 5, 3, 0), (57, 0, 4, 0), (57, 0, 4, 1), (58, 1, 4, 0), (58, 1, 4, 1),
+    (58, 0, 4, 2), (58, 0, 4, 3), (59, 1, 4, 2), (59, 1, 4, 3), (59, 2, 4, 0), (59, 0, 5, 0), (59, 0, 5, 1), (60, 2, 4, 1),
+    (60, 1, 5, 0), (60, 1, 5, 1), (60, 2, 4, 2), (60, 0, 5, 2), (60, 0, 5, 3), (60, 0, 6, 0), (60, 0, 6, 1), (61, 3, 4, 0),
+    (61, 2, 4, 3), (61, 1, 5, 2), (61, 3, 4, 1), (61, 1, 5, 3), (61, 1, 6, 0), (61, 1, 6, 1), (61, 2, 5, 0), (61, 0, 6, 2),
+    (61, 0, 6, 3), (62, 4, 4, 0), (62, 3, 4, 2), (62, 4, 4, 1), (62, 4, 4, 2), (62, 3, 4, 3), (62, 2, 5, 1), (62, 1, 6, 2),
+    (62, 1, 6, 3), (63, 4, 4, 3), (63, 2, 5, 2), (63, 2, 5, 3), (64, 2, 6, 0), (65, 5, 4, 0), (65, 3, 5, 0), (65, 2, 6, 1),
+    (66, 3, 5, 1), (67, 2, 6, 2), (68, 4, 5, 0), (68, 2, 6, 3), (69, 4, 5, 1), (69, 3, 5, 2), (69, 4, 5, 2), (69, 3, 5, 3),
+    (70, 3, 6, 0), (71, 4, 5, 3), (71, 3, 6, 1), (71, 3, 6, 2), (71, 4, 6, 2), (72, 3, 6, 3), (73, 5, 5, 0), (73, 4, 6, 0),
+    (73, 0, 7, 0), (73, 4, 6, 1), (73, 0, 7, 1), (74, 1, 7, 0), (74, 1, 7, 1), (74, 0, 7, 2), (74, 0, 7, 3), (75, 4, 6, 3),
+    (75, 2, 7, 0), (75, 2, 7, 1), (75, 1, 7, 2), (75, 1, 7, 3), (76, 3, 7, 0), (76, 3, 7, 1), (76, 2, 7, 2), (76, 2, 7, 3),
+    (76, 5, 6, 0), (77, 4, 7, 0), (77, 4, 7, 1), (77, 3, 7, 2), (77, 4, 7, 2), (77, 3, 7, 3), (78, 4, 7, 3), (79, 5, 7, 0),
+)
+
+PRE, S0, S1, S2, S3, S4 = range(6)
+STAGES = ("fetch", "stage0", "stage1", "stage2", "stage3", "stage4")
+
+
+def column_sum(ref, at, value):
+    ref[at] = ref[at] + jnp.sum(value, 0, keepdims=True)
+
+
+def backward_kernel(length, plan, n_up_parts, *refs):
+    (w_qkv, w_out, w_up, w_down), refs = refs[:4], refs[4:]
+    x, c, n1, merged, logsum, attended, middle, n2, act, slope, g_down, small, refs = refs[:12] + (refs[12:],)
+    output, input_grad, f_qkv, f_out, f_up, f_down, f_vec, g_qkv, g_out, g_up, mid_grad, ag, back, refs = refs[:13] + (
+        refs[13:],
+    )
+    landing, refs = refs[:8], refs[8:]
+    sets, refs = refs[: 8 * 7], refs[8 * 7 :]
+    tmps, refs = refs[:8], refs[8:]
+    (g_vec, narrow, wide, left, right, acc, branch, dk_acc, dv_acc, sems, csem) = refs
+    tokens, width = x.shape
+    hidden = act.shape[1]
     tile = 512
-
-    def body(n_ref, w_ref, b_ref, a_ref, s_ref):
-        value, slope = gelu_pair(dot(n_ref[...], w_ref[...]) + b_ref[...])
-        a_ref[...] = value.astype(BF16)
-        s_ref[...] = slope.astype(BF16)
-
-    out = pl.BlockSpec((rows // 2, tile), lambda j, i: (i, j))
-    return pl.pallas_call(
-        body,
-        grid=(width // tile, 2),
+    pairs = width // 128
+    p = Place()
+    greet(p)
+    sets = [sets[7 * i : 7 * i + 7] for i in range(8)]
+    half = hidden // n_up_parts
+    entries = [
+        (g_down, f_down),
+        (g_up.at[0], f_up.at[:, :, :, pl.ds(0, half)]),
+        (g_up.at[1], f_up.at[:, :, :, pl.ds(half, half)]),
+        (g_out, f_out),
+        (g_qkv.at[0], f_qkv.at[:, :, :, pl.ds(0, width)]),
+        (g_qkv.at[1], f_qkv.at[:, :, :, pl.ds(width, width)]),
+        (g_qkv.at[2], f_qkv.at[:, :, :, pl.ds(2 * width, width)]),
+        (g_vec, f_vec),
+    ]
+    rs = [Scatter(p, g, f, landing[k], sets[k], tmps[k], sems.at[k]) for k, (g, f) in enumerate(entries)]
+
+    def turn(slot, first, count):
+        table = {}
+        for at, stage, k, i in plan:
+            if first <= at < first + count:
+                table.setdefault(at, []).append(lambda stage=stage, k=k, i=i: getattr(rs[k], STAGES[stage])(i))
+        hook(slot, table)
+
+    loads = [
+        pltpu.make_async_copy(c, left, csem.at[0]),
+        pltpu.make_async_copy(n2, right, csem.at[1]),
+    ]
+    for load in loads:
+        load.start()
+    rs[0].start()
+    narrow[...] = jnp.zeros_like(narrow)
+    wide[...] = jnp.zeros_like(wide)
+    g_vec[...] = jnp.zeros_like(g_vec)
+    acc[...] = jnp.zeros_like(acc)
+    for load in loads:
+        load.wait()
+
+    n_up = hidden // tile
+
+    def ffn_body(wd, s, wu, g):
+        j = pl.program_id(0)
+
+        @pl.when(j == n_up // 2 + 1)
+        def _():
+            rs[1].start()
+
+        turn(3 * j, 0, 3 * n_up)
+        grad = (dot(left[...], rows_of(wd), NT) * s[...].astype(F32)).astype(BF16)
+        at = pl.ds(pl.multiple_of(j * tile, tile), tile)
+        wide[:, at] = jnp.sum(grad.astype(F32), 0, keepdims=True)
+        turn(3 * j + 1, 0, 3 * n_up)
+        g[0] = dot(right[...], grad, TN).astype(BF16).reshape(g.shape[1:])
+        turn(3 * j + 2, 0, 3 * n_up)
+        acc[...] += dot(grad, rows_of(wu), NT)
+
+    per = n_up // n_up_parts
+    q_down = w_down.shape[2]
+    blocks = tile // (2 * q_down)
+    shape = g_up.shape[1:7]
+    pltpu.emit_pipeline(
+        ffn_body,
+        grid=(n_up,),
         in_specs=[
-            pl.BlockSpec((rows // 2, depth), lambda j, i: (i, 0)),
-            pl.BlockSpec((depth, tile), lambda j, i: (0, j)),
-            pl.BlockSpec((1, tile), lambda j, i: (0, j)),
+            pl.BlockSpec((blocks, 2, q_down, width), lambda j: (j, 0, 0, 0)),
+            pl.BlockSpec((tokens, tile), lambda j: (0, j)),
+            whole_spec(w_up, tile),
         ],
-        out_specs=[out, out],
-        out_shape=[jax.ShapeDtypeStruct((rows, width), BF16)] * 2,
-        compiler_params=pltpu.CompilerParams(vmem_limit_bytes=VMEM_LIMIT),
-        name="up_project",
-    )(normed, w_up, b_up)
-
-
-def compute(rows, upstream, weights, small):
+        out_specs=[pl.BlockSpec((1,) + shape + (tile,), lambda j: (j // per, 0, 0, 0, 0, 0, 0, j % per))],
+    )(w_down, slope, w_up, g_up)
+    rs[2].start()
+    load = pltpu.make_async_copy(n1, right, csem.at[1])
+    load.start()
+    base = 3 * n_up
+
+    step = 128
+    n_rows = tokens // step
+
+    def norm_two_body(m, o):
+        i = pl.program_id(0)
+        turn(base + i, base, n_rows)
+        rows = pl.ds(pl.multiple_of(i * step, step), step)
+        upstream = left[rows, :].astype(F32)
+        part, gain, shift = norm_back(m[...], small[6:7], acc[rows, :])
+        total = upstream + part
+        o[...] = total
+        low = total.astype(BF16)
+        branch[rows, :] = low
+        narrow[2:3] += jnp.sum(low.astype(F32), 0, keepdims=True)
+        narrow[3:4] += jnp.sum(upstream, 0, keepdims=True)
+        narrow[6:7] += gain[None]
+        narrow[7:8] += shift[None]
+
+    row_spec = pl.BlockSpec((step, width), lambda i: (i, 0))
+    pltpu.emit_pipeline(norm_two_body, grid=(n_rows,), in_specs=[row_spec], out_specs=[row_spec])(middle, mid_grad)
+    base += n_rows
+
+    n_out = width // 256
+    first_out = base
+
+    def out_body(a, w, g, o):
+        i = pl.program_id(0)
+        turn(first_out + i, first_out, n_out)
+        g[...] = dot(a[...], branch[...], TN).astype(BF16).reshape(g.shape)
+        rows = pl.ds(pl.multiple_of(i * 256, 256), 256)
+        o[...] = dot(branch[rows, :], rows_of(w), NT).astype(BF16)
+
+    q = g_out.shape[5]
+    levels = 256 // (16 * q)
+    assert levels == 1
+    pltpu.emit_pipeline(
+        out_body,
+        grid=(n_out,),
+        in_specs=[pl.BlockSpec((tokens, 256), lambda i: (0, i)), whole_spec(w_out)],
+        out_specs=[
+            pl.BlockSpec((1, 2, 2, 2, 2, q, width), lambda i: (i, 0, 0, 0, 0, 0, 0)),
+            pl.BlockSpec((256, width), lambda i: (i, 0)),
+        ],
+    )(attended, w_out, g_out, ag)
+    rs[3].start()
+    base += n_out
+
+    first_attend = base
+    n_attend = (tokens // length) * pairs
+
+    def attend_body(q, k, v, g, l, d):
+        s, h = pl.program_id(0), pl.program_id(1)
+        turn(first_attend + s * pairs + h, first_attend, n_attend)
+        bwd_body(q, k, v, g, l.at[0, 0], d.at[0], d.at[1], d.at[2], dk_acc, dv_acc, 256)
+        at = pl.ds(pl.multiple_of(h * 128, 128), 128)
+        narrow[0:1, at] += jnp.sum(d[0].astype(F32), 0, keepdims=True)
+        narrow[1:2, at] += jnp.sum(d[2].astype(F32), 0, keepdims=True)
+
+    def head_spec(off):
+        return pl.BlockSpec((length, 128), lambda s, h: (s, off + h))
+
+    pltpu.emit_pipeline(
+        attend_body,
+        grid=(tokens // length, pairs),
+        in_specs=[head_spec(0), head_spec(pairs), head_spec(2 * pairs), head_spec(0)]
+        + [pl.BlockSpec((1, 1, 2, length), lambda s, h: (s, h, 0, 0))],
+        out_specs=[pl.BlockSpec((3, length, 128), lambda s, h: (0, s, h))],
+    )(merged, merged, merged, ag, logsum, back)
+    base += n_attend
+    load.wait()
+
+    first_qkv = base
+    n_qkv = 3 * width // tile
+    per_part = width // tile
+
+    def grad_body(d, g):
+        j = pl.program_id(0)
+        for k in (1, 2):
+
+            @pl.when(j == k * per_part + 1)
+            def _(k=k):
+                rs[3 + k].start()
+
+        turn(first_qkv + j, first_qkv, n_qkv)
+        g[0] = dot(right[...], d[0], TN).astype(BF16).reshape(g.shape[1:])
+
+    shape = g_qkv.shape[1:7]
+    back_spec = pl.BlockSpec((1, tokens, tile), lambda j: (j // per_part, 0, j % per_part))
+    pltpu.emit_pipeline(
+        grad_body,
+        grid=(n_qkv,),
+        in_specs=[back_spec],
+        out_specs=[
+            pl.BlockSpec((1,) + shape + (tile,), lambda j: (j // per_part, 0, 0, 0, 0, 0, 0, j % per_part))
+        ],
+    )(back, g_qkv)
+    rs[6].start()
+    base += n_qkv
+    first_in = base
+    acc[...] = jnp.zeros_like(acc)
+
+    def in_body(d, w):
+        j = pl.program_id(0)
+        turn(first_in + j, first_in, n_qkv)
+        acc[...] += dot(d[0], rows_of(w), NT)
+
+    pltpu.emit_pipeline(in_body, grid=(n_qkv,), in_specs=[back_spec, whole_spec(w_qkv, tile)])(back, w_qkv)
+    base += n_qkv
+
+    first_one = base
+
+    def norm_one_body(v, m, o):
+        i = pl.program_id(0)
+        turn(first_one + i, first_one, n_rows)
+        rows = pl.ds(pl.multiple_of(i * step, step), step)
+        part, gain, shift = norm_back(v[...].astype(F32), small[4:5], acc[rows, :])
+        o[...] = m[...] + part
+        narrow[4:5] += gain[None]
+        narrow[5:6] += shift[None]
+
+    pltpu.emit_pipeline(norm_one_body, grid=(n_rows,), in_specs=[row_spec] * 2, out_specs=[row_spec])(
+        x, mid_grad, input_grad
+    )
+    base += n_rows
+    for k in range(16):
+        z, y, xx = k // 4, (k // 2) % 2, k % 2
+        g_vec[z, y, xx, 0, 0] = narrow[:, 128 * (k // 2) : 128 * (k // 2) + 128]
+        for i in range(2):
+            g_vec[z, y, xx, 0, 1, i : i + 1] = wide[:, 256 * k + 128 * i : 256 * k + 128 * i + 128]
+    rs[7].start()
+    acc[...] = jnp.zeros_like(acc)
+
+    first_down = base
+
+    def down_body(a, w):
+        j = pl.program_id(0)
+        turn(first_down + j, first_down, n_up)
+        acc[...] += dot(a[...], rows_of(w))
+
+    pltpu.emit_pipeline(
+        down_body,
+        grid=(n_up,),
+        in_specs=[
+            pl.BlockSpec((tokens, tile), lambda j: (0, j)),
+            pl.BlockSpec((blocks, 2, q_down, width), lambda j: (j, 0, 0, 0)),
+        ],
+    )(act, w_down)
+    base += n_up
+    first_last = base
+
+    def last_body(m, o):
+        i = pl.program_id(0)
+        turn(first_last + i, first_last, n_rows)
+        rows = pl.ds(pl.multiple_of(i * step, step), step)
+        o[...] = (m[...] + (acc[rows, :] + small[3:4])).astype(BF16)
+
+    pltpu.emit_pipeline(last_body, grid=(n_rows,), in_specs=[row_spec], out_specs=[row_spec])(middle, output)
+    base += n_rows
+    for at, stage, k, i in plan:
+        if at >= base:
+            getattr(rs[k], STAGES[stage])(i)
+    for r in rs:
+        r.finish()
+
+
+def backward_call(weights, x, c, kept, length):
+    n1, merged, logsum, attended, middle, n2, act, slope, g_down, small = kept
+    tokens, width = x.shape
+    hidden = act.shape[1]
+    q, q_down = width // 64, hidden // 64
+    parts = 2
+    low = lambda *shape: jax.ShapeDtypeStruct(shape, BF16)
+    full = lambda *shape: jax.ShapeDtypeStruct(shape, F32)
+    vmem, any_space = pl.BlockSpec(memory_space=pltpu.VMEM), pl.BlockSpec(memory_space=pl.ANY)
+    kinds = [(q_down, width, BF16)] + [(q, hidden // parts, BF16)] * 2 + [(q, width, BF16)] * 4 + [(8, 128, F32)]
+    scratch = []
+    for kind in kinds:
+        scratch += Scatter.scratch(*kind)
+    scratch += [pltpu.VMEM((2, 2, 2, 2) + kind[:2], kind[2]) for kind in kinds]
+    scratch += [
+        pltpu.VMEM((4, 2, 2, 2, 2, 8, 128), F32),
+        pltpu.VMEM((8, width), F32),
+        pltpu.VMEM((1, hidden), F32),
+        pltpu.VMEM((tokens, width), BF16),
+        pltpu.VMEM((tokens, width), BF16),
+        pltpu.VMEM((tokens, width), F32),
+        pltpu.VMEM((tokens, width), BF16),
+        pltpu.VMEM((length, 128), F32),
+        pltpu.VMEM((length, 128), F32),
+        pltpu.SemaphoreType.DMA((8, RS_SEMS)),
+        pltpu.SemaphoreType.DMA((2,)),
+    ]
+    shards = [full(2, 2, q, 3 * width), full(2, 2, q, width), full(2, 2, q, hidden), full(2, 2, q_down, width)]
+    outs = pl.pallas_call(
+        lambda *refs: backward_kernel(length, PLAN, parts, *refs),
+        in_specs=[any_space] * 15 + [vmem],
+        out_specs=[any_space] * 2 + [vmem] * 5 + [any_space] * 14,
+        out_shape=[low(tokens, width), full(tokens, width)]
+        + shards
+        + [full(2, 2, 8, 128)]
+        + [
+            low(3, 4, 2, 2, 2, 2, q, width),
+            low(4, 2, 2, 2, 2, q, width),
+            low(parts, 4, 2, 2, 2, 2, q, hidden // parts),
+            full(tokens, width),
+            low(tokens, width),
+            low(3, tokens, width),
+        ]
+        + [jax.ShapeDtypeStruct((4, 2, 2, 2) + kind[:2], kind[2]) for kind in kinds],
+        scratch_shapes=scratch,
+        compiler_params=pltpu.CompilerParams(
+            collective_id=1, has_side_effects=True, vmem_limit_bytes=66 * 10**6
+        ),
+        name="backward",
+    )(*weights, x, c, n1, merged, logsum, attended, middle, n2, act, slope, g_down.reshape(4, 2, 2, 2, 2, q_down, width), small)
+    grads = [o.reshape(-1, o.shape[-1]) for o in outs[2:6]]
+    return outs[0], outs[1], grads, outs[6].reshape(32, 128)
+
+
+def forward_plain(x, weights, small, length):
     w_qkv, w_out, w_up, w_down = weights
     b_query, b_value, b_out, b_up, b_down, gain_one, shift_one, gain_two, shift_two = small
-    length, width = rows.shape[1], rows.shape[2]
-    tokens = rows.shape[0] * length
-    x = rows.reshape(tokens, width)
-    c = upstream.reshape(tokens, width)
-    xf, cf = x.astype(F32), c.astype(F32)
+    xf = x.astype(F32)
     normed_one = layer_norm(xf, gain_one, shift_one).astype(BF16)
     qkv_bias = jnp.concatenate([b_query, jnp.zeros_like(b_query), b_value])
     merged = (dot(normed_one, w_qkv) + qkv_bias).astype(BF16)
     attended, logsum = attn_fwd(merged, length)
     middle = xf + (dot(attended, w_out) + b_out)
     normed_two = layer_norm(middle, gain_two, shift_two).astype(BF16)
-    activated, slope = up_project(normed_two, w_up, b_up[None])
+    activated, slope = gelu_pair(dot(normed_two, w_up) + b_up)
+    return normed_one, merged, logsum, attended, middle, normed_two, activated.astype(BF16), slope.astype(BF16)
+
+
+def backward(x, c, weights, small, kept, length):
+    w_qkv, w_out, w_up, w_down = weights
+    b_down, gain_one, gain_two = small
+    normed_one, merged, logsum, attended, middle, normed_two, activated, slope = kept
+    width = x.shape[1]
+    xf, cf = x.astype(F32), c.astype(F32)
     output = (middle + (dot(activated, w_down) + b_down)).astype(BF16)
 
     grad_down_bias = jnp.sum(cf, 0)
-    grad_down = dot(activated, c, TN).astype(BF16)
     hidden_grad = (dot(c, w_down, NT) * slope.astype(F32)).astype(BF16)
     grad_up_bias = jnp.sum(hidden_grad.astype(F32), 0)
     grad_up = dot(normed_two, hidden_grad, TN).astype(BF16)
@@ -584,9 +1037,9 @@
     part, grad_gain_one, grad_shift_one = norm_back(xf, gain_one, normed_one_grad)
     input_grad = middle_grad + part
     return (
-        output.reshape(rows.shape),
-        input_grad.reshape(rows.shape),
-        (grad_qkv, grad_out, grad_up, grad_down),
+        output,
+        input_grad,
+        (grad_qkv, grad_out, grad_up),
         (
             grad_query_bias,
             grad_value_bias,
@@ -611,22 +1064,6 @@
     return jnp.pad(rows, ((0, 64 - rows.shape[0]), (0, 0)))
 
 
-def unpack_whole(packed):
-    blocks = packed.reshape(8, 2, 64, 128)
-    narrow = (blocks[:, 0, :8] + blocks[:, 1, :8]).astype(F32)
-    narrow = jnp.moveaxis(narrow, 0, 1).reshape(8, 1024)
-    wide = blocks[:, :, 8:10].astype(F32).reshape(4096)
-    return tuple(narrow[j] for j in range(3)) + (wide,) + tuple(narrow[j] for j in range(3, 8))
-
-
-def pack_grads(vectors):
-    narrow = jnp.stack([v for k, v in enumerate(vectors) if k != 3]).reshape(8, 8, 128)
-    narrow = jnp.repeat(jnp.moveaxis(narrow, 1, 0), 2, axis=0)
-    wide = vectors[3].reshape(16, 2, 128)
-    rows = jnp.concatenate([narrow, wide], 1)
-    return jnp.pad(rows, ((0, 0), (0, 22), (0, 0))).reshape(16 * 32, 128)
-
-
 def unpack_shard(packed):
     odd = lax.axis_index("fsdp") % 2 == 1
     narrow = jnp.where(odd, packed[:8, 64:], packed[:8, :64])
@@ -636,26 +1073,30 @@
 
 def local_ring(block_input, *rest):
     shards, cotangent = rest[:13], rest[13]
-    w_qkv, w_out, w_up, w_down, packed = gather_all(shards[:4] + (pack_shards(shards[4:]),), 0)
-    small = unpack_whole(packed)
-    output, input_grad, mats, vecs = compute(block_input, cotangent, (w_qkv, w_out, w_up, w_down), small)
-    grad_down, grad_up, grad_out, grad_qkv, vec = scatter_all(
-        [mats[3], mats[2], mats[1], mats[0], pack_grads(vecs)], 1
-    )
-    return (output, input_grad, grad_qkv, grad_out, grad_up, grad_down) + unpack_shard(vec)
+    length, width = block_input.shape[1:]
+    x, c = block_input.reshape(-1, width), cotangent.reshape(-1, width)
+    weights, kept = forward_call(shards[:4] + (pack_shards(shards[4:]),), x, c, length)
+    output, input_grad, grads, vec = backward_call(weights, x, c, kept, length)
+    whole = (output.reshape(block_input.shape), input_grad.reshape(block_input.shape))
+    return whole + tuple(grads) + unpack_shard(vec)
 
 
 def local_any(block_input, *rest):
     shards, cotangent = rest[:13], rest[13]
-    whole = [lax.all_gather(shard, "fsdp", axis=0, tiled=True) for shard in shards]
-    small = tuple(v.astype(F32) for v in whole[4:])
-    output, input_grad, mats, vecs = compute(block_input, cotangent, whole[:4], small)
+    length, width = block_input.shape[1:]
+    x, c = block_input.reshape(-1, width), cotangent.reshape(-1, width)
+    gathered = [lax.all_gather(shard, "fsdp", axis=0, tiled=True) for shard in shards]
+    weights, small = gathered[:4], tuple(v.astype(F32) for v in gathered[4:])
+    kept = forward_plain(x, weights, small, length)
+    output, input_grad, mats, vecs = backward(x, c, weights, (small[4], small[5], small[7]), kept, length)
+    mats += (dot(kept[6], c, TN),)
 
     def reduce(grad):
         part = lax.psum_scatter(grad.astype(F32), "fsdp", scatter_dimension=0, tiled=True)
         return lax.psum(part, "seq")
 
-    return (output, input_grad) + tuple(reduce(grad) for grad in mats + vecs)
+    whole = (output.reshape(block_input.shape), input_grad.reshape(block_input.shape))
+    return whole + tuple(reduce(grad) for grad in mats + vecs)
 
 
 def solution(mesh):

time: 516 us -> 361 us (0.70)
  matrix products: 120 us -> 0 us
  other arithmetic: 35.2 us -> 2.16 us
  Pallas kernels: 339 us -> 345 us
  local copies, waits for them, and re-layouts: 17 us -> 11.5 us
    dot_general x15 -> x0, matrix products: 120 us -> none  [dot(): return lax.dot_general(left, right, dims, preferred_element_type=F32)]
    concatenate x3 -> x0, other arithmetic: 14.2 us -> none  [the longest x1 13.4 us: compute(): jnp.concatenate([dot(normed_one, back[j], TN).astype(BF16) for j in range...]
    concatenate x1 -> x0, local copies, waits for them, and re-layouts: 8.63 us -> none  [compute(): jnp.concatenate([dot(normed_one, back[j], TN).astype(BF16) for j in range...]
    reduce_sum x6 -> x0, other arithmetic: 7.88 us -> none  [the longest x1 3.38 us: compute(): grad_out_bias = jnp.sum(branch_grad.astype(F32), 0)]
    pallas_call x5 -> x2, Pallas kernels: 339 us -> 345 us  [the longest x1 182 us: backward_call(): pl.pallas_call(lambda *refs: backward_kernel(length, PLAN, parts, *refs),...]
    add x1 -> x0, other arithmetic: 5.91 us -> none  [compute(): input_grad = middle_grad + part]
where the time goes in v2:
time: 361 us; the launch traced here: 360 us
  Pallas kernels  345 us (96%)
  local copies, waits for them, and re-layouts  11.5 us (3%)
    pallas_call x1, Pallas kernels, backward_call(): pl.pallas_call(lambda *refs: backward_kernel(length, PLAN, parts, *refs),...  182 us
    pallas_call x1, Pallas kernels, forward_call(): pl.pallas_call(lambda *refs: forward_kernel(length, *refs), in_specs=[vme...  163 us
    unnamed x16, local copies, waits for them, and re-layouts  8.76 us

profile of v2, /device:TPU:0, one launch (start us, length us, event | category | flops | bytes accessed | tf_op | source)
XLA Modules:
  0.0 359.7 jit_solution(3434298685268335740)
XLA Ops:
  0.7 0.8 stack.35
  1.5 1.3 fusion.4
  2.8 163.2 %forward.1 = (bf16[32,2,16,3072]{3,2,1,0:T(8,128)(2,1)}, bf16[32,2,16,1024]{3,2,1,0:T(8,128)(2,1)}, bf16[32,2,16,4096]{3,2,1,0:T(8,128)(2,1)}, bf16[32,2,64,1024...) custom-call(bf16[2,2,16,3072]{3,2,1,0:T(8,128)(2,1)} %bitcast.54, ...), custom_call_target="tpu_custom_call" | custom-call | tf_op jit(solution)/shard_map/forward/pallas_call | solution.py:630
  166.0 182.2 %backward.1 = (bf16[1024,1024]{1,0:T(8,128)(2,1)}, f32[1024,1024]{1,0:T(8,128)}, f32[2,2,16,3072]{3,2,1,0:T(8,128)}, f32[2,2,16,1024]{3,2,1,0:T(8,128)}, f32[2,2...) custom-call(bf16[32,2,16,3072]{3,2,1,0:T(8,128)(2,1)} %get-tuple-ele, ...), custom_call_target="tpu_custom_call" | custom-call | tf_op jit(solution)/shard_map/backward/pallas_call | solution.py:974
  348.2 0.0 copy-start
  348.2 1.4 slice_bitcast_fusion
  349.6 0.8 slice_select_fusion
  350.4 0.5 slice_bitcast_fusion.1
  350.9 3.1 copy.36
  354.0 0.0 copy-done
  354.0 0.0 copy-start.3
  354.0 0.0 copy-start.4
  354.0 0.0 copy-start.2
  354.0 2.1 copy.37
  356.2 0.0 copy-done.3
  356.2 0.0 copy-start.1
  356.2 0.9 copy.38
  357.1 0.0 copy-done.4
  357.1 0.7 copy.39
  357.8 0.0 copy-done.2
  357.8 1.0 copy.40
  358.7 0.0 copy-done.1
  358.7 1.0 copy.41
  (1 shorter events, 0.0 us)
Async XLA Ops:
  348.2 5.8 %copy-start = (f32[1024,1024]{1,0:T(8,128)S(1)}, f32[1024,1024]{1,0:T(8,128)}, u32[]{:S(2)}) copy-start(f32[1024,1024]{1,0:T(8,128)} %get-tuple-element.51) | copy-start | bytes 12582916
  354.0 2.1 copy-start.3
  354.0 3.0 copy-start.4
  354.0 3.7 %copy-start.2 = (f32[2,2,16,4096]{3,2,1,0:T(8,128)S(1)}, f32[2,2,16,4096]{3,2,1,0:T(8,128)}, u32[]{:S(2)}) copy-start(f32[2,2,16,4096]{3,2,1,0:T(8,128)} %get-tuple-element.54) | copy-start | bytes 3145732
  356.2 2.6 copy-start.1

commit v3 on v2

--- a/solution.py
+++ b/solution.py
@@ -125,7 +125,6 @@
         own = self.src.at[p.c]
         self.along(own, p.z, True)
         self.along(own, p.z, False)
-        self.spread(own, p.z)
         me = p.block(p.z, p.y, p.x)
         pltpu.make_async_copy(self.src, self.dst.at[pl.ds(2 * me, 2)], self.local).start()
 
@@ -145,13 +144,23 @@
 
     def z_step(self, s):
         p = self.p
+        if s == 0:
+            self.start()
+            return
 
         def body(z, up):
             mine = self.half(z, p.y, p.x)
             wait_bytes(mine, self.sems.at[z])
             self.along(mine, z, up)
-            self.spread(mine, z)
             self.to(mine, mine, 23, p.partner)
+
+        self.at_distance(s, body)
+
+    def spread_step(self, s):
+        p = self.p
+
+        def body(z, up):
+            self.spread(self.src.at[p.c] if s == 0 else self.half(z, p.y, p.x), z)
 
         self.at_distance(s, body)
 
@@ -199,20 +208,7 @@
             wait_bytes(self.dst.at[pl.ds(0, 1)], self.zsend)
 
 
-def z_steps(g):
-    return [g.start] + [lambda s=s: g.z_step(s) for s in (1, 2, 3)]
-
-
-def xy_steps(g):
-    return [lambda s=s: g.xy_step(s) for s in range(4)]
-
-
-def diag_steps(g):
-    return [lambda s=s: g.diag_step(s) for s in range(4)]
-
-
-def weave(*lists):
-    return [item[k] for k in range(max(map(len, lists))) for item in lists if k < len(item)]
+GATHER_STAGES = ("z_step", "spread_step", "xy_step", "diag_step")
 
 
 def hook(index, table):
@@ -222,13 +218,6 @@
         def _(steps=steps):
             for step in steps:
                 step()
-
-
-def spread(steps, slots):
-    table = {}
-    for k, step in enumerate(steps):
-        table.setdefault(slots[min(k * len(slots) // len(steps), len(slots) - 1)], []).append(step)
-    return table
 
 
 RS_SEMS = 44
@@ -475,25 +464,57 @@
     return value.reshape(-1, value.shape[-1])
 
 
-def forward_kernel(length, *refs):
+GATHER_PLAN = (
+    (0, 0, 0, 0), (0, 0, 1, 0), (0, 1, 0, 0), (0, 1, 1, 0), (0, 0, 0, 1), (0, 0, 2, 0), (0, 2, 0, 0), (0, 1, 2, 0),
+    (0, 1, 0, 1), (0, 0, 1, 1), (0, 1, 1, 1), (0, 2, 1, 0), (0, 2, 0, 1), (0, 0, 0, 2), (0, 0, 1, 2), (0, 1, 0, 2),
+    (0, 0, 0, 3), (0, 1, 1, 2), (0, 0, 3, 0), (0, 0, 2, 1), (0, 1, 0, 3), (0, 2, 0, 2), (0, 2, 1, 1), (0, 3, 1, 0),
+    (0, 0, 1, 3), (0, 1, 1, 3), (0, 3, 0, 1), (0, 2, 0, 3), (0, 2, 1, 2), (0, 3, 0, 2), (0, 2, 1, 3), (0, 2, 2, 0),
+    (0, 0, 2, 2), (0, 0, 2, 3), (0, 3, 0, 0), (0, 1, 3, 0), (0, 1, 2, 2), (0, 3, 0, 3), (0, 3, 1, 1), (0, 1, 2, 1),
+    (0, 1, 2, 3), (0, 0, 3, 1), (0, 1, 3, 1), (0, 0, 4, 0), (0, 3, 1, 2), (0, 3, 1, 3), (4, 0, 3, 2), (5, 2, 3, 0),
+    (5, 2, 2, 2), (9, 2, 2, 1), (9, 0, 4, 1), (10, 3, 2, 0), (10, 1, 3, 2), (10, 0, 3, 3), (11, 1, 3, 3), (15, 2, 2, 3),
+    (15, 2, 3, 1), (16, 3, 2, 2), (18, 3, 3, 0), (18, 0, 4, 2), (18, 3, 2, 1), (20, 2, 3, 2), (21, 3, 2, 3), (22, 2, 3, 3),
+    (23, 1, 4, 2), (24, 0, 4, 3), (24, 1, 4, 3), (24, 3, 3, 1), (24, 1, 4, 0), (24, 1, 4, 1), (25, 3, 3, 2), (25, 3, 3, 3),
+    (29, 2, 4, 2), (33, 2, 4, 0), (33, 2, 4, 3), (36, 2, 4, 1), (38, 3, 4, 0), (40, 3, 4, 3), (41, 3, 4, 1), (41, 3, 4, 2),
+)
+
+
+def forward_kernel(length, plan, *refs):
     (shards, refs) = (refs[:5], refs[5:])
-    x_ref, c_ref = refs[:2]
+    x, c = refs[:2]
     (wholes, refs) = (refs[2:7], refs[7:])
-    n1_ref, merged, logsum, attended, middle, n2_ref, act, slope, grad_down, small, refs = refs[:10] + (refs[10:],)
-    b_up, qkv_bias, vec, hidden, sems, vsem = refs
+    n1, merged, logsum, attended, middle, n2, act, slope, grad_down, small, refs = refs[:10] + (refs[10:],)
+    b_up, qkv_bias, vec, hidden, x_ref, c_ref, n1_ref, n2_ref, sems, local = refs
     tokens, width = x_ref.shape
     p = Place()
     greet(p)
     order = [4, 0, 1, 2, 3]
-    g_vec, g_qkv, g_out, g_up, g_down = [Gather(p, shards[i], wholes[i], sems.at[i]) for i in order]
-    head = z_steps(g_vec) + weave(z_steps(g_qkv), xy_steps(g_vec))
-    head += weave(z_steps(g_out), xy_steps(g_qkv), diag_steps(g_vec))
-    for step in head:
-        step()
+    gathers = [Gather(p, shards[i], wholes[i], sems.at[i]) for i in order]
+    g_vec, g_qkv, g_out, g_up, g_down = gathers
+
+    def steps(at):
+        return [
+            lambda stage=stage, w=w, s=s: getattr(gathers[w], GATHER_STAGES[stage])(s)
+            for when, stage, w, s in plan
+            if when == at
+        ]
+
+    def run(at):
+        for step in steps(at):
+            step()
+
+    def turn(index, first, count, skip=0):
+        hook(index, {k: steps(first + k) for k in range(skip, count) if steps(first + k)})
+
+    loads = [pltpu.make_async_copy(x, x_ref, local.at[0]), pltpu.make_async_copy(c, c_ref, local.at[1])]
+    for load in loads:
+        load.start()
+    run(0)
     g_vec.arrived()
-    load = pltpu.make_async_copy(wholes[4], vec, vsem)
+    load = pltpu.make_async_copy(wholes[4], vec, local.at[2])
     load.start()
     load.wait()
+    for load in loads:
+        load.wait()
     for k in range(8):
         small[:, pl.ds(128 * k, 128)] = (vec[4 * k, 0, :8] + vec[4 * k + 2, 0, :8]).astype(F32)
     for k in range(16):
@@ -509,17 +530,18 @@
         return carry
 
     lax.fori_loop(0, tokens // 128, norm_rows, 0)
-    for step in weave(z_steps(g_up), diag_steps(g_qkv)):
-        step()
+    store_n1 = pltpu.make_async_copy(n1_ref, n1, local.at[0])
+    store_n1.start()
+    base = 1
+    run(base)
     g_qkv.arrived()
 
-    rest = weave(xy_steps(g_out), z_steps(g_down)) + diag_steps(g_out) + xy_steps(g_up)
     n_qkv, tile = 3 * width // 512, 512
-    table = spread(rest[:8], range(n_qkv))
+    first_qkv = base
 
     def qkv_body(w_ref, o_ref):
         j = pl.program_id(0)
-        hook(j, table)
+        turn(j, first_qkv, n_qkv, 1)
         bias = qkv_bias[:, pl.ds(pl.multiple_of(j * tile, tile), tile)]
         o_ref[...] = (dot(n1_ref[...], rows_of(w_ref)) + bias).astype(BF16)
 
@@ -531,11 +553,13 @@
     )(wholes[0], merged)
 
     pairs = width // 128
-    attend_table = spread(rest[8:], range(0, (tokens // length) * pairs, 2))
+    base += n_qkv
+    n_attend = (tokens // length) * pairs
+    first_attend = base
 
     def attend_body(q, k, v, o, l):
         s, h = pl.program_id(0), pl.program_id(1)
-        hook(s * pairs + h, attend_table)
+        turn(s * pairs + h, first_attend, n_attend)
         fwd_body(q, k, v, o, l.at[0, 0], 256)
 
     def head_spec(off):
@@ -548,12 +572,14 @@
         out_specs=[head_spec(0), pl.BlockSpec((1, 1, 2, length), lambda s, h: (s, h, 0, 0))],
     )(merged, merged, merged, attended, logsum)
 
+    base += n_attend
+    run(base)
     g_out.arrived()
-    out_table = spread(diag_steps(g_up), range(tokens // 256))
+    n_out, first_out = tokens // 256, base
 
     def out_body(a_ref, w_ref, m_ref):
         i = pl.program_id(0)
-        hook(i, out_table)
+        turn(i, first_out, n_out, 1)
         rows = pl.ds(pl.multiple_of(i * 256, 256), 256)
         value = x_ref[rows, :].astype(F32) + (dot(a_ref[...], rows_of(w_ref)) + small[2:3])
         m_ref[...] = value
@@ -566,9 +592,12 @@
         out_specs=[pl.BlockSpec((256, width), lambda i: (i, 0))],
     )(attended, wholes[1], middle)
 
+    store_n2 = pltpu.make_async_copy(n2_ref, n2, local.at[1])
+    store_n2.start()
+    base += n_out
+    run(base)
     g_up.arrived()
-    n_up = act.shape[1] // tile
-    up_table = spread(xy_steps(g_down), range(1, n_up, 2))
+    n_up, first_up = act.shape[1] // tile, base
 
     def gelu_tile(j, a_ref, s_ref):
         bias = b_up[:, pl.ds(pl.multiple_of(j * tile, tile), tile)]
@@ -579,7 +608,7 @@
 
     def up_body(w_ref, a_ref, s_ref):
         j = pl.program_id(0)
-        hook(j, up_table)
+        turn(j, first_up, n_up + 1, 1)
 
         @pl.when(j == 0)
         def _():
@@ -603,10 +632,11 @@
         out_specs=[late, late],
     )(wholes[2], act, slope)
 
-    down_table = spread(diag_steps(g_down), range(1, n_up, 2))
+    base += n_up + 1
+    first_grad = base
 
     def grad_body(a_ref, o_ref):
-        hook(pl.program_id(0), down_table)
+        turn(pl.program_id(0), first_grad, n_up)
         o_ref[...] = dot(a_ref[...], c_ref[...], TN).astype(BF16)
 
     pltpu.emit_pipeline(
@@ -615,9 +645,12 @@
         in_specs=[pl.BlockSpec((tokens, tile), lambda j: (0, j))],
         out_specs=[pl.BlockSpec((tile, width), lambda j: (j, 0))],
     )(act, grad_down)
+    run(base + n_up)
     g_down.arrived()
-    for g in (g_vec, g_qkv, g_out, g_up, g_down):
+    for g in gathers:
         g.drain()
+    store_n1.wait()
+    store_n2.wait()
 
 
 def forward_call(shards, x, c, length):
@@ -628,9 +661,9 @@
     vmem, any_space = pl.BlockSpec(memory_space=pltpu.VMEM), pl.BlockSpec(memory_space=pl.ANY)
     low = lambda *shape: jax.ShapeDtypeStruct(shape, BF16)
     outs = pl.pallas_call(
-        lambda *refs: forward_kernel(length, *refs),
-        in_specs=[vmem] * 7,
-        out_specs=[any_space] * 5 + [vmem] + [any_space] * 4 + [vmem] + [any_space] * 3 + [vmem],
+        lambda *refs: forward_kernel(length, GATHER_PLAN, *refs),
+        in_specs=[vmem] * 5 + [any_space] * 2,
+        out_specs=[any_space] * 14 + [vmem],
         out_shape=whole
         + [
             low(tokens, width),
@@ -649,8 +682,12 @@
             pltpu.VMEM((1, 3 * width), F32),
             pltpu.VMEM(whole[4].shape, BF16),
             pltpu.VMEM((2, tokens, 512), F32),
+            pltpu.VMEM((tokens, width), BF16),
+            pltpu.VMEM((tokens, width), BF16),
+            pltpu.VMEM((tokens, width), BF16),
+            pltpu.VMEM((tokens, width), BF16),
             pltpu.SemaphoreType.DMA((5, AG_SEMS)),
-            pltpu.SemaphoreType.DMA,
+            pltpu.SemaphoreType.DMA((3,)),
         ],
         compiler_params=pltpu.CompilerParams(collective_id=0, has_side_effects=True, vmem_limit_bytes=VMEM_LIMIT),
         name="forward",
@@ -659,27 +696,27 @@
 
 
 PLAN = (
-    (4, 0, 0, 0), (5, 1, 0, 0), (5, 0, 0, 1), (6, 1, 0, 1), (7, 0, 0, 2), (8, 1, 0, 2), (8, 2, 0, 0), (8, 0, 0, 3),
-    (9, 1, 0, 3), (11, 2, 0, 1), (14, 2, 0, 2), (16, 3, 0, 0), (17, 0, 1, 0), (18, 1, 1, 0), (18, 0, 1, 1), (19, 2, 0, 3),
-    (19, 1, 1, 1), (19, 0, 1, 2), (20, 4, 0, 0), (20, 3, 0, 1), (20, 1, 1, 2), (20, 0, 1, 3), (21, 3, 0, 2), (21, 4, 0, 2),
-    (21, 1, 1, 3), (22, 2, 1, 0), (24, 4, 0, 1), (24, 3, 0, 3), (24, 4, 0, 3), (27, 2, 1, 1), (28, 0, 2, 0), (30, 2, 1, 2),
-    (30, 1, 2, 0), (30, 0, 2, 1), (32, 5, 0, 0), (32, 2, 1, 3), (32, 1, 2, 1), (32, 0, 2, 2), (33, 3, 1, 0), (33, 3, 1, 1),
-    (33, 1, 2, 2), (33, 0, 2, 3), (34, 3, 1, 2), (34, 4, 1, 2), (34, 1, 2, 3), (35, 4, 1, 0), (35, 2, 2, 0), (36, 3, 1, 3),
-    (37, 4, 1, 1), (37, 2, 2, 1), (37, 4, 1, 3), (37, 0, 3, 0), (38, 2, 2, 2), (38, 1, 3, 0), (38, 0, 3, 1), (38, 0, 3, 2),
-    (39, 5, 1, 0), (39, 2, 2, 3), (39, 1, 3, 1), (39, 1, 3, 2), (39, 3, 2, 0), (39, 0, 3, 3), (40, 3, 2, 1), (40, 1, 3, 3),
-    (40, 3, 2, 2), (40, 4, 2, 2), (41, 4, 2, 0), (41, 2, 3, 0), (42, 4, 2, 1), (42, 3, 2, 3), (42, 2, 3, 1), (43, 4, 2, 3),
-    (43, 2, 3, 2), (43, 2, 3, 3), (43, 3, 3, 0), (44, 3, 3, 1), (44, 3, 3, 2), (44, 4, 3, 2), (44, 3, 3, 3), (45, 5, 2, 0),
-    (45, 4, 3, 0), (45, 4, 3, 1), (47, 4, 3, 3), (49, 5, 3, 0), (57, 0, 4, 0), (57, 0, 4, 1), (58, 1, 4, 0), (58, 1, 4, 1),
-    (58, 0, 4, 2), (58, 0, 4, 3), (59, 1, 4, 2), (59, 1, 4, 3), (59, 2, 4, 0), (59, 0, 5, 0), (59, 0, 5, 1), (60, 2, 4, 1),
-    (60, 1, 5, 0), (60, 1, 5, 1), (60, 2, 4, 2), (60, 0, 5, 2), (60, 0, 5, 3), (60, 0, 6, 0), (60, 0, 6, 1), (61, 3, 4, 0),
-    (61, 2, 4, 3), (61, 1, 5, 2), (61, 3, 4, 1), (61, 1, 5, 3), (61, 1, 6, 0), (61, 1, 6, 1), (61, 2, 5, 0), (61, 0, 6, 2),
-    (61, 0, 6, 3), (62, 4, 4, 0), (62, 3, 4, 2), (62, 4, 4, 1), (62, 4, 4, 2), (62, 3, 4, 3), (62, 2, 5, 1), (62, 1, 6, 2),
-    (62, 1, 6, 3), (63, 4, 4, 3), (63, 2, 5, 2), (63, 2, 5, 3), (64, 2, 6, 0), (65, 5, 4, 0), (65, 3, 5, 0), (65, 2, 6, 1),
-    (66, 3, 5, 1), (67, 2, 6, 2), (68, 4, 5, 0), (68, 2, 6, 3), (69, 4, 5, 1), (69, 3, 5, 2), (69, 4, 5, 2), (69, 3, 5, 3),
-    (70, 3, 6, 0), (71, 4, 5, 3), (71, 3, 6, 1), (71, 3, 6, 2), (71, 4, 6, 2), (72, 3, 6, 3), (73, 5, 5, 0), (73, 4, 6, 0),
-    (73, 0, 7, 0), (73, 4, 6, 1), (73, 0, 7, 1), (74, 1, 7, 0), (74, 1, 7, 1), (74, 0, 7, 2), (74, 0, 7, 3), (75, 4, 6, 3),
-    (75, 2, 7, 0), (75, 2, 7, 1), (75, 1, 7, 2), (75, 1, 7, 3), (76, 3, 7, 0), (76, 3, 7, 1), (76, 2, 7, 2), (76, 2, 7, 3),
-    (76, 5, 6, 0), (77, 4, 7, 0), (77, 4, 7, 1), (77, 3, 7, 2), (77, 4, 7, 2), (77, 3, 7, 3), (78, 4, 7, 3), (79, 5, 7, 0),
+    (5, 0, 0, 0), (7, 1, 0, 0), (7, 0, 0, 1), (9, 1, 0, 1), (9, 0, 0, 2), (11, 1, 0, 2), (11, 0, 0, 3), (12, 2, 0, 0),
+    (13, 1, 0, 3), (16, 2, 0, 1), (18, 0, 1, 0), (19, 2, 0, 2), (19, 0, 1, 1), (20, 1, 1, 0), (21, 3, 0, 0), (21, 1, 1, 1),
+    (21, 0, 1, 2), (22, 0, 1, 3), (23, 1, 1, 2), (24, 2, 0, 3), (24, 1, 1, 3), (27, 3, 0, 1), (28, 4, 0, 0), (30, 0, 2, 0),
+    (30, 3, 0, 2), (30, 4, 0, 2), (32, 0, 2, 1), (33, 2, 1, 0), (33, 1, 2, 0), (33, 1, 2, 1), (33, 0, 2, 2), (34, 4, 0, 1),
+    (34, 2, 1, 1), (34, 1, 2, 2), (34, 0, 2, 3), (35, 2, 1, 2), (35, 1, 2, 3), (36, 3, 0, 3), (36, 4, 0, 3), (38, 2, 1, 3),
+    (39, 3, 1, 0), (39, 0, 3, 0), (39, 0, 3, 1), (40, 2, 2, 0), (41, 5, 0, 0), (41, 1, 3, 0), (41, 1, 3, 1), (41, 0, 3, 2),
+    (41, 0, 3, 3), (42, 4, 1, 0), (42, 3, 1, 1), (42, 2, 2, 1), (43, 1, 3, 2), (43, 1, 3, 3), (44, 2, 2, 2), (45, 3, 1, 2),
+    (45, 4, 1, 2), (46, 4, 1, 1), (46, 2, 2, 3), (47, 3, 1, 3), (47, 4, 1, 3), (48, 3, 2, 0), (49, 2, 3, 0), (50, 3, 2, 1),
+    (50, 2, 3, 1), (51, 5, 1, 0), (51, 2, 3, 2), (52, 4, 2, 0), (52, 2, 3, 3), (53, 4, 2, 1), (53, 3, 2, 2), (53, 4, 2, 2),
+    (53, 3, 2, 3), (54, 3, 3, 0), (54, 3, 3, 1), (54, 3, 3, 2), (54, 4, 3, 2), (55, 4, 2, 3), (55, 3, 3, 3), (57, 4, 3, 0),
+    (57, 0, 4, 0), (58, 5, 2, 0), (58, 4, 3, 1), (58, 1, 4, 0), (58, 0, 4, 1), (58, 0, 4, 2), (59, 0, 5, 0), (60, 4, 3, 3),
+    (60, 1, 4, 1), (60, 1, 4, 2), (60, 0, 4, 3), (60, 0, 5, 1), (61, 2, 4, 0), (61, 1, 5, 0), (61, 0, 5, 2), (62, 1, 4, 3),
+    (62, 1, 5, 1), (62, 0, 5, 3), (62, 0, 6, 0), (62, 0, 6, 1), (63, 5, 3, 0), (63, 2, 4, 1), (63, 2, 4, 2), (63, 1, 5, 2),
+    (64, 3, 4, 0), (64, 1, 5, 3), (64, 1, 6, 0), (64, 1, 6, 1), (64, 0, 6, 2), (64, 0, 6, 3), (64, 2, 5, 0), (66, 2, 4, 3),
+    (66, 1, 6, 2), (66, 1, 6, 3), (67, 4, 4, 0), (67, 3, 4, 1), (67, 2, 5, 1), (68, 3, 4, 2), (68, 4, 4, 2), (69, 2, 5, 2),
+    (70, 2, 5, 3), (71, 4, 4, 1), (71, 2, 6, 0), (72, 2, 6, 1), (73, 3, 4, 3), (73, 4, 4, 3), (73, 3, 5, 0), (74, 2, 6, 2),
+    (74, 0, 7, 0), (74, 0, 7, 1), (75, 3, 5, 1), (75, 2, 6, 3), (76, 5, 4, 0), (76, 4, 5, 0), (76, 3, 5, 2), (76, 4, 5, 2),
+    (76, 3, 5, 3), (76, 1, 7, 0), (76, 3, 6, 0), (76, 1, 7, 1), (76, 0, 7, 2), (76, 0, 7, 3), (77, 3, 6, 1), (77, 3, 6, 2),
+    (77, 4, 6, 2), (78, 4, 5, 1), (78, 3, 6, 3), (78, 2, 7, 0), (78, 2, 7, 1), (78, 1, 7, 2), (78, 1, 7, 3), (79, 4, 5, 3),
+    (80, 4, 6, 0), (80, 3, 7, 0), (80, 3, 7, 1), (80, 2, 7, 2), (80, 2, 7, 3), (81, 4, 6, 1), (83, 5, 5, 0), (83, 4, 7, 0),
+    (83, 4, 7, 1), (83, 3, 7, 2), (83, 4, 7, 2), (83, 3, 7, 3), (84, 4, 6, 3), (86, 4, 7, 3), (88, 5, 6, 0), (88, 5, 7, 0),
 )
 
 PRE, S0, S1, S2, S3, S4 = range(6)

time: 361 us -> 296 us (0.82)
  Pallas kernels: 345 us -> 280 us
    pallas_call x1, Pallas kernels: 163 us -> 123 us  [forward_call(): pl.pallas_call(lambda *refs: forward_kernel(length, GATHER_PLAN, *refs),...]
    pallas_call x1, Pallas kernels: 182 us -> 157 us  [backward_call(): pl.pallas_call(lambda *refs: backward_kernel(length, PLAN, parts, *refs),...]
where the time goes in v3:
time: 296 us; the launch traced here: 294 us
  Pallas kernels  280 us (95%)
  local copies, waits for them, and re-layouts  11.5 us (4%)
    pallas_call x1, Pallas kernels, backward_call(): pl.pallas_call(lambda *refs: backward_kernel(length, PLAN, parts, *refs),...  157 us
    pallas_call x1, Pallas kernels, forward_call(): pl.pallas_call(lambda *refs: forward_kernel(length, GATHER_PLAN, *refs),...  123 us
    unnamed x16, local copies, waits for them, and re-layouts  8.76 us

profile of v3, /device:TPU:0, one launch (start us, length us, event | category | flops | bytes accessed | tf_op | source)
XLA Modules:
  0.0 294.1 jit_solution(8918727228294875168)
XLA Ops:
  0.7 0.8 stack.35
  1.5 1.3 fusion.4
  2.8 122.6 %forward.1 = (bf16[32,2,16,3072]{3,2,1,0:T(8,128)(2,1)}, bf16[32,2,16,1024]{3,2,1,0:T(8,128)(2,1)}, bf16[32,2,16,4096]{3,2,1,0:T(8,128)(2,1)}, bf16[32,2,64,1024...) custom-call(bf16[2,2,16,3072]{3,2,1,0:T(8,128)(2,1)} %bitcast.54, ...), custom_call_target="tpu_custom_call" | custom-call | tf_op jit(solution)/shard_map/forward/pallas_call | solution.py:663
  125.4 157.2 %backward.1 = (bf16[1024,1024]{1,0:T(8,128)(2,1)}, f32[1024,1024]{1,0:T(8,128)}, f32[2,2,16,3072]{3,2,1,0:T(8,128)}, f32[2,2,16,1024]{3,2,1,0:T(8,128)}, f32[2,2...) custom-call(bf16[32,2,16,3072]{3,2,1,0:T(8,128)(2,1)} %get-tuple-ele, ...), custom_call_target="tpu_custom_call" | custom-call | tf_op jit(solution)/shard_map/backward/pallas_call | solution.py:1011
  282.6 0.0 copy-start
  282.6 1.4 slice_bitcast_fusion
  284.0 0.8 slice_select_fusion
  284.8 0.5 slice_bitcast_fusion.1
  285.3 3.1 %copy.36 = bf16[2,512,1024]{2,1,0:T(8,128)(2,1)} copy(bf16[2,512,1024]{2,1,0:T(8,128)(2,1)} %bitcast.48) | data formatting | bytes 4194304
  288.4 0.0 copy-done
  288.4 0.0 copy-start.3
  288.4 0.0 copy-start.4
  288.4 0.0 copy-start.2
  288.4 2.1 copy.37
  290.6 0.0 copy-done.3
  290.6 0.0 copy-start.1
  290.6 0.9 copy.38
  291.4 0.0 copy-done.4
  291.4 0.7 copy.39
  292.2 0.0 copy-done.2
  292.2 1.0 copy.40
  293.1 0.0 copy-done.1
  293.1 1.0 copy.41
  (1 shorter events, 0.0 us)
Async XLA Ops:
  282.6 5.8 %copy-start = (f32[1024,1024]{1,0:T(8,128)S(1)}, f32[1024,1024]{1,0:T(8,128)}, u32[]{:S(2)}) copy-start(f32[1024,1024]{1,0:T(8,128)} %get-tuple-element.51) | copy-start | bytes 12582916
  288.4 2.1 copy-start.3
  288.4 3.0 %copy-start.4 = (f32[2,2,16,1024]{3,2,1,0:T(8,128)S(1)}, f32[2,2,16,1024]{3,2,1,0:T(8,128)}, u32[]{:S(2)}) copy-start(f32[2,2,16,1024]{3,2,1,0:T(8,128)} %get-tuple-element.53) | copy-start | bytes 786436
  288.4 3.7 %copy-start.2 = (f32[2,2,16,4096]{3,2,1,0:T(8,128)S(1)}, f32[2,2,16,4096]{3,2,1,0:T(8,128)}, u32[]{:S(2)}) copy-start(f32[2,2,16,4096]{3,2,1,0:T(8,128)} %get-tuple-element.54) | copy-start | bytes 3145732
  290.6 2.6 copy-start.1

commit v4 on v3

--- a/solution.py
+++ b/solution.py
@@ -81,6 +81,14 @@
         pl.semaphore_wait(barrier, 4)
 
 
+def greet_column(p):
+    barrier = pltpu.get_barrier_semaphore()
+    column = [p.dev((p.z + k) % 4, p.y, p.x) for k in (1, 2, 3)]
+    for device in [p.xn, p.yn, p.partner] + column:
+        pl.semaphore_signal(barrier, inc=1, device_id=device, device_id_type=MESH)
+    pl.semaphore_wait(barrier, 6)
+
+
 def remote(src, dst, send, recv, device):
     return pltpu.make_async_remote_copy(
         src_ref=src, dst_ref=dst, send_sem=send, recv_sem=recv, device_id=device, device_id_type=MESH
@@ -349,6 +357,56 @@
         for k, ref in enumerate((self.x1, self.y1, self.x2, self.y2)):
             wait_bytes(ref, self.sems.at[32 + k])
         wait_bytes(self.u.at[pl.ds(0, 3)], self.zsend)
+
+
+class VectorScatter:
+    def __init__(self, p, g, out, bufs, sems):
+        self.p, self.g, self.out, self.sems = p, g, out, sems
+        self.pv, self.xv, self.yv, self.zv, self.t1, self.t2, self.t3 = bufs
+
+    @staticmethod
+    def scratch():
+        shapes = [(4, 2, 2), (4, 2), (4,), (4,), (4, 2, 2), (4, 2), (4,)]
+        return [pltpu.VMEM(shape + (16, 128), F32) for shape in shapes]
+
+    def start(self):
+        remote(self.g, self.pv, self.sems.at[0], self.sems.at[1], self.p.partner).start()
+
+    def cores(self):
+        p = self.p
+        wait_bytes(self.pv, self.sems.at[1])
+        self.t1[...] = self.g[...] + self.pv[...]
+        remote(self.t1.at[:, :, 1 - p.x], self.xv, self.sems.at[2], self.sems.at[3], p.xn).start()
+
+    def over_x(self):
+        p = self.p
+        wait_bytes(self.xv, self.sems.at[3])
+        self.t2[...] = self.t1[:, :, p.x] + self.xv[...]
+        remote(self.t2.at[:, 1 - p.y], self.yv, self.sems.at[4], self.sems.at[5], p.yn).start()
+
+    def over_y(self):
+        p = self.p
+        wait_bytes(self.yv, self.sems.at[5])
+        self.t3[...] = self.t2[:, p.y] + self.yv[...]
+        for k in (1, 2, 3):
+            z = (p.z + k) % 4
+            there = p.dev(z, p.y, p.x)
+            remote(self.t3.at[z], self.zv.at[p.z], self.sems.at[6], self.sems.at[8 + p.z], there).start()
+
+    def over_z(self):
+        p = self.p
+        total = self.t3[p.z]
+        for k in (1, 2, 3):
+            z = (p.z + k) % 4
+            wait_bytes(self.zv.at[z], self.sems.at[8 + z])
+            total = total + self.zv[z]
+        self.out[...] = total
+
+    def finish(self):
+        wait_bytes(self.g, self.sems.at[0])
+        wait_bytes(self.xv, self.sems.at[2])
+        wait_bytes(self.yv, self.sems.at[4])
+        wait_bytes(self.zv.at[pl.ds(0, 3)], self.sems.at[6])
 
 
 def lane_masks(rows, width, dtype=BF16):
@@ -378,36 +436,44 @@
             o=dot(pt,vs[h][:end],TN)
             acc=o if acc is None else acc+o
         o_ref[b*B:end,:]=acc.astype(BF16)
-def bwd_body(q_ref,k_ref,v_ref,g_ref,l_ref,dq_ref,dk_ref,dv_ref,dk_acc,dv_acc,B):
-    S=q_ref.shape[0]
-    low=lane_masks(S,128)
-    q=q_ref[...]*BF16(0.125); k=k_ref[...]; v=v_ref[...]; g=g_ref[...]
-    qs=[pick(h,low,q) for h in (0,1)]; gs=[pick(h,low,g) for h in (0,1)]; ks=[pick(h,low,k) for h in (0,1)]
-    for b in reversed(range(S//B)):
-        end=(b+1)*B
-        dq=None; dk=None; dv=None
-        for h in (0,1):
-            qb=qs[h][b*B:end]; gb=gs[h][b*B:end]
-            st=dot(k[:end],qb,NT)
-            p=jnp.exp(st-l_ref[h:h+1,b*B:end])
-            key=lax.broadcasted_iota(jnp.int32,(B,B),0); qry=lax.broadcasted_iota(jnp.int32,(B,B),1)
-            diag=jnp.where(key<=qry, p[b*B:end], 0.0)
-            p=jnp.concatenate([p[:b*B],diag],0) if b else diag
-            dp=dot(v[:end],gb,NT)
-            inner=jnp.sum(p*dp,0,keepdims=True)
-            ds=(p*(dp-inner)).astype(BF16)
-            pb=p.astype(BF16)
-            dvh=dot(pb,gb,NN); dkh=dot(ds,qb,NN); dqh=dot(ds,ks[h][:end],TN)
-            dq=dqh if dq is None else dq+dqh
-            dk=dkh if dk is None else dk+dkh
-            dv=dvh if dv is None else dv+dvh
-        dq_ref[b*B:end,:]=(dq*0.125).astype(BF16)
-        if b==S//B-1:
-            dk_acc[...]=dk; dv_acc[...]=dv
+def bwd_body(q_ref, k_ref, v_ref, g_ref, l_ref, dq_ref, dk_ref, dv_ref, dk_acc, dv_acc, B):
+    S = q_ref.shape[0]
+    low = lane_masks(S, 128)
+    q = q_ref[...] * BF16(0.125)
+    k, v, g = k_ref[...], v_ref[...], g_ref[...]
+    qs, gs, ks = ([pick(h, low, t) for h in (0, 1)] for t in (q, g, k))
+    key = lax.broadcasted_iota(jnp.int32, (B, B), 0)
+    query = lax.broadcasted_iota(jnp.int32, (B, B), 1)
+    blocks = list(reversed(range(S // B)))
+    scores, grads = {}, {}
+    for b in blocks:
+        end = (b + 1) * B
+        for h in (0, 1):
+            scores[b, h] = dot(k[:end], qs[h][b * B : end], NT)
+            grads[b, h] = dot(v[:end], gs[h][b * B : end], NT)
+    for b in blocks:
+        end = (b + 1) * B
+        dq = dk = dv = None
+        for h in (0, 1):
+            qb, gb = qs[h][b * B : end], gs[h][b * B : end]
+            p = jnp.exp(scores[b, h] - l_ref[h : h + 1, b * B : end])
+            diag = jnp.where(key <= query, p[b * B : end], 0.0)
+            p = jnp.concatenate([p[: b * B], diag], 0) if b else diag
+            inner = jnp.sum(p * grads[b, h], 0, keepdims=True)
+            ds = (p * (grads[b, h] - inner)).astype(BF16)
+            parts = dot(ds, ks[h][:end], TN), dot(ds, qb, NN), dot(p.astype(BF16), gb, NN)
+            dq, dk, dv = parts if h == 0 else (dq + parts[0], dk + parts[1], dv + parts[2])
+        dq_ref[b * B : end, :] = (dq * 0.125).astype(BF16)
+        if b == S // B - 1:
+            dk_acc[...] = dk
+            dv_acc[...] = dv
         else:
-            dk_acc[:end,:]+=dk; dv_acc[:end,:]+=dv
-    dk_ref[...]=dk_acc[...].astype(BF16)
-    dv_ref[...]=dv_acc[...].astype(BF16)
+            dk_acc[:end, :] += dk
+            dv_acc[:end, :] += dv
+    dk_ref[...] = dk_acc[...].astype(BF16)
+    dv_ref[...] = dv_acc[...].astype(BF16)
+
+
 def attn_fwd(merged, S, B=256):
     T=merged.shape[0]; D=merged.shape[1]//3; n=D//128
     def body(q,k,v,o,l): fwd_body(q,k,v,o,l.at[0,0],B)
@@ -465,31 +531,42 @@
 
 
 GATHER_PLAN = (
-    (0, 0, 0, 0), (0, 0, 1, 0), (0, 1, 0, 0), (0, 1, 1, 0), (0, 0, 0, 1), (0, 0, 2, 0), (0, 2, 0, 0), (0, 1, 2, 0),
-    (0, 1, 0, 1), (0, 0, 1, 1), (0, 1, 1, 1), (0, 2, 1, 0), (0, 2, 0, 1), (0, 0, 0, 2), (0, 0, 1, 2), (0, 1, 0, 2),
-    (0, 0, 0, 3), (0, 1, 1, 2), (0, 0, 3, 0), (0, 0, 2, 1), (0, 1, 0, 3), (0, 2, 0, 2), (0, 2, 1, 1), (0, 3, 1, 0),
-    (0, 0, 1, 3), (0, 1, 1, 3), (0, 3, 0, 1), (0, 2, 0, 3), (0, 2, 1, 2), (0, 3, 0, 2), (0, 2, 1, 3), (0, 2, 2, 0),
-    (0, 0, 2, 2), (0, 0, 2, 3), (0, 3, 0, 0), (0, 1, 3, 0), (0, 1, 2, 2), (0, 3, 0, 3), (0, 3, 1, 1), (0, 1, 2, 1),
-    (0, 1, 2, 3), (0, 0, 3, 1), (0, 1, 3, 1), (0, 0, 4, 0), (0, 3, 1, 2), (0, 3, 1, 3), (4, 0, 3, 2), (5, 2, 3, 0),
-    (5, 2, 2, 2), (9, 2, 2, 1), (9, 0, 4, 1), (10, 3, 2, 0), (10, 1, 3, 2), (10, 0, 3, 3), (11, 1, 3, 3), (15, 2, 2, 3),
-    (15, 2, 3, 1), (16, 3, 2, 2), (18, 3, 3, 0), (18, 0, 4, 2), (18, 3, 2, 1), (20, 2, 3, 2), (21, 3, 2, 3), (22, 2, 3, 3),
-    (23, 1, 4, 2), (24, 0, 4, 3), (24, 1, 4, 3), (24, 3, 3, 1), (24, 1, 4, 0), (24, 1, 4, 1), (25, 3, 3, 2), (25, 3, 3, 3),
-    (29, 2, 4, 2), (33, 2, 4, 0), (33, 2, 4, 3), (36, 2, 4, 1), (38, 3, 4, 0), (40, 3, 4, 3), (41, 3, 4, 1), (41, 3, 4, 2),
+    (0, 0, 1, 0), (0, 1, 1, 0), (0, 0, 0, 0), (0, 0, 2, 0), (0, 1, 0, 0), (0, 1, 2, 0), (0, 0, 0, 1), (0, 2, 1, 0),
+    (0, 0, 1, 1), (0, 2, 0, 0), (0, 1, 0, 1), (0, 1, 1, 1), (0, 0, 2, 1), (0, 2, 2, 0), (0, 0, 0, 2), (0, 1, 0, 2),
+    (0, 0, 1, 2), (0, 1, 1, 2), (0, 2, 0, 1), (0, 0, 3, 0), (0, 3, 0, 0), (0, 0, 0, 3), (0, 0, 2, 2), (0, 2, 0, 2),
+    (0, 1, 2, 2), (0, 0, 1, 3), (0, 1, 0, 3), (0, 3, 1, 0), (0, 2, 1, 2), (0, 1, 1, 3), (0, 0, 5, 0), (0, 3, 0, 1),
+    (0, 3, 0, 2), (0, 0, 3, 1), (0, 2, 0, 3), (0, 0, 2, 3), (0, 1, 2, 3), (0, 3, 0, 3), (0, 2, 1, 1), (0, 2, 1, 3),
+    (0, 1, 3, 0), (0, 1, 2, 1), (0, 0, 4, 0), (0, 1, 3, 1), (0, 0, 6, 0), (1, 3, 1, 1), (1, 3, 1, 3), (1, 1, 5, 0),
+    (1, 3, 1, 2), (1, 2, 2, 3), (1, 0, 3, 2), (1, 2, 2, 2), (1, 2, 3, 0), (2, 0, 4, 1), (2, 1, 3, 2), (3, 2, 2, 1),
+    (5, 1, 4, 0), (6, 2, 3, 1), (6, 0, 5, 1), (6, 0, 4, 2), (7, 3, 2, 2), (7, 1, 4, 1), (9, 2, 5, 0), (9, 3, 2, 3),
+    (10, 1, 4, 2), (10, 3, 2, 0), (10, 0, 5, 2), (10, 3, 2, 1), (10, 3, 3, 0), (11, 0, 6, 1), (11, 2, 3, 2), (11, 0, 3, 3),
+    (12, 1, 3, 3), (12, 0, 4, 3), (12, 1, 4, 3), (12, 1, 5, 2), (14, 0, 5, 3), (16, 0, 6, 2), (16, 2, 4, 0), (17, 2, 4, 3),
+    (17, 2, 3, 3), (18, 1, 5, 1), (19, 2, 4, 2), (20, 2, 4, 1), (20, 3, 3, 2), (21, 3, 3, 3), (21, 3, 3, 1), (22, 1, 5, 3),
+    (22, 2, 5, 2), (22, 0, 6, 3), (24, 3, 4, 0), (25, 2, 5, 1), (25, 3, 4, 3), (25, 1, 6, 1), (25, 2, 5, 3), (26, 3, 4, 2),
+    (26, 1, 6, 3), (26, 3, 4, 1), (26, 1, 6, 0), (27, 3, 5, 2), (29, 3, 5, 3), (29, 3, 5, 1), (29, 1, 6, 2), (30, 3, 5, 0),
+    (34, 2, 6, 0), (36, 2, 6, 1), (36, 2, 6, 2), (36, 2, 6, 3), (38, 3, 6, 0), (41, 3, 6, 1), (42, 3, 6, 2), (42, 3, 6, 3),
 )
 
 
 def forward_kernel(length, plan, *refs):
-    (shards, refs) = (refs[:5], refs[5:])
+    (s_qkv, s_out, s_up, s_down, s_vec), refs = refs[:5], refs[5:]
     x, c = refs[:2]
-    (wholes, refs) = (refs[2:7], refs[7:])
+    (wholes, refs) = (refs[2:9], refs[9:])
     n1, merged, logsum, attended, middle, n2, act, slope, grad_down, small, refs = refs[:10] + (refs[10:],)
-    b_up, qkv_bias, vec, hidden, x_ref, c_ref, n1_ref, n2_ref, sems, local = refs
+    b_up, qkv_bias, vec, x_ref, c_ref, n1_ref, n2_ref, first_half, second_half, sems, local = refs
     tokens, width = x_ref.shape
     p = Place()
+    for part, half in enumerate((first_half, second_half)):
+        for k in range(3):
+            columns = pl.ds(k * width + part * width // 2, width // 2)
+            half[:, :, :, pl.ds(k * width // 2, width // 2)] = s_qkv[:, :, :, columns]
     greet(p)
-    order = [4, 0, 1, 2, 3]
-    gathers = [Gather(p, shards[i], wholes[i], sems.at[i]) for i in order]
-    g_vec, g_qkv, g_out, g_up, g_down = gathers
+    n_half = s_up.shape[3] // 2
+    lows, highs = (s_up.at[:, :, :, pl.ds(k * n_half, n_half)] for k in (0, 1))
+    sources = (first_half, second_half, s_out, lows, highs, s_down, s_vec)
+    order = [6, 0, 1, 2, 3, 4, 5]
+    gathers = [Gather(p, sources[i], wholes[i], sems.at[i]) for i in order]
+    g_vec, g_first, g_second, g_out, g_low, g_high, g_down = gathers
 
     def steps(at):
         return [
@@ -510,7 +587,7 @@
         load.start()
     run(0)
     g_vec.arrived()
-    load = pltpu.make_async_copy(wholes[4], vec, local.at[2])
+    load = pltpu.make_async_copy(wholes[6], vec, local.at[2])
     load.start()
     load.wait()
     for load in loads:
@@ -533,46 +610,51 @@
     store_n1 = pltpu.make_async_copy(n1_ref, n1, local.at[0])
     store_n1.start()
     base = 1
-    run(base)
-    g_qkv.arrived()
-
-    n_qkv, tile = 3 * width // 512, 512
-    first_qkv = base
-
-    def qkv_body(w_ref, o_ref):
-        j = pl.program_id(0)
-        turn(j, first_qkv, n_qkv, 1)
-        bias = qkv_bias[:, pl.ds(pl.multiple_of(j * tile, tile), tile)]
-        o_ref[...] = (dot(n1_ref[...], rows_of(w_ref)) + bias).astype(BF16)
-
-    pltpu.emit_pipeline(
-        qkv_body,
-        grid=(n_qkv,),
-        in_specs=[whole_spec(wholes[0], tile)],
-        out_specs=[pl.BlockSpec((tokens, tile), lambda j: (0, j))],
-    )(wholes[0], merged)
-
-    pairs = width // 128
-    base += n_qkv
+    tile = 512
+
+    halves = width // tile
+    pairs = width // 128 // halves
     n_attend = (tokens // length) * pairs
-    first_attend = base
-
-    def attend_body(q, k, v, o, l):
-        s, h = pl.program_id(0), pl.program_id(1)
-        turn(s * pairs + h, first_attend, n_attend)
-        fwd_body(q, k, v, o, l.at[0, 0], 256)
 
     def head_spec(off):
         return pl.BlockSpec((length, 128), lambda s, h: (s, off + h))
 
-    pltpu.emit_pipeline(
-        attend_body,
-        grid=(tokens // length, pairs),
-        in_specs=[head_spec(0), head_spec(pairs), head_spec(2 * pairs)],
-        out_specs=[head_spec(0), pl.BlockSpec((1, 1, 2, length), lambda s, h: (s, h, 0, 0))],
-    )(merged, merged, merged, attended, logsum)
-
-    base += n_attend
+    for part, (g, whole) in enumerate(((g_first, wholes[0]), (g_second, wholes[1]))):
+        run(base)
+        g.arrived()
+
+        def qkv_body(w_ref, o_ref, first=base, part=part):
+            j = pl.program_id(0)
+            turn(j, first, 3, 1)
+            at = pl.ds(pl.multiple_of((j * halves + part) * tile, tile), tile)
+            o_ref[...] = (dot(n1_ref[...], rows_of(w_ref)) + qkv_bias[:, at]).astype(BF16)
+
+        pltpu.emit_pipeline(
+            qkv_body,
+            grid=(3,),
+            in_specs=[whole_spec(whole, tile)],
+            out_specs=[pl.BlockSpec((tokens, tile), lambda j, part=part: (0, j * halves + part))],
+        )(whole, merged)
+        base += 3
+
+        def attend_body(q, k, v, o, l, first=base):
+            s, h = pl.program_id(0), pl.program_id(1)
+            turn(s * pairs + h, first, n_attend)
+            fwd_body(q, k, v, o, l.at[0, 0], 256)
+
+        off = part * pairs
+        third = width // 128
+        pltpu.emit_pipeline(
+            attend_body,
+            grid=(tokens // length, pairs),
+            in_specs=[head_spec(off), head_spec(third + off), head_spec(2 * third + off)],
+            out_specs=[
+                head_spec(off),
+                pl.BlockSpec((1, 1, 2, length), lambda s, h, off=off: (s, off + h, 0, 0)),
+            ],
+        )(merged, merged, merged, attended, logsum)
+        base += n_attend
+
     run(base)
     g_out.arrived()
     n_out, first_out = tokens // 256, base
@@ -588,51 +670,36 @@
     pltpu.emit_pipeline(
         out_body,
         grid=(tokens // 256,),
-        in_specs=[pl.BlockSpec((256, width), lambda i: (i, 0)), whole_spec(wholes[1])],
+        in_specs=[pl.BlockSpec((256, width), lambda i: (i, 0)), whole_spec(wholes[2])],
         out_specs=[pl.BlockSpec((256, width), lambda i: (i, 0))],
-    )(attended, wholes[1], middle)
+    )(attended, wholes[2], middle)
 
     store_n2 = pltpu.make_async_copy(n2_ref, n2, local.at[1])
     store_n2.start()
     base += n_out
-    run(base)
-    g_up.arrived()
-    n_up, first_up = act.shape[1] // tile, base
-
-    def gelu_tile(j, a_ref, s_ref):
-        bias = b_up[:, pl.ds(pl.multiple_of(j * tile, tile), tile)]
-
-        value, grad = gelu_pair(hidden[j % 2] + bias)
-        a_ref[...] = value.astype(BF16)
-        s_ref[...] = grad.astype(BF16)
-
-    def up_body(w_ref, a_ref, s_ref):
-        j = pl.program_id(0)
-        turn(j, first_up, n_up + 1, 1)
-
-        @pl.when(j == 0)
-        def _():
-            hidden[0] = dot(n2_ref[...], rows_of(w_ref))
-
-        @pl.when(jnp.logical_and(j > 0, j < n_up))
-        def _():
-            gelu_tile(j - 1, a_ref, s_ref)
-            hidden[j % 2] = dot(n2_ref[...], rows_of(w_ref))
-
-        @pl.when(j == n_up)
-        def _():
-            gelu_tile(j - 1, a_ref, s_ref)
-
-    n, two, q, _ = wholes[2].shape
-    late = pl.BlockSpec((tokens, tile), lambda j: (0, jnp.maximum(j - 1, 0)))
-    pltpu.emit_pipeline(
-        up_body,
-        grid=(n_up + 1,),
-        in_specs=[pl.BlockSpec((n, two, q, tile), lambda j: (0, 0, 0, jnp.minimum(j, n_up - 1)))],
-        out_specs=[late, late],
-    )(wholes[2], act, slope)
-
-    base += n_up + 1
+    n_up = act.shape[1] // tile
+    n_part = n_up // 2
+    for part, (g, whole) in enumerate(((g_low, wholes[3]), (g_high, wholes[4]))):
+        run(base)
+        g.arrived()
+
+        def up_body(w_ref, a_ref, s_ref, first=base, part=part):
+            j = pl.program_id(0)
+            turn(j, first, n_part, 1)
+            bias = b_up[:, pl.ds(pl.multiple_of((part * n_part + j) * tile, tile), tile)]
+            value, grad = gelu_pair(dot(n2_ref[...], rows_of(w_ref)) + bias)
+            a_ref[...] = value.astype(BF16)
+            s_ref[...] = grad.astype(BF16)
+
+        column_spec = pl.BlockSpec((tokens, tile), lambda j, part=part: (0, part * n_part + j))
+        pltpu.emit_pipeline(
+            up_body,
+            grid=(n_part,),
+            in_specs=[whole_spec(whole, tile)],
+            out_specs=[column_spec, column_spec],
+        )(whole, act, slope)
+        base += n_part
+
     first_grad = base
 
     def grad_body(a_ref, o_ref):
@@ -657,13 +724,16 @@
     tokens, width = x.shape
     hidden = 16 * shards[3].shape[0]
     views = [s.reshape(2, 2, s.shape[0] // 4, s.shape[1]) for s in shards]
-    whole = [jax.ShapeDtypeStruct((32,) + v.shape[1:], v.dtype) for v in views]
+    q = views[0].shape[2]
+    columns = [3 * width // 2] * 2 + [width] + [hidden // 2] * 2
+    whole = [jax.ShapeDtypeStruct((32, 2, q, n), BF16) for n in columns]
+    whole += [jax.ShapeDtypeStruct((32,) + v.shape[1:], BF16) for v in views[3:]]
     vmem, any_space = pl.BlockSpec(memory_space=pltpu.VMEM), pl.BlockSpec(memory_space=pl.ANY)
     low = lambda *shape: jax.ShapeDtypeStruct(shape, BF16)
     outs = pl.pallas_call(
         lambda *refs: forward_kernel(length, GATHER_PLAN, *refs),
         in_specs=[vmem] * 5 + [any_space] * 2,
-        out_specs=[any_space] * 14 + [vmem],
+        out_specs=[any_space] * 16 + [vmem],
         out_shape=whole
         + [
             low(tokens, width),
@@ -680,43 +750,42 @@
         scratch_shapes=[
             pltpu.VMEM((1, hidden), F32),
             pltpu.VMEM((1, 3 * width), F32),
-            pltpu.VMEM(whole[4].shape, BF16),
-            pltpu.VMEM((2, tokens, 512), F32),
+            pltpu.VMEM(whole[6].shape, BF16),
             pltpu.VMEM((tokens, width), BF16),
             pltpu.VMEM((tokens, width), BF16),
             pltpu.VMEM((tokens, width), BF16),
             pltpu.VMEM((tokens, width), BF16),
-            pltpu.SemaphoreType.DMA((5, AG_SEMS)),
+            pltpu.VMEM((2, 2, q, 3 * width // 2), BF16),
+            pltpu.VMEM((2, 2, q, 3 * width // 2), BF16),
+            pltpu.SemaphoreType.DMA((7, AG_SEMS)),
             pltpu.SemaphoreType.DMA((3,)),
         ],
         compiler_params=pltpu.CompilerParams(collective_id=0, has_side_effects=True, vmem_limit_bytes=VMEM_LIMIT),
         name="forward",
     )(*views, x, c)
-    return outs[:4], outs[5:]
+    return outs[:6], outs[7:]
 
 
 PLAN = (
-    (5, 0, 0, 0), (7, 1, 0, 0), (7, 0, 0, 1), (9, 1, 0, 1), (9, 0, 0, 2), (11, 1, 0, 2), (11, 0, 0, 3), (12, 2, 0, 0),
-    (13, 1, 0, 3), (16, 2, 0, 1), (18, 0, 1, 0), (19, 2, 0, 2), (19, 0, 1, 1), (20, 1, 1, 0), (21, 3, 0, 0), (21, 1, 1, 1),
-    (21, 0, 1, 2), (22, 0, 1, 3), (23, 1, 1, 2), (24, 2, 0, 3), (24, 1, 1, 3), (27, 3, 0, 1), (28, 4, 0, 0), (30, 0, 2, 0),
-    (30, 3, 0, 2), (30, 4, 0, 2), (32, 0, 2, 1), (33, 2, 1, 0), (33, 1, 2, 0), (33, 1, 2, 1), (33, 0, 2, 2), (34, 4, 0, 1),
-    (34, 2, 1, 1), (34, 1, 2, 2), (34, 0, 2, 3), (35, 2, 1, 2), (35, 1, 2, 3), (36, 3, 0, 3), (36, 4, 0, 3), (38, 2, 1, 3),
-    (39, 3, 1, 0), (39, 0, 3, 0), (39, 0, 3, 1), (40, 2, 2, 0), (41, 5, 0, 0), (41, 1, 3, 0), (41, 1, 3, 1), (41, 0, 3, 2),
-    (41, 0, 3, 3), (42, 4, 1, 0), (42, 3, 1, 1), (42, 2, 2, 1), (43, 1, 3, 2), (43, 1, 3, 3), (44, 2, 2, 2), (45, 3, 1, 2),
-    (45, 4, 1, 2), (46, 4, 1, 1), (46, 2, 2, 3), (47, 3, 1, 3), (47, 4, 1, 3), (48, 3, 2, 0), (49, 2, 3, 0), (50, 3, 2, 1),
-    (50, 2, 3, 1), (51, 5, 1, 0), (51, 2, 3, 2), (52, 4, 2, 0), (52, 2, 3, 3), (53, 4, 2, 1), (53, 3, 2, 2), (53, 4, 2, 2),
-    (53, 3, 2, 3), (54, 3, 3, 0), (54, 3, 3, 1), (54, 3, 3, 2), (54, 4, 3, 2), (55, 4, 2, 3), (55, 3, 3, 3), (57, 4, 3, 0),
-    (57, 0, 4, 0), (58, 5, 2, 0), (58, 4, 3, 1), (58, 1, 4, 0), (58, 0, 4, 1), (58, 0, 4, 2), (59, 0, 5, 0), (60, 4, 3, 3),
-    (60, 1, 4, 1), (60, 1, 4, 2), (60, 0, 4, 3), (60, 0, 5, 1), (61, 2, 4, 0), (61, 1, 5, 0), (61, 0, 5, 2), (62, 1, 4, 3),
-    (62, 1, 5, 1), (62, 0, 5, 3), (62, 0, 6, 0), (62, 0, 6, 1), (63, 5, 3, 0), (63, 2, 4, 1), (63, 2, 4, 2), (63, 1, 5, 2),
-    (64, 3, 4, 0), (64, 1, 5, 3), (64, 1, 6, 0), (64, 1, 6, 1), (64, 0, 6, 2), (64, 0, 6, 3), (64, 2, 5, 0), (66, 2, 4, 3),
-    (66, 1, 6, 2), (66, 1, 6, 3), (67, 4, 4, 0), (67, 3, 4, 1), (67, 2, 5, 1), (68, 3, 4, 2), (68, 4, 4, 2), (69, 2, 5, 2),
-    (70, 2, 5, 3), (71, 4, 4, 1), (71, 2, 6, 0), (72, 2, 6, 1), (73, 3, 4, 3), (73, 4, 4, 3), (73, 3, 5, 0), (74, 2, 6, 2),
-    (74, 0, 7, 0), (74, 0, 7, 1), (75, 3, 5, 1), (75, 2, 6, 3), (76, 5, 4, 0), (76, 4, 5, 0), (76, 3, 5, 2), (76, 4, 5, 2),
-    (76, 3, 5, 3), (76, 1, 7, 0), (76, 3, 6, 0), (76, 1, 7, 1), (76, 0, 7, 2), (76, 0, 7, 3), (77, 3, 6, 1), (77, 3, 6, 2),
-    (77, 4, 6, 2), (78, 4, 5, 1), (78, 3, 6, 3), (78, 2, 7, 0), (78, 2, 7, 1), (78, 1, 7, 2), (78, 1, 7, 3), (79, 4, 5, 3),
-    (80, 4, 6, 0), (80, 3, 7, 0), (80, 3, 7, 1), (80, 2, 7, 2), (80, 2, 7, 3), (81, 4, 6, 1), (83, 5, 5, 0), (83, 4, 7, 0),
-    (83, 4, 7, 1), (83, 3, 7, 2), (83, 4, 7, 2), (83, 3, 7, 3), (84, 4, 6, 3), (86, 4, 7, 3), (88, 5, 6, 0), (88, 5, 7, 0),
+    (4, 0, 0, 0), (6, 1, 0, 0), (10, 0, 0, 1), (13, 1, 0, 1), (14, 2, 0, 0), (18, 0, 0, 2), (18, 0, 1, 0), (19, 0, 1, 1),
+    (20, 1, 0, 2), (22, 0, 0, 3), (24, 1, 1, 0), (25, 1, 1, 1), (25, 1, 0, 3), (28, 0, 2, 0), (30, 1, 2, 0), (31, 0, 2, 2),
+    (33, 3, 0, 0), (33, 1, 2, 2), (33, 2, 1, 1), (33, 2, 0, 1), (34, 0, 2, 1), (36, 2, 2, 0), (36, 2, 0, 2), (36, 1, 2, 1),
+    (36, 0, 1, 3), (38, 2, 1, 0), (39, 1, 1, 3), (39, 0, 3, 1), (39, 0, 3, 0), (41, 2, 0, 3), (42, 0, 2, 3), (43, 0, 1, 2),
+    (44, 3, 1, 1), (44, 3, 0, 1), (44, 2, 2, 1), (44, 1, 3, 1), (46, 2, 1, 3), (46, 1, 2, 3), (47, 1, 1, 2), (49, 1, 3, 0),
+    (49, 0, 3, 2), (50, 2, 3, 1), (50, 0, 3, 3), (51, 1, 3, 3), (51, 3, 0, 2), (51, 3, 1, 0), (51, 3, 2, 1), (51, 1, 3, 2),
+    (54, 4, 0, 0), (54, 3, 2, 0), (54, 2, 3, 0), (55, 2, 3, 3), (55, 2, 2, 2), (55, 2, 1, 2), (56, 2, 3, 2), (57, 2, 2, 3),
+    (57, 3, 3, 1), (57, 0, 4, 1), (57, 4, 0, 1), (57, 0, 4, 0), (58, 1, 4, 0), (58, 1, 4, 1), (58, 0, 4, 3), (58, 3, 1, 2),
+    (58, 0, 5, 0), (58, 3, 3, 0), (58, 4, 1, 2), (59, 1, 5, 0), (59, 0, 5, 1), (60, 1, 5, 1), (60, 4, 2, 0), (60, 3, 2, 2),
+    (60, 0, 6, 0), (60, 2, 4, 0), (61, 0, 5, 2), (61, 3, 0, 3), (61, 2, 4, 1), (61, 0, 6, 1), (61, 4, 2, 2), (61, 1, 6, 0),
+    (61, 2, 5, 0), (62, 4, 1, 0), (62, 2, 5, 1), (62, 3, 4, 0), (62, 4, 1, 1), (62, 1, 6, 1), (62, 4, 0, 3), (62, 0, 6, 3),
+    (62, 3, 2, 3), (62, 1, 4, 3), (62, 4, 2, 1), (62, 0, 6, 2), (63, 1, 5, 2), (63, 2, 6, 0), (63, 3, 1, 3), (63, 3, 3, 2),
+    (63, 0, 5, 3), (63, 1, 6, 2), (63, 3, 3, 3), (63, 0, 4, 2), (63, 4, 3, 0), (64, 3, 5, 0), (64, 2, 6, 1), (64, 1, 5, 3),
+    (64, 4, 3, 1), (64, 4, 2, 3), (64, 3, 5, 1), (64, 1, 6, 3), (64, 4, 1, 3), (65, 1, 4, 2), (65, 4, 4, 0), (66, 3, 6, 0),
+    (66, 2, 4, 3), (67, 2, 6, 2), (67, 4, 5, 0), (67, 4, 0, 2), (67, 2, 5, 2), (67, 3, 6, 1), (67, 2, 5, 3), (68, 4, 6, 0),
+    (68, 4, 3, 3), (68, 3, 4, 1), (68, 2, 6, 3), (68, 3, 4, 3), (68, 5, 0, 0), (68, 4, 5, 1), (68, 2, 4, 2), (68, 4, 3, 2),
+    (68, 3, 6, 2), (68, 4, 4, 3), (68, 4, 6, 1), (69, 3, 5, 2), (69, 3, 5, 3), (69, 4, 5, 2), (69, 3, 6, 3), (69, 4, 6, 3),
+    (69, 5, 2, 0), (69, 5, 1, 0), (69, 4, 6, 2), (69, 3, 4, 2), (69, 4, 4, 2), (69, 5, 3, 0), (69, 4, 4, 1), (69, 4, 5, 3),
+    (71, 5, 6, 0), (71, 5, 4, 0), (71, 5, 5, 0),
 )
 
 PRE, S0, S1, S2, S3, S4 = range(6)
@@ -728,22 +797,23 @@
 
 
 def backward_kernel(length, plan, n_up_parts, *refs):
-    (w_qkv, w_out, w_up, w_down), refs = refs[:4], refs[4:]
+    (w_first, w_second, w_out, w_low, w_high, w_down), refs = refs[:6], refs[6:]
     x, c, n1, merged, logsum, attended, middle, n2, act, slope, g_down, small, refs = refs[:12] + (refs[12:],)
     output, input_grad, f_qkv, f_out, f_up, f_down, f_vec, g_qkv, g_out, g_up, mid_grad, ag, back, refs = refs[:13] + (
         refs[13:],
     )
-    landing, refs = refs[:8], refs[8:]
-    sets, refs = refs[: 8 * 7], refs[8 * 7 :]
-    tmps, refs = refs[:8], refs[8:]
-    (g_vec, narrow, wide, left, right, acc, branch, dk_acc, dv_acc, sems, csem) = refs
+    landing, refs = refs[:7], refs[7:]
+    sets, refs = refs[: 7 * 7], refs[7 * 7 :]
+    tmps, refs = refs[:7], refs[7:]
+    vec_bufs, refs = refs[:7], refs[7:]
+    (g_vec, narrow, wide, left, right, acc, out_acc, branch, dk_acc, dv_acc, sems, vec_sems, csem) = refs
     tokens, width = x.shape
     hidden = act.shape[1]
     tile = 512
     pairs = width // 128
     p = Place()
-    greet(p)
-    sets = [sets[7 * i : 7 * i + 7] for i in range(8)]
+    greet_column(p)
+    sets = [sets[7 * i : 7 * i + 7] for i in range(7)]
     half = hidden // n_up_parts
     entries = [
         (g_down, f_down),
@@ -753,9 +823,10 @@
         (g_qkv.at[0], f_qkv.at[:, :, :, pl.ds(0, width)]),
         (g_qkv.at[1], f_qkv.at[:, :, :, pl.ds(width, width)]),
         (g_qkv.at[2], f_qkv.at[:, :, :, pl.ds(2 * width, width)]),
-        (g_vec, f_vec),
     ]
     rs = [Scatter(p, g, f, landing[k], sets[k], tmps[k], sems.at[k]) for k, (g, f) in enumerate(entries)]
+
+    vectors = VectorScatter(p, g_vec, f_vec, vec_bufs, vec_sems)
 
     def turn(slot, first, count):
         table = {}
@@ -775,12 +846,13 @@
     wide[...] = jnp.zeros_like(wide)
     g_vec[...] = jnp.zeros_like(g_vec)
     acc[...] = jnp.zeros_like(acc)
+    out_acc[...] = jnp.zeros_like(out_acc)
     for load in loads:
         load.wait()
 
     n_up = hidden // tile
 
-    def ffn_body(wd, s, wu, g):
+    def ffn_body(wd, s, wu_low, wu_high, g):
         j = pl.program_id(0)
 
         @pl.when(j == n_up // 2 + 1)
@@ -794,22 +866,31 @@
         turn(3 * j + 1, 0, 3 * n_up)
         g[0] = dot(right[...], grad, TN).astype(BF16).reshape(g.shape[1:])
         turn(3 * j + 2, 0, 3 * n_up)
-        acc[...] += dot(grad, rows_of(wu), NT)
+
+        @pl.when(j < n_up // 2)
+        def _():
+            acc[...] += dot(grad, rows_of(wu_low), NT)
+
+        @pl.when(j >= n_up // 2)
+        def _():
+            acc[...] += dot(grad, rows_of(wu_high), NT)
 
     per = n_up // n_up_parts
     q_down = w_down.shape[2]
     blocks = tile // (2 * q_down)
     shape = g_up.shape[1:7]
+    n, two, q, _ = w_low.shape
     pltpu.emit_pipeline(
         ffn_body,
         grid=(n_up,),
         in_specs=[
             pl.BlockSpec((blocks, 2, q_down, width), lambda j: (j, 0, 0, 0)),
             pl.BlockSpec((tokens, tile), lambda j: (0, j)),
-            whole_spec(w_up, tile),
+            pl.BlockSpec((n, two, q, tile), lambda j: (0, 0, 0, jnp.minimum(j, n_up // 2 - 1))),
+            pl.BlockSpec((n, two, q, tile), lambda j: (0, 0, 0, jnp.maximum(j - n_up // 2, 0))),
         ],
         out_specs=[pl.BlockSpec((1,) + shape + (tile,), lambda j: (j // per, 0, 0, 0, 0, 0, 0, j % per))],
-    )(w_down, slope, w_up, g_up)
+    )(w_down, slope, w_low, w_high, g_up)
     rs[2].start()
     load = pltpu.make_async_copy(n1, right, csem.at[1])
     load.start()
@@ -817,10 +898,13 @@
 
     step = 128
     n_rows = tokens // step
-
-    def norm_two_body(m, o):
+    thin = hidden // (2 * n_rows)
+    first_two = base
+
+    def norm_two_body(m, a, w, o):
         i = pl.program_id(0)
-        turn(base + i, base, n_rows)
+        turn(first_two + i, first_two, n_rows)
+        out_acc[...] += dot(a[...], rows_of(w))
         rows = pl.ds(pl.multiple_of(i * step, step), step)
         upstream = left[rows, :].astype(F32)
         part, gain, shift = norm_back(m[...], small[6:7], acc[rows, :])
@@ -834,7 +918,16 @@
         narrow[7:8] += shift[None]
 
     row_spec = pl.BlockSpec((step, width), lambda i: (i, 0))
-    pltpu.emit_pipeline(norm_two_body, grid=(n_rows,), in_specs=[row_spec], out_specs=[row_spec])(middle, mid_grad)
+    pltpu.emit_pipeline(
+        norm_two_body,
+        grid=(n_rows,),
+        in_specs=[
+            row_spec,
+            pl.BlockSpec((tokens, thin), lambda i: (0, i)),
+            pl.BlockSpec((thin // (2 * q_down), 2, q_down, width), lambda i: (i, 0, 0, 0)),
+        ],
+        out_specs=[row_spec],
+    )(middle, act, w_down, mid_grad)
     base += n_rows
 
     n_out = width // 256
@@ -916,15 +1009,33 @@
     first_in = base
     acc[...] = jnp.zeros_like(acc)
 
-    def in_body(d, w):
+    def in_body(d, w_one, w_two):
         j = pl.program_id(0)
         turn(first_in + j, first_in, n_qkv)
-        acc[...] += dot(d[0], rows_of(w), NT)
-
-    pltpu.emit_pipeline(in_body, grid=(n_qkv,), in_specs=[back_spec, whole_spec(w_qkv, tile)])(back, w_qkv)
+
+        @pl.when(j < 3)
+        def _():
+            acc[...] += dot(d[0], rows_of(w_one), NT)
+
+        @pl.when(j >= 3)
+        def _():
+            acc[...] += dot(d[0], rows_of(w_two), NT)
+
+    n, two, q, _ = w_first.shape
+    pltpu.emit_pipeline(
+        in_body,
+        grid=(n_qkv,),
+        in_specs=[
+            pl.BlockSpec((1, tokens, tile), lambda j: (j % 3, 0, j // 3)),
+            pl.BlockSpec((n, two, q, tile), lambda j: (0, 0, 0, jnp.minimum(j, 2))),
+            pl.BlockSpec((n, two, q, tile), lambda j: (0, 0, 0, jnp.maximum(j - 3, 0))),
+        ],
+    )(back, w_first, w_second)
     base += n_qkv
 
     first_one = base
+    step = 256
+    n_rows = tokens // step
 
     def norm_one_body(v, m, o):
         i = pl.program_id(0)
@@ -935,49 +1046,55 @@
         narrow[4:5] += gain[None]
         narrow[5:6] += shift[None]
 
+    row_spec = pl.BlockSpec((step, width), lambda i: (i, 0))
     pltpu.emit_pipeline(norm_one_body, grid=(n_rows,), in_specs=[row_spec] * 2, out_specs=[row_spec])(
         x, mid_grad, input_grad
     )
     base += n_rows
     for k in range(16):
-        z, y, xx = k // 4, (k // 2) % 2, k % 2
-        g_vec[z, y, xx, 0, 0] = narrow[:, 128 * (k // 2) : 128 * (k // 2) + 128]
+        at = (k // 4, (k // 2) % 2, k % 2)
+        g_vec[at + (pl.ds(0, 8),)] = narrow[:, 128 * (k // 2) : 128 * (k // 2) + 128]
         for i in range(2):
-            g_vec[z, y, xx, 0, 1, i : i + 1] = wide[:, 256 * k + 128 * i : 256 * k + 128 * i + 128]
-    rs[7].start()
-    acc[...] = jnp.zeros_like(acc)
-
+            g_vec[at + (pl.ds(8 + i, 1),)] = wide[:, 256 * k + 128 * i : 256 * k + 128 * i + 128]
+
+    load = pltpu.make_async_copy(middle, acc, csem.at[0])
+    load.start()
     first_down = base
+    n_down = n_up // 2
+    vector_steps = {0: [vectors.start], 1: [vectors.cores], 3: [vectors.over_x]}
 
     def down_body(a, w):
         j = pl.program_id(0)
-        turn(first_down + j, first_down, n_up)
-        acc[...] += dot(a[...], rows_of(w))
+        hook(j, vector_steps)
+        turn(first_down + j, first_down, n_down)
+        out_acc[...] += dot(a[...], rows_of(w))
 
     pltpu.emit_pipeline(
         down_body,
-        grid=(n_up,),
+        grid=(n_down,),
         in_specs=[
-            pl.BlockSpec((tokens, tile), lambda j: (0, j)),
-            pl.BlockSpec((blocks, 2, q_down, width), lambda j: (j, 0, 0, 0)),
+            pl.BlockSpec((tokens, tile), lambda j: (0, n_down + j)),
+            pl.BlockSpec((blocks, 2, q_down, width), lambda j: (n_down + j, 0, 0, 0)),
         ],
     )(act, w_down)
-    base += n_up
-    first_last = base
-
-    def last_body(m, o):
-        i = pl.program_id(0)
-        turn(first_last + i, first_last, n_rows)
-        rows = pl.ds(pl.multiple_of(i * step, step), step)
-        o[...] = (m[...] + (acc[rows, :] + small[3:4])).astype(BF16)
-
-    pltpu.emit_pipeline(last_body, grid=(n_rows,), in_specs=[row_spec], out_specs=[row_spec])(middle, output)
-    base += n_rows
+    base += n_down
+    load.wait()
+    n_last, step = 4, tokens // 4
+    stores = []
+    for i in range(n_last):
+        rows = pl.ds(i * step, step)
+        branch[rows, :] = (acc[rows, :] + (out_acc[rows, :] + small[3:4])).astype(BF16)
+        stores.append(pltpu.make_async_copy(branch.at[rows], output.at[rows], csem.at[i]))
+        stores[-1].start()
+    vectors.over_y()
     for at, stage, k, i in plan:
         if at >= base:
             getattr(rs[k], STAGES[stage])(i)
-    for r in rs:
+    vectors.over_z()
+    for r in rs + [vectors]:
         r.finish()
+    for store in stores:
+        store.wait()
 
 
 def backward_call(weights, x, c, kept, length):
@@ -989,32 +1106,35 @@
     low = lambda *shape: jax.ShapeDtypeStruct(shape, BF16)
     full = lambda *shape: jax.ShapeDtypeStruct(shape, F32)
     vmem, any_space = pl.BlockSpec(memory_space=pltpu.VMEM), pl.BlockSpec(memory_space=pl.ANY)
-    kinds = [(q_down, width, BF16)] + [(q, hidden // parts, BF16)] * 2 + [(q, width, BF16)] * 4 + [(8, 128, F32)]
+    kinds = [(q_down, width, BF16)] + [(q, hidden // parts, BF16)] * 2 + [(q, width, BF16)] * 4
     scratch = []
     for kind in kinds:
         scratch += Scatter.scratch(*kind)
     scratch += [pltpu.VMEM((2, 2, 2, 2) + kind[:2], kind[2]) for kind in kinds]
+    scratch += VectorScatter.scratch()
     scratch += [
-        pltpu.VMEM((4, 2, 2, 2, 2, 8, 128), F32),
+        pltpu.VMEM((4, 2, 2, 16, 128), F32),
         pltpu.VMEM((8, width), F32),
         pltpu.VMEM((1, hidden), F32),
         pltpu.VMEM((tokens, width), BF16),
         pltpu.VMEM((tokens, width), BF16),
         pltpu.VMEM((tokens, width), F32),
+        pltpu.VMEM((tokens, width), F32),
         pltpu.VMEM((tokens, width), BF16),
         pltpu.VMEM((length, 128), F32),
         pltpu.VMEM((length, 128), F32),
-        pltpu.SemaphoreType.DMA((8, RS_SEMS)),
-        pltpu.SemaphoreType.DMA((2,)),
+        pltpu.SemaphoreType.DMA((7, RS_SEMS)),
+        pltpu.SemaphoreType.DMA((12,)),
+        pltpu.SemaphoreType.DMA((4,)),
     ]
     shards = [full(2, 2, q, 3 * width), full(2, 2, q, width), full(2, 2, q, hidden), full(2, 2, q_down, width)]
     outs = pl.pallas_call(
         lambda *refs: backward_kernel(length, PLAN, parts, *refs),
-        in_specs=[any_space] * 15 + [vmem],
-        out_specs=[any_space] * 2 + [vmem] * 5 + [any_space] * 14,
+        in_specs=[any_space] * 17 + [vmem],
+        out_specs=[any_space] * 2 + [vmem] * 5 + [any_space] * 13,
         out_shape=[low(tokens, width), full(tokens, width)]
         + shards
-        + [full(2, 2, 8, 128)]
+        + [full(16, 128)]
         + [
             low(3, 4, 2, 2, 2, 2, q, width),
             low(4, 2, 2, 2, 2, q, width),
@@ -1031,7 +1151,7 @@
         name="backward",
     )(*weights, x, c, n1, merged, logsum, attended, middle, n2, act, slope, g_down.reshape(4, 2, 2, 2, 2, q_down, width), small)
     grads = [o.reshape(-1, o.shape[-1]) for o in outs[2:6]]
-    return outs[0], outs[1], grads, outs[6].reshape(32, 128)
+    return outs[0], outs[1], grads, outs[6]
 
 
 def forward_plain(x, weights, small, length):

time: 296 us -> 283 us (0.956)
  Pallas kernels: 280 us -> 267 us
    pallas_call x1, Pallas kernels: 157 us -> 149 us  [backward_call(): pl.pallas_call(lambda *refs: backward_kernel(length, PLAN, parts, *refs),...]
    pallas_call x1, Pallas kernels: 123 us -> 119 us  [forward_call(): pl.pallas_call(lambda *refs: forward_kernel(length, GATHER_PLAN, *refs),...]
where the time goes in v4:
time: 283 us; the launch traced here: 282 us
  Pallas kernels  267 us (94%)
  local copies, waits for them, and re-layouts  11.5 us (4%)
    pallas_call x1, Pallas kernels, backward_call(): pl.pallas_call(lambda *refs: backward_kernel(length, PLAN, parts, *refs),...  149 us
    pallas_call x1, Pallas kernels, forward_call(): pl.pallas_call(lambda *refs: forward_kernel(length, GATHER_PLAN, *refs),...  119 us
    unnamed x16, local copies, waits for them, and re-layouts  8.76 us

profile of v4, /device:TPU:0, one launch (start us, length us, event | category | flops | bytes accessed | tf_op | source)
XLA Modules:
  0.0 281.8 jit_solution(15073747754430999598)
XLA Ops:
  0.7 0.8 stack.35
  1.5 1.3 fusion.4
  2.8 118.6 %forward.1 = (bf16[32,2,16,1536]{3,2,1,0:T(8,128)(2,1)}, bf16[32,2,16,1536]{3,2,1,0:T(8,128)(2,1)}, bf16[32,2,16,1024]{3,2,1,0:T(8,128)(2,1)}, bf16[32,2,16,2048...) custom-call(bf16[2,2,16,3072]{3,2,1,0:T(8,128)(2,1)} %bitcast.53, ...), custom_call_target="tpu_custom_call" | custom-call | tf_op jit(solution)/shard_map/forward/pallas_call | solution.py:733
  121.4 148.9 %backward.1 = (bf16[1024,1024]{1,0:T(8,128)(2,1)}, f32[1024,1024]{1,0:T(8,128)}, f32[2,2,16,3072]{3,2,1,0:T(8,128)}, f32[2,2,16,1024]{3,2,1,0:T(8,128)}, f32[2,2...) custom-call(bf16[32,2,16,1536]{3,2,1,0:T(8,128)(2,1)} %get-tuple-ele, ...), custom_call_target="tpu_custom_call" | custom-call | tf_op jit(solution)/shard_map/backward/pallas_call | solution.py:1131
  270.3 0.0 copy-start
  270.3 1.4 slice_bitcast_fusion
  271.7 0.8 slice_select_fusion
  272.5 0.5 slice_bitcast_fusion.1
  273.1 3.1 %copy.36 = bf16[2,512,1024]{2,1,0:T(8,128)(2,1)} copy(bf16[2,512,1024]{2,1,0:T(8,128)(2,1)} %bitcast.47) | data formatting | bytes 4194304
  276.1 0.0 copy-done
  276.2 0.0 copy-start.3
  276.2 0.0 copy-start.4
  276.2 0.0 copy-start.2
  276.2 2.1 copy.37
  278.3 0.0 copy-done.3
  278.3 0.0 copy-start.1
  278.3 0.9 copy.38
  279.2 0.0 copy-done.4
  279.2 0.7 copy.39
  279.9 0.0 copy-done.2
  279.9 1.0 copy.40
  280.9 0.0 copy-done.1
  280.9 1.0 copy.41
  (1 shorter events, 0.0 us)
Async XLA Ops:
  270.3 5.9 %copy-start = (f32[1024,1024]{1,0:T(8,128)S(1)}, f32[1024,1024]{1,0:T(8,128)}, u32[]{:S(2)}) copy-start(f32[1024,1024]{1,0:T(8,128)} %get-tuple-element.55) | copy-start | bytes 12582916
  276.2 2.1 copy-start.3
  276.2 3.0 %copy-start.4 = (f32[2,2,16,1024]{3,2,1,0:T(8,128)S(1)}, f32[2,2,16,1024]{3,2,1,0:T(8,128)}, u32[]{:S(2)}) copy-start(f32[2,2,16,1024]{3,2,1,0:T(8,128)} %get-tuple-element.57) | copy-start | bytes 786436
  276.2 3.7 %copy-start.2 = (f32[2,2,16,4096]{3,2,1,0:T(8,128)S(1)}, f32[2,2,16,4096]{3,2,1,0:T(8,128)}, u32[]{:S(2)}) copy-start(f32[2,2,16,4096]{3,2,1,0:T(8,128)} %get-tuple-element.58) | copy-start | bytes 3145732
  278.3 2.6 copy-start.1

commit v5 on v4

--- a/solution.py
+++ b/solution.py
@@ -220,12 +220,25 @@
 
 
 def hook(index, table):
-    for k, steps in table.items():
-
-        @pl.when(index == k)
-        def _(steps=steps):
-            for step in steps:
-                step()
+    keys = sorted(table)
+    if len(keys) <= 1:
+        for k in keys:
+
+            @pl.when(index == k)
+            def _(k=k):
+                for step in table[k]:
+                    step()
+
+        return
+    middle = keys[len(keys) // 2]
+
+    @pl.when(index < middle)
+    def _():
+        hook(index, {k: table[k] for k in keys if k < middle})
+
+    @pl.when(index >= middle)
+    def _():
+        hook(index, {k: table[k] for k in keys if k >= middle})
 
 
 RS_SEMS = 44
@@ -266,14 +279,14 @@
         p = self.p
         z = self.level(i)
         wait_bytes(self.o.at[z], self.sem(1, i))
-        wait_bytes(self.tmp.at[i % 2], self.sems.at[40 + i])
-
-        def add(j, carry):
-            y, x, k = j // 4, (j // 2) % 2, j % 2
-            self.o[z, y, x, k] = self.o[z, y, x, k] + self.tmp[i % 2, y, x, k]
-            return carry
-
-        lax.fori_loop(0, 8, add, 0)
+        if self.tmp is None:
+            theirs = self.pr.at[z]
+            wait_bytes(theirs, self.sem(0, i))
+        else:
+            theirs = self.tmp.at[i % 2]
+            wait_bytes(theirs, self.sems.at[40 + i])
+
+        self.o[z] = self.o[z] + theirs[...]
         remote(self.o.at[z, :, 1 - p.x, 0], self.x1.at[z], self.sems.at[32], self.sem(2, i), p.xn).start()
         remote(self.o.at[z, 1 - p.y, :, 1], self.y1.at[z], self.sems.at[33], self.sem(3, i), p.yn).start()
 
@@ -400,7 +413,9 @@
             z = (p.z + k) % 4
             wait_bytes(self.zv.at[z], self.sems.at[8 + z])
             total = total + self.zv[z]
-        self.out[...] = total
+        narrow = lax.broadcasted_iota(jnp.int32, total.shape, 0) < 8
+        moved = jnp.logical_and(narrow, p.x == 1)
+        self.out[...] = jnp.where(moved, pltpu.roll(total, 64, 1), total)
 
     def finish(self):
         wait_bytes(self.g, self.sems.at[0])
@@ -518,11 +533,11 @@
     return value, slope
 
 
-def whole_spec(ref, tile=None):
+def whole_spec(ref, tile=None, first=0):
     n, two, q, width = ref.shape
     if tile is None:
         return pl.BlockSpec((n, two, q, width), lambda j: (0, 0, 0, 0))
-    return pl.BlockSpec((n, two, q, tile), lambda j: (0, 0, 0, j))
+    return pl.BlockSpec((n, two, q, tile), lambda j: (0, 0, 0, first + j))
 
 
 def rows_of(block):
@@ -551,7 +566,7 @@
 def forward_kernel(length, plan, *refs):
     (s_qkv, s_out, s_up, s_down, s_vec), refs = refs[:5], refs[5:]
     x, c = refs[:2]
-    (wholes, refs) = (refs[2:9], refs[9:])
+    (w_qkv, w_out, w_up, w_down, w_vec), refs = refs[2:7], refs[7:]
     n1, merged, logsum, attended, middle, n2, act, slope, grad_down, small, refs = refs[:10] + (refs[10:],)
     b_up, qkv_bias, vec, x_ref, c_ref, n1_ref, n2_ref, first_half, second_half, sems, local = refs
     tokens, width = x_ref.shape
@@ -563,9 +578,17 @@
     greet(p)
     n_half = s_up.shape[3] // 2
     lows, highs = (s_up.at[:, :, :, pl.ds(k * n_half, n_half)] for k in (0, 1))
-    sources = (first_half, second_half, s_out, lows, highs, s_down, s_vec)
-    order = [6, 0, 1, 2, 3, 4, 5]
-    gathers = [Gather(p, sources[i], wholes[i], sems.at[i]) for i in order]
+    columns = 3 * width // 2
+    pieces = [
+        (s_vec, w_vec),
+        (first_half, w_qkv.at[:, :, :, pl.ds(0, columns)]),
+        (second_half, w_qkv.at[:, :, :, pl.ds(columns, columns)]),
+        (s_out, w_out),
+        (lows, w_up.at[:, :, :, pl.ds(0, n_half)]),
+        (highs, w_up.at[:, :, :, pl.ds(n_half, n_half)]),
+        (s_down, w_down),
+    ]
+    gathers = [Gather(p, source, whole, sems.at[i]) for i, (source, whole) in enumerate(pieces)]
     g_vec, g_first, g_second, g_out, g_low, g_high, g_down = gathers
 
     def steps(at):
@@ -587,7 +610,7 @@
         load.start()
     run(0)
     g_vec.arrived()
-    load = pltpu.make_async_copy(wholes[6], vec, local.at[2])
+    load = pltpu.make_async_copy(w_vec, vec, local.at[2])
     load.start()
     load.wait()
     for load in loads:
@@ -619,7 +642,7 @@
     def head_spec(off):
         return pl.BlockSpec((length, 128), lambda s, h: (s, off + h))
 
-    for part, (g, whole) in enumerate(((g_first, wholes[0]), (g_second, wholes[1]))):
+    for part, g in enumerate((g_first, g_second)):
         run(base)
         g.arrived()
 
@@ -632,9 +655,9 @@
         pltpu.emit_pipeline(
             qkv_body,
             grid=(3,),
-            in_specs=[whole_spec(whole, tile)],
+            in_specs=[whole_spec(w_qkv, tile, 3 * part)],
             out_specs=[pl.BlockSpec((tokens, tile), lambda j, part=part: (0, j * halves + part))],
-        )(whole, merged)
+        )(w_qkv, merged)
         base += 3
 
         def attend_body(q, k, v, o, l, first=base):
@@ -670,16 +693,16 @@
     pltpu.emit_pipeline(
         out_body,
         grid=(tokens // 256,),
-        in_specs=[pl.BlockSpec((256, width), lambda i: (i, 0)), whole_spec(wholes[2])],
+        in_specs=[pl.BlockSpec((256, width), lambda i: (i, 0)), whole_spec(w_out)],
         out_specs=[pl.BlockSpec((256, width), lambda i: (i, 0))],
-    )(attended, wholes[2], middle)
+    )(attended, w_out, middle)
 
     store_n2 = pltpu.make_async_copy(n2_ref, n2, local.at[1])
     store_n2.start()
     base += n_out
     n_up = act.shape[1] // tile
     n_part = n_up // 2
-    for part, (g, whole) in enumerate(((g_low, wholes[3]), (g_high, wholes[4]))):
+    for part, g in enumerate((g_low, g_high)):
         run(base)
         g.arrived()
 
@@ -695,9 +718,9 @@
         pltpu.emit_pipeline(
             up_body,
             grid=(n_part,),
-            in_specs=[whole_spec(whole, tile)],
+            in_specs=[whole_spec(w_up, tile, part * n_part)],
             out_specs=[column_spec, column_spec],
-        )(whole, act, slope)
+        )(w_up, act, slope)
         base += n_part
 
     first_grad = base
@@ -725,15 +748,13 @@
     hidden = 16 * shards[3].shape[0]
     views = [s.reshape(2, 2, s.shape[0] // 4, s.shape[1]) for s in shards]
     q = views[0].shape[2]
-    columns = [3 * width // 2] * 2 + [width] + [hidden // 2] * 2
-    whole = [jax.ShapeDtypeStruct((32, 2, q, n), BF16) for n in columns]
-    whole += [jax.ShapeDtypeStruct((32,) + v.shape[1:], BF16) for v in views[3:]]
+    whole = [jax.ShapeDtypeStruct((32,) + v.shape[1:], BF16) for v in views]
     vmem, any_space = pl.BlockSpec(memory_space=pltpu.VMEM), pl.BlockSpec(memory_space=pl.ANY)
     low = lambda *shape: jax.ShapeDtypeStruct(shape, BF16)
     outs = pl.pallas_call(
         lambda *refs: forward_kernel(length, GATHER_PLAN, *refs),
         in_specs=[vmem] * 5 + [any_space] * 2,
-        out_specs=[any_space] * 16 + [vmem],
+        out_specs=[any_space] * 14 + [vmem],
         out_shape=whole
         + [
             low(tokens, width),
@@ -750,7 +771,7 @@
         scratch_shapes=[
             pltpu.VMEM((1, hidden), F32),
             pltpu.VMEM((1, 3 * width), F32),
-            pltpu.VMEM(whole[6].shape, BF16),
+            pltpu.VMEM(whole[4].shape, BF16),
             pltpu.VMEM((tokens, width), BF16),
             pltpu.VMEM((tokens, width), BF16),
             pltpu.VMEM((tokens, width), BF16),
@@ -763,29 +784,26 @@
         compiler_params=pltpu.CompilerParams(collective_id=0, has_side_effects=True, vmem_limit_bytes=VMEM_LIMIT),
         name="forward",
     )(*views, x, c)
-    return outs[:6], outs[7:]
+    return outs[:4], outs[5:]
 
 
 PLAN = (
-    (4, 0, 0, 0), (6, 1, 0, 0), (10, 0, 0, 1), (13, 1, 0, 1), (14, 2, 0, 0), (18, 0, 0, 2), (18, 0, 1, 0), (19, 0, 1, 1),
-    (20, 1, 0, 2), (22, 0, 0, 3), (24, 1, 1, 0), (25, 1, 1, 1), (25, 1, 0, 3), (28, 0, 2, 0), (30, 1, 2, 0), (31, 0, 2, 2),
-    (33, 3, 0, 0), (33, 1, 2, 2), (33, 2, 1, 1), (33, 2, 0, 1), (34, 0, 2, 1), (36, 2, 2, 0), (36, 2, 0, 2), (36, 1, 2, 1),
-    (36, 0, 1, 3), (38, 2, 1, 0), (39, 1, 1, 3), (39, 0, 3, 1), (39, 0, 3, 0), (41, 2, 0, 3), (42, 0, 2, 3), (43, 0, 1, 2),
-    (44, 3, 1, 1), (44, 3, 0, 1), (44, 2, 2, 1), (44, 1, 3, 1), (46, 2, 1, 3), (46, 1, 2, 3), (47, 1, 1, 2), (49, 1, 3, 0),
-    (49, 0, 3, 2), (50, 2, 3, 1), (50, 0, 3, 3), (51, 1, 3, 3), (51, 3, 0, 2), (51, 3, 1, 0), (51, 3, 2, 1), (51, 1, 3, 2),
-    (54, 4, 0, 0), (54, 3, 2, 0), (54, 2, 3, 0), (55, 2, 3, 3), (55, 2, 2, 2), (55, 2, 1, 2), (56, 2, 3, 2), (57, 2, 2, 3),
-    (57, 3, 3, 1), (57, 0, 4, 1), (57, 4, 0, 1), (57, 0, 4, 0), (58, 1, 4, 0), (58, 1, 4, 1), (58, 0, 4, 3), (58, 3, 1, 2),
-    (58, 0, 5, 0), (58, 3, 3, 0), (58, 4, 1, 2), (59, 1, 5, 0), (59, 0, 5, 1), (60, 1, 5, 1), (60, 4, 2, 0), (60, 3, 2, 2),
-    (60, 0, 6, 0), (60, 2, 4, 0), (61, 0, 5, 2), (61, 3, 0, 3), (61, 2, 4, 1), (61, 0, 6, 1), (61, 4, 2, 2), (61, 1, 6, 0),
-    (61, 2, 5, 0), (62, 4, 1, 0), (62, 2, 5, 1), (62, 3, 4, 0), (62, 4, 1, 1), (62, 1, 6, 1), (62, 4, 0, 3), (62, 0, 6, 3),
-    (62, 3, 2, 3), (62, 1, 4, 3), (62, 4, 2, 1), (62, 0, 6, 2), (63, 1, 5, 2), (63, 2, 6, 0), (63, 3, 1, 3), (63, 3, 3, 2),
-    (63, 0, 5, 3), (63, 1, 6, 2), (63, 3, 3, 3), (63, 0, 4, 2), (63, 4, 3, 0), (64, 3, 5, 0), (64, 2, 6, 1), (64, 1, 5, 3),
-    (64, 4, 3, 1), (64, 4, 2, 3), (64, 3, 5, 1), (64, 1, 6, 3), (64, 4, 1, 3), (65, 1, 4, 2), (65, 4, 4, 0), (66, 3, 6, 0),
-    (66, 2, 4, 3), (67, 2, 6, 2), (67, 4, 5, 0), (67, 4, 0, 2), (67, 2, 5, 2), (67, 3, 6, 1), (67, 2, 5, 3), (68, 4, 6, 0),
-    (68, 4, 3, 3), (68, 3, 4, 1), (68, 2, 6, 3), (68, 3, 4, 3), (68, 5, 0, 0), (68, 4, 5, 1), (68, 2, 4, 2), (68, 4, 3, 2),
-    (68, 3, 6, 2), (68, 4, 4, 3), (68, 4, 6, 1), (69, 3, 5, 2), (69, 3, 5, 3), (69, 4, 5, 2), (69, 3, 6, 3), (69, 4, 6, 3),
-    (69, 5, 2, 0), (69, 5, 1, 0), (69, 4, 6, 2), (69, 3, 4, 2), (69, 4, 4, 2), (69, 5, 3, 0), (69, 4, 4, 1), (69, 4, 5, 3),
-    (71, 5, 6, 0), (71, 5, 4, 0), (71, 5, 5, 0),
+    (4, 0, 0, 0), (7, 1, 0, 0), (7, 0, 0, 1), (9, 0, 0, 2), (11, 1, 0, 1), (11, 0, 0, 3), (13, 1, 0, 2), (18, 2, 0, 0),
+    (18, 1, 0, 3), (20, 0, 1, 1), (21, 2, 0, 2), (22, 2, 0, 1), (25, 3, 0, 0), (27, 1, 1, 1), (28, 0, 2, 0), (28, 0, 1, 0),
+    (30, 0, 2, 1), (30, 1, 2, 0), (32, 1, 1, 0), (32, 1, 2, 1), (34, 0, 1, 2), (35, 1, 1, 2), (35, 2, 2, 0), (35, 3, 0, 1),
+    (35, 2, 1, 1), (37, 0, 2, 3), (39, 1, 2, 3), (39, 0, 2, 2), (39, 0, 1, 3), (40, 4, 0, 0), (40, 1, 1, 3), (40, 1, 2, 2),
+    (40, 3, 1, 1), (40, 2, 2, 1), (40, 1, 3, 1), (41, 1, 3, 0), (46, 2, 1, 0), (47, 3, 0, 2), (48, 2, 1, 2), (48, 2, 0, 3),
+    (48, 2, 2, 3), (49, 1, 3, 3), (50, 2, 3, 0), (50, 3, 1, 0), (51, 1, 3, 2), (53, 2, 1, 3), (54, 2, 3, 1), (54, 4, 1, 0),
+    (55, 2, 3, 3), (55, 2, 3, 2), (55, 2, 2, 2), (57, 1, 4, 0), (57, 3, 0, 3), (57, 1, 4, 1), (57, 4, 0, 1), (57, 3, 2, 0),
+    (58, 1, 4, 2), (58, 4, 1, 1), (58, 3, 3, 3), (58, 3, 2, 1), (58, 3, 3, 1), (59, 1, 5, 1), (59, 3, 3, 0), (59, 3, 2, 2),
+    (59, 1, 5, 0), (59, 1, 4, 3), (61, 2, 4, 0), (61, 3, 1, 3), (61, 1, 6, 0), (62, 3, 1, 2), (62, 4, 1, 3), (62, 2, 5, 0),
+    (62, 4, 0, 3), (62, 1, 6, 1), (62, 3, 2, 3), (62, 1, 5, 3), (62, 4, 2, 1), (62, 4, 2, 0), (62, 4, 3, 1), (62, 2, 5, 1),
+    (64, 2, 6, 0), (64, 2, 4, 1), (64, 3, 5, 0), (64, 3, 4, 0), (65, 1, 5, 2), (66, 2, 6, 1), (66, 2, 4, 3), (66, 4, 2, 3),
+    (66, 4, 3, 0), (66, 1, 6, 2), (66, 2, 4, 2), (66, 3, 5, 1), (66, 3, 3, 2), (66, 1, 6, 3), (66, 2, 5, 3), (66, 4, 5, 0),
+    (67, 2, 5, 2), (67, 3, 6, 0), (67, 4, 4, 0), (67, 3, 4, 1), (68, 4, 3, 3), (68, 2, 6, 2), (68, 3, 6, 1), (69, 4, 6, 0),
+    (69, 3, 4, 2), (69, 3, 4, 3), (69, 2, 6, 3), (69, 5, 2, 0), (69, 4, 4, 3), (69, 5, 0, 0), (69, 4, 4, 1), (69, 5, 1, 0),
+    (69, 4, 5, 1), (69, 3, 5, 2), (69, 3, 5, 3), (69, 4, 5, 3), (70, 4, 6, 1), (70, 3, 6, 2), (70, 5, 3, 0), (70, 3, 6, 3),
+    (70, 4, 6, 3), (71, 5, 4, 0), (72, 5, 5, 0), (72, 5, 6, 0),
 )
 
 PRE, S0, S1, S2, S3, S4 = range(6)
@@ -797,14 +815,15 @@
 
 
 def backward_kernel(length, plan, n_up_parts, *refs):
-    (w_first, w_second, w_out, w_low, w_high, w_down), refs = refs[:6], refs[6:]
+    (w_qkv, w_out, w_up, w_down), refs = refs[:4], refs[4:]
     x, c, n1, merged, logsum, attended, middle, n2, act, slope, g_down, small, refs = refs[:12] + (refs[12:],)
     output, input_grad, f_qkv, f_out, f_up, f_down, f_vec, g_qkv, g_out, g_up, mid_grad, ag, back, refs = refs[:13] + (
         refs[13:],
     )
-    landing, refs = refs[:7], refs[7:]
+    landing, refs = refs[:3], refs[3:]
     sets, refs = refs[: 7 * 7], refs[7 * 7 :]
-    tmps, refs = refs[:7], refs[7:]
+    tmps, refs = refs[:3] + (None,) * 4, refs[3:]
+    landing, refs = landing + refs[:4], refs[4:]
     vec_bufs, refs = refs[:7], refs[7:]
     (g_vec, narrow, wide, left, right, acc, out_acc, branch, dk_acc, dv_acc, sems, vec_sems, csem) = refs
     tokens, width = x.shape
@@ -828,10 +847,10 @@
 
     vectors = VectorScatter(p, g_vec, f_vec, vec_bufs, vec_sems)
 
-    def turn(slot, first, count):
+    def turn(slot, first, count, step=1):
         table = {}
         for at, stage, k, i in plan:
-            if first <= at < first + count:
+            if at in range(first, first + count, step):
                 table.setdefault(at, []).append(lambda stage=stage, k=k, i=i: getattr(rs[k], STAGES[stage])(i))
         hook(slot, table)
 
@@ -847,50 +866,44 @@
     g_vec[...] = jnp.zeros_like(g_vec)
     acc[...] = jnp.zeros_like(acc)
     out_acc[...] = jnp.zeros_like(out_acc)
-    for load in loads:
-        load.wait()
 
     n_up = hidden // tile
 
-    def ffn_body(wd, s, wu_low, wu_high, g):
+    def ffn_body(wd, s, wu, g):
         j = pl.program_id(0)
+
+        @pl.when(j == 0)
+        def _():
+            for load in loads:
+                load.wait()
 
         @pl.when(j == n_up // 2 + 1)
         def _():
             rs[1].start()
 
-        turn(3 * j, 0, 3 * n_up)
+        turn(3 * j, 0, 3 * n_up - 0, 3)
         grad = (dot(left[...], rows_of(wd), NT) * s[...].astype(F32)).astype(BF16)
         at = pl.ds(pl.multiple_of(j * tile, tile), tile)
         wide[:, at] = jnp.sum(grad.astype(F32), 0, keepdims=True)
-        turn(3 * j + 1, 0, 3 * n_up)
+        turn(3 * j + 1, 1, 3 * n_up - 1, 3)
         g[0] = dot(right[...], grad, TN).astype(BF16).reshape(g.shape[1:])
-        turn(3 * j + 2, 0, 3 * n_up)
-
-        @pl.when(j < n_up // 2)
-        def _():
-            acc[...] += dot(grad, rows_of(wu_low), NT)
-
-        @pl.when(j >= n_up // 2)
-        def _():
-            acc[...] += dot(grad, rows_of(wu_high), NT)
+        turn(3 * j + 2, 2, 3 * n_up - 2, 3)
+        acc[...] += dot(grad, rows_of(wu), NT)
 
     per = n_up // n_up_parts
     q_down = w_down.shape[2]
     blocks = tile // (2 * q_down)
     shape = g_up.shape[1:7]
-    n, two, q, _ = w_low.shape
     pltpu.emit_pipeline(
         ffn_body,
         grid=(n_up,),
         in_specs=[
             pl.BlockSpec((blocks, 2, q_down, width), lambda j: (j, 0, 0, 0)),
             pl.BlockSpec((tokens, tile), lambda j: (0, j)),
-            pl.BlockSpec((n, two, q, tile), lambda j: (0, 0, 0, jnp.minimum(j, n_up // 2 - 1))),
-            pl.BlockSpec((n, two, q, tile), lambda j: (0, 0, 0, jnp.maximum(j - n_up // 2, 0))),
+            whole_spec(w_up, tile),
         ],
         out_specs=[pl.BlockSpec((1,) + shape + (tile,), lambda j: (j // per, 0, 0, 0, 0, 0, 0, j % per))],
-    )(w_down, slope, w_low, w_high, g_up)
+    )(w_down, slope, w_up, g_up)
     rs[2].start()
     load = pltpu.make_async_copy(n1, right, csem.at[1])
     load.start()
@@ -1009,28 +1022,15 @@
     first_in = base
     acc[...] = jnp.zeros_like(acc)
 
-    def in_body(d, w_one, w_two):
-        j = pl.program_id(0)
-        turn(first_in + j, first_in, n_qkv)
-
-        @pl.when(j < 3)
-        def _():
-            acc[...] += dot(d[0], rows_of(w_one), NT)
-
-        @pl.when(j >= 3)
-        def _():
-            acc[...] += dot(d[0], rows_of(w_two), NT)
-
-    n, two, q, _ = w_first.shape
+    def in_body(d, w):
+        turn(first_in + pl.program_id(0), first_in, n_qkv)
+        acc[...] += dot(d[0], rows_of(w), NT)
+
     pltpu.emit_pipeline(
         in_body,
         grid=(n_qkv,),
-        in_specs=[
-            pl.BlockSpec((1, tokens, tile), lambda j: (j % 3, 0, j // 3)),
-            pl.BlockSpec((n, two, q, tile), lambda j: (0, 0, 0, jnp.minimum(j, 2))),
-            pl.BlockSpec((n, two, q, tile), lambda j: (0, 0, 0, jnp.maximum(j - 3, 0))),
-        ],
-    )(back, w_first, w_second)
+        in_specs=[pl.BlockSpec((1, tokens, tile), lambda j: (j % 3, 0, j // 3)), whole_spec(w_qkv, tile)],
+    )(back, w_qkv)
     base += n_qkv
 
     first_one = base
@@ -1110,7 +1110,8 @@
     scratch = []
     for kind in kinds:
         scratch += Scatter.scratch(*kind)
-    scratch += [pltpu.VMEM((2, 2, 2, 2) + kind[:2], kind[2]) for kind in kinds]
+    scratch += [pltpu.VMEM((2, 2, 2, 2) + kind[:2], kind[2]) for kind in kinds[:3]]
+    scratch += [pltpu.VMEM((4, 2, 2, 2) + kind[:2], kind[2]) for kind in kinds[3:]]
     scratch += VectorScatter.scratch()
     scratch += [
         pltpu.VMEM((4, 2, 2, 16, 128), F32),
@@ -1130,8 +1131,8 @@
     shards = [full(2, 2, q, 3 * width), full(2, 2, q, width), full(2, 2, q, hidden), full(2, 2, q_down, width)]
     outs = pl.pallas_call(
         lambda *refs: backward_kernel(length, PLAN, parts, *refs),
-        in_specs=[any_space] * 17 + [vmem],
-        out_specs=[any_space] * 2 + [vmem] * 5 + [any_space] * 13,
+        in_specs=[any_space] * 15 + [vmem],
+        out_specs=[any_space] * 2 + [vmem] * 5 + [any_space] * 9,
         out_shape=[low(tokens, width), full(tokens, width)]
         + shards
         + [full(16, 128)]
@@ -1143,7 +1144,7 @@
             low(tokens, width),
             low(3, tokens, width),
         ]
-        + [jax.ShapeDtypeStruct((4, 2, 2, 2) + kind[:2], kind[2]) for kind in kinds],
+        + [jax.ShapeDtypeStruct((4, 2, 2, 2) + kind[:2], kind[2]) for kind in kinds[:3]],
         scratch_shapes=scratch,
         compiler_params=pltpu.CompilerParams(
             collective_id=1, has_side_effects=True, vmem_limit_bytes=66 * 10**6
@@ -1222,8 +1223,7 @@
 
 
 def unpack_shard(packed):
-    odd = lax.axis_index("fsdp") % 2 == 1
-    narrow = jnp.where(odd, packed[:8, 64:], packed[:8, :64])
+    narrow = packed[:8, :64]
     wide = packed[8:10].reshape(256)
     return tuple(narrow[j] for j in range(3)) + (wide,) + tuple(narrow[j] for j in range(3, 8))
 

time: 283 us -> 277 us (0.979)
  Pallas kernels: 267 us -> 260 us
    pallas_call x1, Pallas kernels: 149 us -> 143 us  [backward_call(): pl.pallas_call(lambda *refs: backward_kernel(length, PLAN, parts, *refs),...]
where the time goes in v5:
time: 277 us; the launch traced here: 275 us
  Pallas kernels  260 us (94%)
  local copies, waits for them, and re-layouts  12.5 us (5%)
    pallas_call x1, Pallas kernels, backward_call(): pl.pallas_call(lambda *refs: backward_kernel(length, PLAN, parts, *refs),...  143 us
    pallas_call x1, Pallas kernels, forward_call(): pl.pallas_call(lambda *refs: forward_kernel(length, GATHER_PLAN, *refs),...  118 us
    unnamed x16, local copies, waits for them, and re-layouts  8.76 us

profile of v5, /device:TPU:0, one launch (start us, length us, event | category | flops | bytes accessed | tf_op | source)
XLA Modules:
  0.0 275.0 jit_solution(15120420504516333398)
XLA Ops:
  0.7 0.8 stack.35
  1.5 1.3 fusion.4
  2.8 117.8 %forward.1 = (bf16[32,2,16,3072]{3,2,1,0:T(8,128)(2,1)}, bf16[32,2,16,1024]{3,2,1,0:T(8,128)(2,1)}, bf16[32,2,16,4096]{3,2,1,0:T(8,128)(2,1)}, bf16[32,2,64,1024...) custom-call(bf16[2,2,16,3072]{3,2,1,0:T(8,128)(2,1)} %bitcast.53, ...), custom_call_target="tpu_custom_call" | custom-call | tf_op jit(solution)/shard_map/forward/pallas_call | solution.py:754
  120.6 142.6 %backward.1 = (bf16[1024,1024]{1,0:T(8,128)(2,1)}, f32[1024,1024]{1,0:T(8,128)}, f32[2,2,16,3072]{3,2,1,0:T(8,128)}, f32[2,2,16,1024]{3,2,1,0:T(8,128)}, f32[2,2...) custom-call(bf16[32,2,16,3072]{3,2,1,0:T(8,128)(2,1)} %get-tuple-ele, ...), custom_call_target="tpu_custom_call" | custom-call | tf_op jit(solution)/shard_map/backward/pallas_call | solution.py:1132
  263.3 0.0 copy-start
  263.3 1.4 slice_bitcast_fusion
  264.7 1.5 slice_bitcast_fusion.1
  266.2 3.1 %copy.36 = bf16[2,512,1024]{2,1,0:T(8,128)(2,1)} copy(bf16[2,512,1024]{2,1,0:T(8,128)(2,1)} %bitcast.47) | data formatting | bytes 4194304
  269.3 0.0 copy-done
  269.3 0.0 copy-start.3
  269.3 0.0 copy-start.4
  269.3 0.0 copy-start.2
  269.3 2.1 copy.37
  271.4 0.0 copy-done.3
  271.4 0.0 copy-start.1
  271.4 0.9 copy.38
  272.3 0.0 copy-done.4
  272.3 0.7 copy.39
  273.0 0.0 copy-done.2
  273.0 1.0 copy.40
  274.0 0.0 copy-done.1
  274.0 1.0 copy.41
  (1 shorter events, 0.0 us)
Async XLA Ops:
  263.3 6.0 %copy-start = (f32[1024,1024]{1,0:T(8,128)S(1)}, f32[1024,1024]{1,0:T(8,128)}, u32[]{:S(2)}) copy-start(f32[1024,1024]{1,0:T(8,128)} %get-tuple-element.51) | copy-start | bytes 12582916
  269.3 2.1 copy-start.3
  269.3 3.0 %copy-start.4 = (f32[2,2,16,1024]{3,2,1,0:T(8,128)S(1)}, f32[2,2,16,1024]{3,2,1,0:T(8,128)}, u32[]{:S(2)}) copy-start(f32[2,2,16,1024]{3,2,1,0:T(8,128)} %get-tuple-element.53) | copy-start | bytes 786436
  269.3 3.7 %copy-start.2 = (f32[2,2,16,4096]{3,2,1,0:T(8,128)S(1)}, f32[2,2,16,4096]{3,2,1,0:T(8,128)}, u32[]{:S(2)}) copy-start(f32[2,2,16,4096]{3,2,1,0:T(8,128)} %get-tuple-element.54) | copy-start | bytes 3145732
  271.4 2.6 copy-start.1
